TPU v7x, 512 devices: a whole 4x4x16 slice. The times are simulated.
512 devices in a mesh: row: 16 (over x, z_hi, core), vec: 32 (over z_lo, y).
Axes of the slice: x: 4, y: 4, z: 16 (z_hi: 2, z_lo: 8; z = z_hi * 8 + z_lo), core: 2. Of those that a mesh axis runs over, the one named last changes fastest.
Arguments:
- old_vectors: float32 [640, 49152], P('vec', 'row'), may hold values from -6 to 6
- panel_source: int32 [256], replicated, may hold values from 0 to 639, as said below
- secular: float32 [4096, 256], P('vec'), may hold values from -0.375 to 0.375
- reflectors: float32 [256, 49152], P('vec', 'row'), may hold values from -6 to 6
- wy_factor: float32 [256, 256], replicated, as said below
- cholesky_panel: float32 [256, 49152], P('vec', 'row'), may hold values from -0.02734375 to 0.02734375
- panel_inverse: float32 [256, 256], replicated, as said below
Outputs:
- vectors: float32 [4096, 49152], P('vec', 'row')
Inputs may be any that keep to these rules, and one draw needn't show every extreme that they name: `panel_source`: distinct numbers; each block of 20 consecutive old vectors (those of one index of vec) supplies at most 12 panel columns, and some block supplies exactly 12. `wy_factor`: upper triangular. `panel_inverse`: upper triangular.
All inputs are finite; a program needn't handle non-finite values.
Results may differ from a plain program's by a relative error of at most 0.0001.
Values sent between devices are 32-bit elements; how exact they have to be, the bound alone decides.
No kernel may reach another device: no remote copies, remote signals or barrier semaphores. Data moves between devices by JAX's collectives and lax.ppermute only.
A program may use at most 64 MiB of HBM per device.

v0:
```python
import jax
import jax.numpy as jnp
from jax import lax
from jax.sharding import Mesh
from jax.sharding import PartitionSpec as P


ROW = ("x", "zh", "core")
VEC = ("z", "y")
HOPS = (4, 2, 1)


def product(left, right, contract=(1, 0)):
    return lax.dot_general(
        left,
        right,
        (((contract[0],), (contract[1],)), ((), ())),
        precision=lax.Precision.HIGHEST,
        preferred_element_type=jnp.float32,
    )


def onehot(index, width):
    return (index[:, None] == jnp.arange(width, dtype=jnp.int32)[None, :]).astype(jnp.float32)


def doubled(block, axis, hops):
    width = lax.axis_size(axis)
    for hop in hops:
        other = lax.ppermute(block, axis, [(i, i ^ hop) for i in range(width)])
        block = jnp.concatenate([block, other], axis=0)
    return block


def place_of(index, mine, hops):
    apart = index ^ mine
    return sum(((apart // hop) % 2) << k for k, hop in enumerate(hops))


def spread(array, axis):
    copies = jnp.broadcast_to(array[None], (lax.axis_size(axis), *array.shape))
    return lax.all_to_all(copies, axis, 0, 0)


def summed_rows(partial):
    parts = partial.reshape(lax.axis_size("y"), -1, partial.shape[1])
    group = lax.axis_size("x") * lax.axis_size("core")
    parts = jnp.broadcast_to(parts[None], (group, *parts.shape)).reshape(-1, *parts.shape[1:])
    parts = lax.all_to_all(parts, ("x", "core", "y"), 0, 0)
    own = jnp.sum(parts, axis=0)
    own = own + lax.ppermute(own, "zh", [(0, 1), (1, 0)])
    return spread(spread(own, "z"), "y")


def per_device(
    old_vectors, panel_source, secular, reflectors, wy_factor, cholesky_panel, panel_inverse
):
    panel = secular.shape[1]
    old_count, row_count = old_vectors.shape
    z_width, y_width = lax.axis_size("z"), lax.axis_size("y")
    vec_width = z_width * y_width
    z_index, y_index = lax.axis_index("z"), lax.axis_index("y")
    row_index = lax.axis_index(ROW)
    share = panel // vec_width
    slots = 3 * share // 2
    cols = row_count // y_width

    owner = panel_source // old_count
    local = panel_source % old_count
    order = jnp.arange(panel, dtype=jnp.int32)
    same = (owner[:, None] == owner[None, :]) & (order[:, None] > order[None, :])
    earlier = jnp.sum(same.astype(jnp.int32), axis=1)
    mine = owner == z_index * y_width + y_index
    picker = (
        (earlier[None, :] == jnp.arange(slots, dtype=jnp.int32)[:, None]) & mine[None, :]
    ).astype(jnp.float32)
    chooser = product(picker, onehot(local, old_count))
    buffer = product(chooser, old_vectors)

    packed = jnp.concatenate([reflectors, cholesky_panel, buffer], axis=0)
    packed = packed.reshape(packed.shape[0], y_width, cols).transpose(1, 0, 2)
    packed = lax.all_to_all(packed, "y", 0, 0)
    own_reflectors = packed[:, :share].reshape(-1, cols)
    own_cholesky = packed[:, share : 2 * share].reshape(-1, cols)
    own_slots = packed[:, 2 * share :].reshape(-1, cols)
    first = row_index * row_count + y_index * cols
    below = first + jnp.arange(cols, dtype=jnp.int32) >= panel
    own_cholesky = jnp.where(below[None, :], own_cholesky, 0.0)

    all_reflectors = doubled(own_reflectors, "z", HOPS)
    all_slots = doubled(own_slots, "z", HOPS)

    group = share * y_width
    turned = onehot(place_of(order // group, z_index, HOPS) * group + order % group, panel)
    inner = product(product(own_slots, all_reflectors, (1, 1)), turned, (1, 1))
    inner = summed_rows(inner).reshape(-1, panel)
    summed_at = ((owner % y_width) * z_width + owner // y_width) * slots + earlier
    inner = product(onehot(summed_at, slots * vec_width), inner)
    coeff = product(inner, product(wy_factor, turned, (0, 0)))

    z_place = place_of(owner // y_width, z_index, HOPS)
    held_at = (z_place * y_width + owner % y_width) * slots + earlier
    gathered = product(onehot(held_at, slots * vec_width), all_slots)
    transformed = gathered - product(coeff, all_reflectors)

    blocks = [transformed]
    for d in range(1, y_width):
        turn = [(i, (i + d) % y_width) for i in range(y_width)]
        blocks.append(lax.ppermute(transformed, "y", turn))
    cross = summed_rows(product(own_cholesky, transformed, (1, 1)))
    cross = cross.transpose(1, 0, 2, 3).reshape(-1, panel)
    correction = product(secular, cross, (1, 1))

    applied = jnp.zeros((secular.shape[0], row_count), jnp.float32)
    for d, block in enumerate(blocks):
        at = ((y_index - d + y_width) % y_width) * cols
        applied = lax.dynamic_update_slice(applied, product(secular, block), (0, at))
    head = applied[:, :panel]
    solved = product(head - correction, panel_inverse, (1, 1))
    return lax.dynamic_update_slice(applied, jnp.where(row_index == 0, solved, head), (0, 0))


def solution(mesh):
    split = Mesh(mesh.devices.reshape(mesh.shape["row"] // 4, 2, 2, 8, 4), ROW + VEC)

    return jax.shard_map(
        per_device,
        mesh=split,
        in_specs=(P(VEC, ROW), P(), P(VEC, None), P(VEC, ROW), P(), P(VEC, ROW), P()),
        out_specs=P(VEC, ROW),
        check_vma=False,
    )
```

profile of v0, /device:TPU:1, one launch (start us, length us, event | category | flops | bytes accessed | tf_op | source)
XLA Modules:
  0.0 251.7 jit_solution(13439359801746424117)
XLA Ops:
  0.0 0.7 and_select_fusion.7
  0.7 0.7 broadcast_compare_fusion
  1.4 0.2 convert_reduce_fusion
  1.6 0.2 fusion.25
  1.8 0.3 fusion.55
  2.2 1.0 pad_maximum_fusion.4
  3.1 0.2 reshape.137
  3.3 0.1 copy.46
  3.4 11.0 %all_to_all.35 = f32[4,28,768]{2,1,0:T(8,128)S(1)} all-to-all(f32[4,28,768]{2,1,0:T(8,128)S(1)} %bitcast.55), channel_id=1, replica_groups=mesh['x'=4,'zh'=2,'core'=2,'z'=8,'y'=4] {'y'}, dimensions={0} | all-to-all | bytes 688128 | tf_op jit(solution)/shard_map/all_to_all | solution.py:82
  14.4 9.8 %collective-permute-start.3 = (f32[32,768]{1,0:T(8,128)S(1)}, f32[32,768]{1,0:T(8,128)S(1)}, u32[]{:S(2)}, u32[]{:S(2)}) collective-permute-start(f32[32,768]{1,0:T(8,128)S(1)} %slice_bitcast_fusion), channel_id=1, source_target_pairs={{0,16},{4,20},{8,24},{12,28},{16,0},{20,4},{24,8},{28,12},{1,17},{... | collective-permute-start | bytes 294920 | tf_op jit(solution)/shard_map/ppermute | solution.py:30
  24.2 2.0 collective-permute-done.3
  26.3 8.7 %collective-permute-start.4 = (f32[64,768]{1,0:T(8,128)S(1)}, f32[64,768]{1,0:T(8,128)S(1)}, u32[]{:S(2)}, u32[]{:S(2)}) collective-permute-start(f32[64,768]{1,0:T(8,128)S(1)} %pad_maximum_fusion.7), channel_id=1, source_target_pairs={{0,8},{4,12},{8,0},{12,4},{16,24},{20,28},{24,16},{28,20},{1,9},{5... | collective-permute-start | bytes 589832 | tf_op jit(solution)/shard_map/ppermute | solution.py:30
  34.9 3.0 %collective-permute-done.4 = f32[64,768]{1,0:T(8,128)S(1)} collective-permute-done((f32[64,768]{1,0:T(8,128)S(1)}, f32[64,768]{1,0:T(8,128)S(1)}, u32[]{:S(2)}, u32[]{:S(2)}) %collective-permute-start.4) | collective-permute-done | bytes 196640 | tf_op jit(solution)/shard_map/ppermute | solution.py:30
  38.0 8.9 %collective-permute-start.5 = (f32[128,768]{1,0:T(8,128)S(1)}, f32[128,768]{1,0:T(8,128)S(1)}, u32[]{:S(2)}, u32[]{:S(2)}) collective-permute-start(f32[128,768]{1,0:T(8,128)S(1)} %pad_maximum_fusion.5), channel_id=1, source_target_pairs={{0,4},{4,0},{8,12},{12,8},{16,20},{20,16},{24,28},{28,24},{1,5},{5... | collective-permute-start | bytes 1179656 | tf_op jit(solution)/shard_map/ppermute | solution.py:30
  47.0 7.7 %collective-permute-done.5 = f32[128,768]{1,0:T(8,128)S(1)} collective-permute-done((f32[128,768]{1,0:T(8,128)S(1)}, f32[128,768]{1,0:T(8,128)S(1)}, u32[]{:S(2)}, u32[]{:S(2)}) %collective-permute-start.5) | collective-permute-done | bytes 393248 | tf_op jit(solution)/shard_map/ppermute | solution.py:30
  54.6 0.8 fusion.16
  55.5 0.0 copy-start.4
  55.5 0.3 fusion.19
  55.8 0.1 broadcast_in_dim.30
  55.9 18.3 %all_to_all.36 = f32[32,12,256]{2,1,0:T(8,128)S(1)} all-to-all(f32[32,12,256]{2,1,0:T(8,128)S(1)} %bitcast.54), channel_id=1, replica_groups=mesh['x'=4,'zh'=2,'core'=2,'z'=8,'y'=4] {'x','core','y'}, dimensions={0} | all-to-all | bytes 786432 | tf_op jit(solution)/shard_map/all_to_all | solution.py:49
  74.2 0.1 reduce_sum.28
  74.2 16.0 %collective-permute-start.6 = (f32[12,256]{1,0:T(8,128)S(1)}, f32[12,256]{1,0:T(8,128)S(1)}, u32[]{:S(2)}, u32[]{:S(2)}) collective-permute-start(f32[12,256]{1,0:T(8,128)S(1)} %reduce_sum.28), channel_id=1, source_target_pairs={{0,64},{64,0},{1,65},{65,1},{2,66},{66,2},{3,67},{67,3},{4,68},{68... | collective-permute-start | bytes 36872 | tf_op jit(solution)/shard_map/ppermute | solution.py:51
  90.2 1.1 collective-permute-done.6
  91.4 0.7 broadcast_in_dim.31
  92.0 7.5 %all-to-all-start.2 = ((f32[8,12,256]{2,1,0:T(8,128)}), f32[8,12,256]{2,1,0:T(8,128)S(1)}, u32[]{:S(2)}, u32[]{:S(2)}) async-start(f32[8,12,256]{2,1,0:T(8,128)} %broadcast_in_dim.31), calls=%async_computation.2 | async-start | bytes 262144 | tf_op jit(solution)/shard_map/all_to_all | solution.py:42
  99.5 0.5 fusion.18
  99.9 7.3 %collective-permute-start = (f32[48,768]{1,0:T(8,128)S(1)}, f32[48,768]{1,0:T(8,128)S(1)}, u32[]{:S(2)}, u32[]{:S(2)}) collective-permute-start(f32[48,768]{1,0:T(8,128)S(1)} %reshape.138), channel_id=1, source_target_pairs={{0,16},{4,20},{8,24},{12,28},{16,0},{20,4},{24,8},{28,12},{1,17},{... | collective-permute-start | bytes 442376 | tf_op jit(solution)/shard_map/ppermute | solution.py:30
  107.3 16.9 %collective-permute-done = f32[48,768]{1,0:T(8,128)S(1)} collective-permute-done((f32[48,768]{1,0:T(8,128)S(1)}, f32[48,768]{1,0:T(8,128)S(1)}, u32[]{:S(2)}, u32[]{:S(2)}) %collective-permute-start) | collective-permute-done | bytes 147488 | tf_op jit(solution)/shard_map/ppermute | solution.py:30
  124.2 1.9 collective-permute-start.1
  126.1 0.1 copy.38
  126.2 0.8 broadcast_in_dim.32
  127.0 3.5 %all-to-all-start.3 = ((f32[4,8,12,256]{3,1,2,0:T(8,128)}), f32[4,8,12,256]{3,1,2,0:T(8,128)S(1)}, u32[]{:S(2)}, u32[]{:S(2)}) async-start(f32[4,8,12,256]{3,1,2,0:T(8,128)} %broadcast_in_dim.32), calls=%async_computation.3 | async-start | bytes 786432 | tf_op jit(solution)/shard_map/all_to_all | solution.py:42
  130.5 9.0 %collective-permute-done.1 = f32[96,768]{1,0:T(8,128)S(1)} collective-permute-done((f32[96,768]{1,0:T(8,128)S(1)}, f32[96,768]{1,0:T(8,128)S(1)}, u32[]{:S(2)}, u32[]{:S(2)}) %collective-permute-start.1) | collective-permute-done | bytes 294944 | tf_op jit(solution)/shard_map/ppermute | solution.py:30
  139.5 0.9 pad_maximum_fusion.1
  140.3 2.0 collective-permute-start.2
  142.4 0.1 copy.39
  142.6 0.4 fusion.17
  143.0 0.4 fusion.56
  143.5 0.8 fusion.15
  144.3 12.8 %collective-permute-done.2 = f32[192,768]{1,0:T(8,128)} collective-permute-done((f32[192,768]{1,0:T(8,128)}, f32[192,768]{1,0:T(8,128)}, u32[]{:S(2)}, u32[]{:S(2)}) %collective-permute-start.2) | collective-permute-done | bytes 589856 | tf_op jit(solution)/shard_map/ppermute | solution.py:30
  157.1 2.0 convolution_subtract_fusion
  159.1 2.9 %collective-permute-start.7 = (f32[256,768]{1,0:T(8,128)S(1)}, f32[256,768]{1,0:T(8,128)}, u32[]{:S(2)}, u32[]{:S(2)}) collective-permute-start(f32[256,768]{1,0:T(8,128)S(1)} %convolution_subtract_fusion), channel_id=1, source_target_pairs={{0,1},{1,2},{2,3},{3,0},{4,5},{5,6},{6,7},{7,4},{8,9},{9,10},{10,1... | collective-permute-start | bytes 2359304 | tf_op jit(solution)/shard_map/ppermute | solution.py:109
  161.9 0.8 fusion.13
  162.8 0.7 broadcast_in_dim.35
  163.5 6.3 %all-to-all-start.4 = ((f32[32,8,256]{2,1,0:T(8,128)}), f32[32,8,256]{2,1,0:T(8,128)S(1)}, u32[]{:S(2)}, u32[]{:S(2)}) async-start(f32[32,8,256]{2,1,0:T(8,128)} %bitcast.8), calls=%async_computation.4 | async-start | bytes 524288 | tf_op jit(solution)/shard_map/all_to_all | solution.py:49
  169.8 4.9 %collective-permute-start.8 = (f32[256,768]{1,0:T(8,128)S(1)}, f32[256,768]{1,0:T(8,128)}, u32[]{:S(2)}, u32[]{:S(2)}) collective-permute-start(f32[256,768]{1,0:T(8,128)S(1)} %convolution_subtract_fusion), channel_id=1, source_target_pairs={{0,2},{1,3},{2,0},{3,1},{4,6},{5,7},{6,4},{7,5},{8,10},{9,11},{10,... | collective-permute-start | bytes 2359304 | tf_op jit(solution)/shard_map/ppermute | solution.py:109
  174.7 26.6 %all-to-all-done.4 = f32[32,8,256]{2,1,0:T(8,128)S(1)} async-done(((f32[32,8,256]{2,1,0:T(8,128)}), f32[32,8,256]{2,1,0:T(8,128)S(1)}, u32[]{:S(2)}, u32[]{:S(2)}) %all-to-all-start.4) | async-done | bytes 262176 | tf_op jit(solution)/shard_map/all_to_all | solution.py:49
  201.3 9.4 %collective-permute-start.10 = (f32[8,256]{1,0:T(8,128)S(1)}, f32[8,256]{1,0:T(8,128)S(1)}, u32[]{:S(2)}, u32[]{:S(2)}) collective-permute-start(f32[8,256]{1,0:T(8,128)S(1)} %reduce_sum.29), channel_id=1, source_target_pairs={{0,64},{64,0},{1,65},{65,1},{2,66},{66,2},{3,67},{67,3},{4,68},{68... | collective-permute-start | bytes 24584 | tf_op jit(solution)/shard_map/ppermute | solution.py:51
  210.7 3.7 %collective-permute-done.10 = f32[8,256]{1,0:T(8,128)S(1)} collective-permute-done((f32[8,256]{1,0:T(8,128)S(1)}, f32[8,256]{1,0:T(8,128)S(1)}, u32[]{:S(2)}, u32[]{:S(2)}) %collective-permute-start.10) | collective-permute-done | bytes 8224 | tf_op jit(solution)/shard_map/ppermute | solution.py:51
  214.5 0.6 broadcast_in_dim.36
  215.1 5.8 %all-to-all-start.5 = ((f32[8,8,256]{2,1,0:T(8,128)}), f32[8,8,256]{2,1,0:T(8,128)S(1)}, u32[]{:S(2)}, u32[]{:S(2)}) async-start(f32[8,8,256]{2,1,0:T(8,128)} %broadcast_in_dim.36), calls=%async_computation.5 | async-start | bytes 131072 | tf_op jit(solution)/shard_map/all_to_all | solution.py:42
  220.9 1.9 collective-permute-start.9
  222.9 7.8 %all-to-all-done.5 = f32[8,8,256]{2,1,0:T(8,128)S(1)} async-done(((f32[8,8,256]{2,1,0:T(8,128)}), f32[8,8,256]{2,1,0:T(8,128)S(1)}, u32[]{:S(2)}, u32[]{:S(2)}) %all-to-all-start.5) | async-done | bytes 65568 | tf_op jit(solution)/shard_map/all_to_all | solution.py:42
  230.7 0.7 broadcast_in_dim.37
  231.4 3.6 %all-to-all-start.6 = ((f32[4,8,8,256]{3,2,1,0:T(8,128)}), f32[4,8,8,256]{3,2,1,0:T(8,128)S(1)}, u32[]{:S(2)}, u32[]{:S(2)}) async-start(f32[4,8,8,256]{3,2,1,0:T(8,128)} %broadcast_in_dim.37), calls=%async_computation.6 | async-start | bytes 524288 | tf_op jit(solution)/shard_map/all_to_all | solution.py:42
  235.0 0.1 broadcast_in_dim.28
  235.1 1.4 fusion.3
  236.5 5.1 %all-to-all-done.6 = f32[4,8,8,256]{3,2,1,0:T(8,128)S(1)} async-done(((f32[4,8,8,256]{3,2,1,0:T(8,128)}), f32[4,8,8,256]{3,2,1,0:T(8,128)S(1)}, u32[]{:S(2)}, u32[]{:S(2)}) %all-to-all-start.6) | async-done | bytes 262176 | tf_op jit(solution)/shard_map/all_to_all | solution.py:42
  241.6 2.5 %fusion.2 = f32[128,3072]{0,1:T(8,128)S(1)} fusion(f32[128,3072]{0,1:T(8,128)S(1)} %fusion.3, s32[]{:T(128)S(6)} %select_n.159, f32[256,768]{1,0:T(8,128)} %collective-permute-done.7, f32[128,256]{1,0:T(8,128)S(1)} %copy-done.1), kind=kOutput, calls=%fused_computation.6 | convolution fusion | flops 301989888 | bytes 1310724 | tf_op jit(solution)/shard_map/dot_general | solution.py:14
  244.2 2.6 %fusion.1 = f32[128,3072]{0,1:T(8,128)S(1)} fusion(f32[128,3072]{0,1:T(8,128)S(1)} %fusion.2, s32[]{:T(128)S(6)} %select_n.161, f32[256,768]{1,0:T(8,128)} %collective-permute-done.8, f32[128,256]{1,0:T(8,128)S(1)} %copy-done.1), kind=kOutput, calls=%fused_computation.4 | convolution fusion | flops 301989888 | bytes 1310724 | tf_op jit(solution)/shard_map/dot_general | solution.py:14
  246.8 2.5 %fusion = f32[128,3072]{0,1:T(8,128)S(1)} fusion(f32[128,3072]{0,1:T(8,128)S(1)} %fusion.1, s32[]{:T(128)S(6)} %select_n.163, f32[256,768]{1,0:T(8,128)} %collective-permute-done.9, f32[128,256]{1,0:T(8,128)S(1)} %copy-done.1), kind=kOutput, calls=%fused_computation.2 | convolution fusion | flops 301989888 | bytes 1310724 | tf_op jit(solution)/shard_map/dot_general | solution.py:14
  249.3 0.4 fusion.12
  249.7 0.4 fusion.11
  250.1 1.6 copy.42
  (32 shorter events, 0.3 us)
Async XLA Ops:
  0.0 1.8 copy-start
  14.4 11.8 %collective-permute-start.3 = (f32[32,768]{1,0:T(8,128)S(1)}, f32[32,768]{1,0:T(8,128)S(1)}, u32[]{:S(2)}, u32[]{:S(2)}) collective-permute-start(f32[32,768]{1,0:T(8,128)S(1)} %slice_bitcast_fusion), channel_id=1, source_target_pairs={{0,16},{4,20},{8,24},{12,28},{16,0},{20,4},{24,8},{28,12},{1,17},{... | collective-permute-start | bytes 294920 | tf_op jit(solution)/shard_map/ppermute | solution.py:30
  26.3 11.7 %collective-permute-start.4 = (f32[64,768]{1,0:T(8,128)S(1)}, f32[64,768]{1,0:T(8,128)S(1)}, u32[]{:S(2)}, u32[]{:S(2)}) collective-permute-start(f32[64,768]{1,0:T(8,128)S(1)} %pad_maximum_fusion.7), channel_id=1, source_target_pairs={{0,8},{4,12},{8,0},{12,4},{16,24},{20,28},{24,16},{28,20},{1,9},{5... | collective-permute-start | bytes 589832 | tf_op jit(solution)/shard_map/ppermute | solution.py:30
  38.0 16.6 %collective-permute-start.5 = (f32[128,768]{1,0:T(8,128)S(1)}, f32[128,768]{1,0:T(8,128)S(1)}, u32[]{:S(2)}, u32[]{:S(2)}) collective-permute-start(f32[128,768]{1,0:T(8,128)S(1)} %pad_maximum_fusion.5), channel_id=1, source_target_pairs={{0,4},{4,0},{8,12},{12,8},{16,20},{20,16},{24,28},{28,24},{1,5},{5... | collective-permute-start | bytes 1179656 | tf_op jit(solution)/shard_map/ppermute | solution.py:30
  54.6 1.3 copy-start.2
  55.5 44.0 %copy-start.4 = (f32[256,256]{1,0:T(8,128)S(1)}, f32[256,256]{1,0:T(8,128)}, u32[]{:S(2)}) copy-start(f32[256,256]{1,0:T(8,128)} %param.11) | copy-start | bytes 786436
  74.2 17.1 %collective-permute-start.6 = (f32[12,256]{1,0:T(8,128)S(1)}, f32[12,256]{1,0:T(8,128)S(1)}, u32[]{:S(2)}, u32[]{:S(2)}) collective-permute-start(f32[12,256]{1,0:T(8,128)S(1)} %reduce_sum.28), channel_id=1, source_target_pairs={{0,64},{64,0},{1,65},{65,1},{2,66},{66,2},{3,67},{67,3},{4,68},{68... | collective-permute-start | bytes 36872 | tf_op jit(solution)/shard_map/ppermute | solution.py:51
  92.0 34.1 %all-to-all-start.2 = ((f32[8,12,256]{2,1,0:T(8,128)}), f32[8,12,256]{2,1,0:T(8,128)S(1)}, u32[]{:S(2)}, u32[]{:S(2)}) async-start(f32[8,12,256]{2,1,0:T(8,128)} %broadcast_in_dim.31), calls=%async_computation.2 | async-start | bytes 262144 | tf_op jit(solution)/shard_map/all_to_all | solution.py:42
  99.9 24.2 %collective-permute-start = (f32[48,768]{1,0:T(8,128)S(1)}, f32[48,768]{1,0:T(8,128)S(1)}, u32[]{:S(2)}, u32[]{:S(2)}) collective-permute-start(f32[48,768]{1,0:T(8,128)S(1)} %reshape.138), channel_id=1, source_target_pairs={{0,16},{4,20},{8,24},{12,28},{16,0},{20,4},{24,8},{28,12},{1,17},{... | collective-permute-start | bytes 442376 | tf_op jit(solution)/shard_map/ppermute | solution.py:30
  124.2 15.3 %collective-permute-start.1 = (f32[96,768]{1,0:T(8,128)S(1)}, f32[96,768]{1,0:T(8,128)S(1)}, u32[]{:S(2)}, u32[]{:S(2)}) collective-permute-start(f32[96,768]{1,0:T(8,128)S(1)} %pad_maximum_fusion.6), channel_id=1, source_target_pairs={{0,8},{4,12},{8,0},{12,4},{16,24},{20,28},{24,16},{28,20},{1,9},{5... | collective-permute-start | bytes 884744 | tf_op jit(solution)/shard_map/ppermute | solution.py:30
  127.0 15.4 %all-to-all-start.3 = ((f32[4,8,12,256]{3,1,2,0:T(8,128)}), f32[4,8,12,256]{3,1,2,0:T(8,128)S(1)}, u32[]{:S(2)}, u32[]{:S(2)}) async-start(f32[4,8,12,256]{3,1,2,0:T(8,128)} %broadcast_in_dim.32), calls=%async_computation.3 | async-start | bytes 786432 | tf_op jit(solution)/shard_map/all_to_all | solution.py:42
  140.3 3.1 %copy-start.3 = (f32[128,768]{1,0:T(8,128)S(1)}, f32[128,768]{1,0:T(8,128)}, u32[]{:S(2)}) copy-start(f32[128,768]{1,0:T(8,128)} %copy-done.2) | copy-start | bytes 1179652
  140.3 16.7 %collective-permute-start.2 = (f32[192,768]{1,0:T(8,128)}, f32[192,768]{1,0:T(8,128)}, u32[]{:S(2)}, u32[]{:S(2)}) collective-permute-start(f32[192,768]{1,0:T(8,128)} %pad_maximum_fusion.1), channel_id=1, source_target_pairs={{0,4},{4,0},{8,12},{12,8},{16,20},{20,16},{24,28},{28,24},{1,5},{5... | collective-permute-start | bytes 1769480 | tf_op jit(solution)/shard_map/ppermute | solution.py:30
  159.1 82.5 %collective-permute-start.7 = (f32[256,768]{1,0:T(8,128)S(1)}, f32[256,768]{1,0:T(8,128)}, u32[]{:S(2)}, u32[]{:S(2)}) collective-permute-start(f32[256,768]{1,0:T(8,128)S(1)} %convolution_subtract_fusion), channel_id=1, source_target_pairs={{0,1},{1,2},{2,3},{3,0},{4,5},{5,6},{6,7},{7,4},{8,9},{9,10},{10,1... | collective-permute-start | bytes 2359304 | tf_op jit(solution)/shard_map/ppermute | solution.py:109
  163.5 37.8 %all-to-all-start.4 = ((f32[32,8,256]{2,1,0:T(8,128)}), f32[32,8,256]{2,1,0:T(8,128)S(1)}, u32[]{:S(2)}, u32[]{:S(2)}) async-start(f32[32,8,256]{2,1,0:T(8,128)} %bitcast.8), calls=%async_computation.4 | async-start | bytes 524288 | tf_op jit(solution)/shard_map/all_to_all | solution.py:49
  169.8 65.3 %copy-start.1 = (f32[128,256]{1,0:T(8,128)S(1)}, f32[128,256]{1,0:T(8,128)}, u32[]{:S(2)}) copy-start(f32[128,256]{1,0:T(8,128)} %param.9) | copy-start | bytes 393220
  169.8 74.4 %collective-permute-start.8 = (f32[256,768]{1,0:T(8,128)S(1)}, f32[256,768]{1,0:T(8,128)}, u32[]{:S(2)}, u32[]{:S(2)}) collective-permute-start(f32[256,768]{1,0:T(8,128)S(1)} %convolution_subtract_fusion), channel_id=1, source_target_pairs={{0,2},{1,3},{2,0},{3,1},{4,6},{5,7},{6,4},{7,5},{8,10},{9,11},{10,... | collective-permute-start | bytes 2359304 | tf_op jit(solution)/shard_map/ppermute | solution.py:109
  201.3 13.1 %collective-permute-start.10 = (f32[8,256]{1,0:T(8,128)S(1)}, f32[8,256]{1,0:T(8,128)S(1)}, u32[]{:S(2)}, u32[]{:S(2)}) collective-permute-start(f32[8,256]{1,0:T(8,128)S(1)} %reduce_sum.29), channel_id=1, source_target_pairs={{0,64},{64,0},{1,65},{65,1},{2,66},{66,2},{3,67},{67,3},{4,68},{68... | collective-permute-start | bytes 24584 | tf_op jit(solution)/shard_map/ppermute | solution.py:51
  215.1 15.6 %all-to-all-start.5 = ((f32[8,8,256]{2,1,0:T(8,128)}), f32[8,8,256]{2,1,0:T(8,128)S(1)}, u32[]{:S(2)}, u32[]{:S(2)}) async-start(f32[8,8,256]{2,1,0:T(8,128)} %broadcast_in_dim.36), calls=%async_computation.5 | async-start | bytes 131072 | tf_op jit(solution)/shard_map/all_to_all | solution.py:42
  220.9 25.9 %collective-permute-start.9 = (f32[256,768]{1,0:T(8,128)S(1)}, f32[256,768]{1,0:T(8,128)}, u32[]{:S(2)}, u32[]{:S(2)}) collective-permute-start(f32[256,768]{1,0:T(8,128)S(1)} %convolution_subtract_fusion), channel_id=1, source_target_pairs={{0,3},{1,0},{2,1},{3,2},{4,7},{5,4},{6,5},{7,6},{8,11},{9,8},{10,9... | collective-permute-start | bytes 2359304 | tf_op jit(solution)/shard_map/ppermute | solution.py:109
  231.4 10.2 %all-to-all-start.6 = ((f32[4,8,8,256]{3,2,1,0:T(8,128)}), f32[4,8,8,256]{3,2,1,0:T(8,128)S(1)}, u32[]{:S(2)}, u32[]{:S(2)}) async-start(f32[4,8,8,256]{3,2,1,0:T(8,128)} %broadcast_in_dim.37), calls=%async_computation.6 | async-start | bytes 524288 | tf_op jit(solution)/shard_map/all_to_all | solution.py:42
  244.2 5.5 %copy-start.5 = (f32[256,256]{1,0:T(8,128)S(1)}, f32[256,256]{1,0:T(8,128)}, u32[]{:S(2)}) copy-start(f32[256,256]{1,0:T(8,128)} %param.13) | copy-start | bytes 786436
where the time goes:
time: 255 us; the launch traced here: 252 us
  starting transfers between devices  100 us (39%)
  waiting for transfers between devices  95.7 us (38%)
  blocking collectives  29.3 us (11%)
  matrix products  16.4 us (6%)
  local copies, waits for them, and re-layouts  5.88 us (2%)
  other arithmetic  3.67 us (1%)
    ppermute x6, waiting for transfers between devices, doubled(): other = lax.ppermute(block, axis, [(i, i ^ hop) for i in range(width)])  51.4 us
    ppermute x6, starting transfers between devices, doubled(): other = lax.ppermute(block, axis, [(i, i ^ hop) for i in range(width)])  38.6 us
    all_to_all x1, waiting for transfers between devices, summed_rows(): parts = lax.all_to_all(parts, ('x', 'core', 'y'), 0, 0)  26.6 us
    ppermute x2, starting transfers between devices, summed_rows(): own = own + lax.ppermute(own, 'zh', [(0, 1), (1, 0)])  25.4 us
    all_to_all x4, starting transfers between devices, spread(): return lax.all_to_all(copies, axis, 0, 0)  20.3 us
    all_to_all x1, blocking collectives, summed_rows(): parts = lax.all_to_all(parts, ('x', 'core', 'y'), 0, 0)  18.3 us
    dot_general x16, matrix products, product(): lax.dot_general(left, right, (((contract[0],), (contract[1],)), ((), ()))...  16.4 us
    all_to_all x4, waiting for transfers between devices, spread(): return lax.all_to_all(copies, axis, 0, 0)  12.8 us
  transfers between devices with their start and end apart: 16, of which 11 were waited for; matrix products, arithmetic and copies ran while one was open for 5% of the time, Pallas kernels for 0%

commit v1 on v0

--- a/solution.py
+++ b/solution.py
@@ -48,8 +48,10 @@
     parts = jnp.broadcast_to(parts[None], (group, *parts.shape)).reshape(-1, *parts.shape[1:])
     parts = lax.all_to_all(parts, ("x", "core", "y"), 0, 0)
     own = jnp.sum(parts, axis=0)
-    own = own + lax.ppermute(own, "zh", [(0, 1), (1, 0)])
-    return spread(spread(own, "z"), "y")
+    halves = spread(own, ("zh", "z"))
+    halves = halves.reshape(lax.axis_size("zh"), -1, *own.shape)
+    column = jnp.sum(halves, axis=0)
+    return spread(column, "y")
 
 
 def per_device(

time: 255 us -> 234 us (0.918)
  starting transfers between devices: 100 us -> 82.8 us
  waiting for transfers between devices: 95.7 us -> 92.2 us
    ppermute x2 -> x0, starting transfers between devices: 25.4 us -> none  [summed_rows(): own = own + lax.ppermute(own, 'zh', [(0, 1), (1, 0)])]
    all_to_all x4, starting transfers between devices: 20.3 us -> 28.5 us  [spread(): return lax.all_to_all(copies, axis, 0, 0)]
    ppermute x6, waiting for transfers between devices: 51.4 us -> 56.9 us  [doubled(): other = lax.ppermute(block, axis, [(i, i ^ hop) for i in range(width)])]
    ppermute x2 -> x0, waiting for transfers between devices: 4.86 us -> none  [summed_rows(): own = own + lax.ppermute(own, 'zh', [(0, 1), (1, 0)])]
    all_to_all x4, waiting for transfers between devices: 12.8 us -> 8.58 us  [spread(): return lax.all_to_all(copies, axis, 0, 0)]
  transfers between devices with their start and end apart: 16 -> 14, of which waited for: 11 -> 8; matrix products, arithmetic and copies ran while one was open for 5% -> 7% of each run, Pallas kernels for 0% -> 0%
where the time goes in v1:
time: 234 us; the launch traced here: 231 us
  waiting for transfers between devices  92.2 us (39%)
  starting transfers between devices  82.8 us (35%)
  blocking collectives  29.3 us (13%)
  matrix products  16.4 us (7%)
  local copies, waits for them, and re-layouts  5.98 us (3%)
  other arithmetic  3.7 us (2%)
    ppermute x6, waiting for transfers between devices, doubled(): other = lax.ppermute(block, axis, [(i, i ^ hop) for i in range(width)])  56.9 us
    ppermute x6, starting transfers between devices, doubled(): other = lax.ppermute(block, axis, [(i, i ^ hop) for i in range(width)])  38.5 us
    all_to_all x4, starting transfers between devices, spread(): return lax.all_to_all(copies, axis, 0, 0)  28.5 us
    all_to_all x1, waiting for transfers between devices, summed_rows(): parts = lax.all_to_all(parts, ('x', 'core', 'y'), 0, 0)  26.8 us
    all_to_all x1, blocking collectives, summed_rows(): parts = lax.all_to_all(parts, ('x', 'core', 'y'), 0, 0)  18.3 us
    dot_general x16, matrix products, product(): lax.dot_general(left, right, (((contract[0],), (contract[1],)), ((), ()))...  16.4 us
    all_to_all x1, blocking collectives, per_device(): packed = lax.all_to_all(packed, 'y', 0, 0)  11 us
    ppermute x3, starting transfers between devices, per_device(): blocks.append(lax.ppermute(transformed, 'y', turn))  9.78 us
  transfers between devices with their start and end apart: 14, of which 8 were waited for; matrix products, arithmetic and copies ran while one was open for 7% of the time, Pallas kernels for 0%

profile of v1, /device:TPU:1, one launch (start us, length us, event | category | flops | bytes accessed | tf_op | source)
XLA Modules:
  0.0 231.0 jit_solution(137719516806464915)
XLA Ops:
  0.0 0.7 and_select_fusion.7
  0.7 0.7 broadcast_compare_fusion
  1.4 0.2 convert_reduce_fusion
  1.6 0.2 fusion.25
  1.8 0.3 fusion.55
  2.2 1.0 pad_maximum_fusion.4
  3.1 0.2 reshape.143
  3.3 0.1 copy.50
  3.4 11.0 %all_to_all.35 = f32[4,28,768]{2,1,0:T(8,128)S(1)} all-to-all(f32[4,28,768]{2,1,0:T(8,128)S(1)} %bitcast.57), channel_id=1, replica_groups=mesh['x'=4,'zh'=2,'core'=2,'z'=8,'y'=4] {'y'}, dimensions={0} | all-to-all | bytes 688128 | tf_op jit(solution)/shard_map/all_to_all | solution.py:84
  14.4 9.8 %collective-permute-start.3 = (f32[32,768]{1,0:T(8,128)S(1)}, f32[32,768]{1,0:T(8,128)S(1)}, u32[]{:S(2)}, u32[]{:S(2)}) collective-permute-start(f32[32,768]{1,0:T(8,128)S(1)} %slice_bitcast_fusion), channel_id=1, source_target_pairs={{0,16},{4,20},{8,24},{12,28},{16,0},{20,4},{24,8},{28,12},{1,17},{... | collective-permute-start | bytes 294920 | tf_op jit(solution)/shard_map/ppermute | solution.py:30
  24.2 2.0 collective-permute-done.3
  26.3 8.7 %collective-permute-start.4 = (f32[64,768]{1,0:T(8,128)S(1)}, f32[64,768]{1,0:T(8,128)S(1)}, u32[]{:S(2)}, u32[]{:S(2)}) collective-permute-start(f32[64,768]{1,0:T(8,128)S(1)} %pad_maximum_fusion.7), channel_id=1, source_target_pairs={{0,8},{4,12},{8,0},{12,4},{16,24},{20,28},{24,16},{28,20},{1,9},{5... | collective-permute-start | bytes 589832 | tf_op jit(solution)/shard_map/ppermute | solution.py:30
  34.9 3.0 %collective-permute-done.4 = f32[64,768]{1,0:T(8,128)S(1)} collective-permute-done((f32[64,768]{1,0:T(8,128)S(1)}, f32[64,768]{1,0:T(8,128)S(1)}, u32[]{:S(2)}, u32[]{:S(2)}) %collective-permute-start.4) | collective-permute-done | bytes 196640 | tf_op jit(solution)/shard_map/ppermute | solution.py:30
  38.0 8.9 %collective-permute-start.5 = (f32[128,768]{1,0:T(8,128)S(1)}, f32[128,768]{1,0:T(8,128)S(1)}, u32[]{:S(2)}, u32[]{:S(2)}) collective-permute-start(f32[128,768]{1,0:T(8,128)S(1)} %pad_maximum_fusion.5), channel_id=1, source_target_pairs={{0,4},{4,0},{8,12},{12,8},{16,20},{20,16},{24,28},{28,24},{1,5},{5... | collective-permute-start | bytes 1179656 | tf_op jit(solution)/shard_map/ppermute | solution.py:30
  47.0 7.7 %collective-permute-done.5 = f32[128,768]{1,0:T(8,128)S(1)} collective-permute-done((f32[128,768]{1,0:T(8,128)S(1)}, f32[128,768]{1,0:T(8,128)S(1)}, u32[]{:S(2)}, u32[]{:S(2)}) %collective-permute-start.5) | collective-permute-done | bytes 393248 | tf_op jit(solution)/shard_map/ppermute | solution.py:30
  54.6 0.8 fusion.16
  55.5 0.3 fusion.19
  55.8 0.0 copy-start.4
  55.8 0.1 broadcast_in_dim.30
  55.9 18.3 %all_to_all.36 = f32[32,12,256]{2,1,0:T(8,128)S(1)} all-to-all(f32[32,12,256]{2,1,0:T(8,128)S(1)} %bitcast.56), channel_id=1, replica_groups=mesh['x'=4,'zh'=2,'core'=2,'z'=8,'y'=4] {'x','core','y'}, dimensions={0} | all-to-all | bytes 786432 | tf_op jit(solution)/shard_map/all_to_all | solution.py:49
  74.2 0.1 reduce_sum.46
  74.2 0.7 broadcast_in_dim.31
  75.0 15.5 %all-to-all-start.2 = ((f32[16,12,256]{2,1,0:T(8,128)}), f32[16,12,256]{2,1,0:T(8,128)S(1)}, u32[]{:S(2)}, u32[]{:S(2)}) async-start(f32[16,12,256]{2,1,0:T(8,128)} %broadcast_in_dim.31), calls=%async_computation.2 | async-start | bytes 524288 | tf_op jit(solution)/shard_map/all_to_all | solution.py:42
  90.4 0.5 fusion.18
  90.9 7.2 %collective-permute-start = (f32[48,768]{1,0:T(8,128)S(1)}, f32[48,768]{1,0:T(8,128)S(1)}, u32[]{:S(2)}, u32[]{:S(2)}) collective-permute-start(f32[48,768]{1,0:T(8,128)S(1)} %reshape.144), channel_id=1, source_target_pairs={{0,16},{4,20},{8,24},{12,28},{16,0},{20,4},{24,8},{28,12},{1,17},{... | collective-permute-start | bytes 442376 | tf_op jit(solution)/shard_map/ppermute | solution.py:30
  98.1 21.9 %collective-permute-done = f32[48,768]{1,0:T(8,128)S(1)} collective-permute-done((f32[48,768]{1,0:T(8,128)S(1)}, f32[48,768]{1,0:T(8,128)S(1)}, u32[]{:S(2)}, u32[]{:S(2)}) %collective-permute-start) | collective-permute-done | bytes 147488 | tf_op jit(solution)/shard_map/ppermute | solution.py:30
  120.1 1.9 collective-permute-start.1
  122.0 0.0 all-to-all-done.2
  122.0 0.1 copy.48
  122.1 0.8 broadcast_in_dim.32
  122.9 3.5 %all-to-all-start.3 = ((f32[4,8,12,256]{3,1,2,0:T(8,128)}), f32[4,8,12,256]{3,1,2,0:T(8,128)S(1)}, u32[]{:S(2)}, u32[]{:S(2)}) async-start(f32[4,8,12,256]{3,1,2,0:T(8,128)} %broadcast_in_dim.32), calls=%async_computation.3 | async-start | bytes 786432 | tf_op jit(solution)/shard_map/all_to_all | solution.py:42
  126.4 9.5 %collective-permute-done.1 = f32[96,768]{1,0:T(8,128)S(1)} collective-permute-done((f32[96,768]{1,0:T(8,128)S(1)}, f32[96,768]{1,0:T(8,128)S(1)}, u32[]{:S(2)}, u32[]{:S(2)}) %collective-permute-start.1) | collective-permute-done | bytes 294944 | tf_op jit(solution)/shard_map/ppermute | solution.py:30
  135.9 0.9 pad_maximum_fusion.1
  136.7 2.0 collective-permute-start.2
  138.8 0.0 all-to-all-done.3
  138.8 0.1 copy.40
  139.0 0.4 fusion.17
  139.4 0.4 fusion.56
  139.9 0.8 fusion.15
  140.7 12.8 %collective-permute-done.2 = f32[192,768]{1,0:T(8,128)} collective-permute-done((f32[192,768]{1,0:T(8,128)}, f32[192,768]{1,0:T(8,128)}, u32[]{:S(2)}, u32[]{:S(2)}) %collective-permute-start.2) | collective-permute-done | bytes 589856 | tf_op jit(solution)/shard_map/ppermute | solution.py:30
  153.5 2.0 convolution_subtract_fusion
  155.4 3.1 %collective-permute-start.6 = (f32[256,768]{1,0:T(8,128)S(1)}, f32[256,768]{1,0:T(8,128)}, u32[]{:S(2)}, u32[]{:S(2)}) collective-permute-start(f32[256,768]{1,0:T(8,128)S(1)} %convolution_subtract_fusion), channel_id=1, source_target_pairs={{0,1},{1,2},{2,3},{3,0},{4,5},{5,6},{6,7},{7,4},{8,9},{9,10},{10,1... | collective-permute-start | bytes 2359304 | tf_op jit(solution)/shard_map/ppermute | solution.py:111
  158.5 0.8 fusion.13
  159.4 0.0 copy-start.1
  159.4 0.7 broadcast_in_dim.35
  160.1 6.1 %all-to-all-start.4 = ((f32[32,8,256]{2,1,0:T(8,128)}), f32[32,8,256]{2,1,0:T(8,128)S(1)}, u32[]{:S(2)}, u32[]{:S(2)}) async-start(f32[32,8,256]{2,1,0:T(8,128)} %bitcast.9), calls=%async_computation.4 | async-start | bytes 524288 | tf_op jit(solution)/shard_map/all_to_all | solution.py:49
  166.2 4.8 %collective-permute-start.7 = (f32[256,768]{1,0:T(8,128)S(1)}, f32[256,768]{1,0:T(8,128)}, u32[]{:S(2)}, u32[]{:S(2)}) collective-permute-start(f32[256,768]{1,0:T(8,128)S(1)} %convolution_subtract_fusion), channel_id=1, source_target_pairs={{0,2},{1,3},{2,0},{3,1},{4,6},{5,7},{6,4},{7,5},{8,10},{9,11},{10,... | collective-permute-start | bytes 2359304 | tf_op jit(solution)/shard_map/ppermute | solution.py:111
  170.9 26.8 %all-to-all-done.4 = f32[32,8,256]{2,1,0:T(8,128)S(1)} async-done(((f32[32,8,256]{2,1,0:T(8,128)}), f32[32,8,256]{2,1,0:T(8,128)S(1)}, u32[]{:S(2)}, u32[]{:S(2)}) %all-to-all-start.4) | async-done | bytes 262176 | tf_op jit(solution)/shard_map/all_to_all | solution.py:49
  197.7 0.7 broadcast_in_dim.36
  198.4 6.0 %all-to-all-start.5 = ((f32[16,8,256]{2,1,0:T(8,128)}), f32[16,8,256]{2,1,0:T(8,128)S(1)}, u32[]{:S(2)}, u32[]{:S(2)}) async-start(f32[16,8,256]{2,1,0:T(8,128)} %broadcast_in_dim.36), calls=%async_computation.5 | async-start | bytes 262144 | tf_op jit(solution)/shard_map/all_to_all | solution.py:42
  204.4 1.9 collective-permute-start.8
  206.4 0.1 broadcast_in_dim.28
  206.5 1.4 fusion.3
  207.9 8.6 %all-to-all-done.5 = f32[16,8,256]{2,1,0:T(8,128)S(1)} async-done(((f32[16,8,256]{2,1,0:T(8,128)}), f32[16,8,256]{2,1,0:T(8,128)S(1)}, u32[]{:S(2)}, u32[]{:S(2)}) %all-to-all-start.5) | async-done | bytes 131104 | tf_op jit(solution)/shard_map/all_to_all | solution.py:42
  216.5 0.7 broadcast_in_dim.37
  217.2 3.6 %all-to-all-start.6 = ((f32[4,8,8,256]{3,2,1,0:T(8,128)}), f32[4,8,8,256]{3,2,1,0:T(8,128)S(1)}, u32[]{:S(2)}, u32[]{:S(2)}) async-start(f32[4,8,8,256]{3,2,1,0:T(8,128)} %broadcast_in_dim.37), calls=%async_computation.6 | async-start | bytes 524288 | tf_op jit(solution)/shard_map/all_to_all | solution.py:42
  220.8 2.5 %fusion.2 = f32[128,3072]{0,1:T(8,128)S(1)} fusion(f32[128,3072]{0,1:T(8,128)S(1)} %fusion.3, s32[]{:T(128)S(6)} %select_n.159, f32[256,768]{1,0:T(8,128)} %collective-permute-done.6, f32[128,256]{1,0:T(8,128)S(1)} %copy-done.1), kind=kOutput, calls=%fused_computation.6 | convolution fusion | flops 301989888 | bytes 1310724 | tf_op jit(solution)/shard_map/dot_general | solution.py:14
  223.4 2.5 %fusion.1 = f32[128,3072]{0,1:T(8,128)S(1)} fusion(f32[128,3072]{0,1:T(8,128)S(1)} %fusion.2, s32[]{:T(128)S(6)} %select_n.161, f32[256,768]{1,0:T(8,128)} %collective-permute-done.7, f32[128,256]{1,0:T(8,128)S(1)} %copy-done.1), kind=kOutput, calls=%fused_computation.4 | convolution fusion | flops 301989888 | bytes 1310724 | tf_op jit(solution)/shard_map/dot_general | solution.py:14
  225.9 0.0 copy-start.5
  226.0 2.6 %fusion = f32[128,3072]{0,1:T(8,128)S(1)} fusion(f32[128,3072]{0,1:T(8,128)S(1)} %fusion.1, s32[]{:T(128)S(6)} %select_n.163, f32[256,768]{1,0:T(8,128)} %collective-permute-done.8, f32[128,256]{1,0:T(8,128)S(1)} %copy-done.1), kind=kOutput, calls=%fused_computation.2 | convolution fusion | flops 301989888 | bytes 1310724 | tf_op jit(solution)/shard_map/dot_general | solution.py:14
  228.5 0.0 all-to-all-done.6
  228.6 0.4 fusion.12
  229.0 0.4 fusion.11
  229.4 1.6 copy.43
  (28 shorter events, 0.3 us)
Async XLA Ops:
  0.0 1.8 copy-start
  14.4 11.8 %collective-permute-start.3 = (f32[32,768]{1,0:T(8,128)S(1)}, f32[32,768]{1,0:T(8,128)S(1)}, u32[]{:S(2)}, u32[]{:S(2)}) collective-permute-start(f32[32,768]{1,0:T(8,128)S(1)} %slice_bitcast_fusion), channel_id=1, source_target_pairs={{0,16},{4,20},{8,24},{12,28},{16,0},{20,4},{24,8},{28,12},{1,17},{... | collective-permute-start | bytes 294920 | tf_op jit(solution)/shard_map/ppermute | solution.py:30
  26.3 11.7 %collective-permute-start.4 = (f32[64,768]{1,0:T(8,128)S(1)}, f32[64,768]{1,0:T(8,128)S(1)}, u32[]{:S(2)}, u32[]{:S(2)}) collective-permute-start(f32[64,768]{1,0:T(8,128)S(1)} %pad_maximum_fusion.7), channel_id=1, source_target_pairs={{0,8},{4,12},{8,0},{12,4},{16,24},{20,28},{24,16},{28,20},{1,9},{5... | collective-permute-start | bytes 589832 | tf_op jit(solution)/shard_map/ppermute | solution.py:30
  38.0 16.6 %collective-permute-start.5 = (f32[128,768]{1,0:T(8,128)S(1)}, f32[128,768]{1,0:T(8,128)S(1)}, u32[]{:S(2)}, u32[]{:S(2)}) collective-permute-start(f32[128,768]{1,0:T(8,128)S(1)} %pad_maximum_fusion.5), channel_id=1, source_target_pairs={{0,4},{4,0},{8,12},{12,8},{16,20},{20,16},{24,28},{28,24},{1,5},{5... | collective-permute-start | bytes 1179656 | tf_op jit(solution)/shard_map/ppermute | solution.py:30
  54.6 1.3 copy-start.2
  55.8 34.6 %copy-start.4 = (f32[256,256]{1,0:T(8,128)S(1)}, f32[256,256]{1,0:T(8,128)}, u32[]{:S(2)}) copy-start(f32[256,256]{1,0:T(8,128)} %param.11) | copy-start | bytes 786436
  75.0 47.0 %all-to-all-start.2 = ((f32[16,12,256]{2,1,0:T(8,128)}), f32[16,12,256]{2,1,0:T(8,128)S(1)}, u32[]{:S(2)}, u32[]{:S(2)}) async-start(f32[16,12,256]{2,1,0:T(8,128)} %broadcast_in_dim.31), calls=%async_computation.2 | async-start | bytes 524288 | tf_op jit(solution)/shard_map/all_to_all | solution.py:42
  90.9 29.1 %collective-permute-start = (f32[48,768]{1,0:T(8,128)S(1)}, f32[48,768]{1,0:T(8,128)S(1)}, u32[]{:S(2)}, u32[]{:S(2)}) collective-permute-start(f32[48,768]{1,0:T(8,128)S(1)} %reshape.144), channel_id=1, source_target_pairs={{0,16},{4,20},{8,24},{12,28},{16,0},{20,4},{24,8},{28,12},{1,17},{... | collective-permute-start | bytes 442376 | tf_op jit(solution)/shard_map/ppermute | solution.py:30
  120.1 15.8 %collective-permute-start.1 = (f32[96,768]{1,0:T(8,128)S(1)}, f32[96,768]{1,0:T(8,128)S(1)}, u32[]{:S(2)}, u32[]{:S(2)}) collective-permute-start(f32[96,768]{1,0:T(8,128)S(1)} %pad_maximum_fusion.6), channel_id=1, source_target_pairs={{0,8},{4,12},{8,0},{12,4},{16,24},{20,28},{24,16},{28,20},{1,9},{5... | collective-permute-start | bytes 884744 | tf_op jit(solution)/shard_map/ppermute | solution.py:30
  122.9 15.9 %all-to-all-start.3 = ((f32[4,8,12,256]{3,1,2,0:T(8,128)}), f32[4,8,12,256]{3,1,2,0:T(8,128)S(1)}, u32[]{:S(2)}, u32[]{:S(2)}) async-start(f32[4,8,12,256]{3,1,2,0:T(8,128)} %broadcast_in_dim.32), calls=%async_computation.3 | async-start | bytes 786432 | tf_op jit(solution)/shard_map/all_to_all | solution.py:42
  136.7 3.1 %copy-start.3 = (f32[128,768]{1,0:T(8,128)S(1)}, f32[128,768]{1,0:T(8,128)}, u32[]{:S(2)}) copy-start(f32[128,768]{1,0:T(8,128)} %copy-done.2) | copy-start | bytes 1179652
  136.7 16.7 %collective-permute-start.2 = (f32[192,768]{1,0:T(8,128)}, f32[192,768]{1,0:T(8,128)}, u32[]{:S(2)}, u32[]{:S(2)}) collective-permute-start(f32[192,768]{1,0:T(8,128)} %pad_maximum_fusion.1), channel_id=1, source_target_pairs={{0,4},{4,0},{8,12},{12,8},{16,20},{20,16},{24,28},{28,24},{1,5},{5... | collective-permute-start | bytes 1769480 | tf_op jit(solution)/shard_map/ppermute | solution.py:30
  155.4 65.4 %collective-permute-start.6 = (f32[256,768]{1,0:T(8,128)S(1)}, f32[256,768]{1,0:T(8,128)}, u32[]{:S(2)}, u32[]{:S(2)}) collective-permute-start(f32[256,768]{1,0:T(8,128)S(1)} %convolution_subtract_fusion), channel_id=1, source_target_pairs={{0,1},{1,2},{2,3},{3,0},{4,5},{5,6},{6,7},{7,4},{8,9},{9,10},{10,1... | collective-permute-start | bytes 2359304 | tf_op jit(solution)/shard_map/ppermute | solution.py:111
  159.4 47.2 %copy-start.1 = (f32[128,256]{1,0:T(8,128)S(1)}, f32[128,256]{1,0:T(8,128)}, u32[]{:S(2)}) copy-start(f32[128,256]{1,0:T(8,128)} %param.9) | copy-start | bytes 393220
  160.1 37.6 %all-to-all-start.4 = ((f32[32,8,256]{2,1,0:T(8,128)}), f32[32,8,256]{2,1,0:T(8,128)S(1)}, u32[]{:S(2)}, u32[]{:S(2)}) async-start(f32[32,8,256]{2,1,0:T(8,128)} %bitcast.9), calls=%async_computation.4 | async-start | bytes 524288 | tf_op jit(solution)/shard_map/all_to_all | solution.py:49
  166.2 57.2 %collective-permute-start.7 = (f32[256,768]{1,0:T(8,128)S(1)}, f32[256,768]{1,0:T(8,128)}, u32[]{:S(2)}, u32[]{:S(2)}) collective-permute-start(f32[256,768]{1,0:T(8,128)S(1)} %convolution_subtract_fusion), channel_id=1, source_target_pairs={{0,2},{1,3},{2,0},{3,1},{4,6},{5,7},{6,4},{7,5},{8,10},{9,11},{10,... | collective-permute-start | bytes 2359304 | tf_op jit(solution)/shard_map/ppermute | solution.py:111
  198.4 18.1 %all-to-all-start.5 = ((f32[16,8,256]{2,1,0:T(8,128)}), f32[16,8,256]{2,1,0:T(8,128)S(1)}, u32[]{:S(2)}, u32[]{:S(2)}) async-start(f32[16,8,256]{2,1,0:T(8,128)} %broadcast_in_dim.36), calls=%async_computation.5 | async-start | bytes 262144 | tf_op jit(solution)/shard_map/all_to_all | solution.py:42
  204.4 21.6 %collective-permute-start.8 = (f32[256,768]{1,0:T(8,128)S(1)}, f32[256,768]{1,0:T(8,128)}, u32[]{:S(2)}, u32[]{:S(2)}) collective-permute-start(f32[256,768]{1,0:T(8,128)S(1)} %convolution_subtract_fusion), channel_id=1, source_target_pairs={{0,3},{1,0},{2,1},{3,2},{4,7},{5,4},{6,5},{7,6},{8,11},{9,8},{10,9... | collective-permute-start | bytes 2359304 | tf_op jit(solution)/shard_map/ppermute | solution.py:111
  217.2 11.3 %all-to-all-start.6 = ((f32[4,8,8,256]{3,2,1,0:T(8,128)}), f32[4,8,8,256]{3,2,1,0:T(8,128)S(1)}, u32[]{:S(2)}, u32[]{:S(2)}) async-start(f32[4,8,8,256]{3,2,1,0:T(8,128)} %broadcast_in_dim.37), calls=%async_computation.6 | async-start | bytes 524288 | tf_op jit(solution)/shard_map/all_to_all | solution.py:42
  225.9 3.0 %copy-start.5 = (f32[256,256]{1,0:T(8,128)S(1)}, f32[256,256]{1,0:T(8,128)}, u32[]{:S(2)}) copy-start(f32[256,256]{1,0:T(8,128)} %param.13) | copy-start | bytes 786436

commit v2 on v1

--- a/solution.py
+++ b/solution.py
@@ -105,16 +105,19 @@
     gathered = product(onehot(held_at, slots * vec_width), all_slots)
     transformed = gathered - product(coeff, all_reflectors)
 
-    blocks = [transformed]
-    for d in range(1, y_width):
-        turn = [(i, (i + d) % y_width) for i in range(y_width)]
-        blocks.append(lax.ppermute(transformed, "y", turn))
+    ahead = [(i, (i + 1) % y_width) for i in range(y_width)]
+    behind = [(i, (i - 1) % y_width) for i in range(y_width)]
+    before = lax.ppermute(transformed, "y", ahead)
+    after = lax.ppermute(transformed, "y", behind)
+    upper = lax.ppermute(before[: panel // 2], "y", ahead)
+    lower = lax.ppermute(after[panel // 2 :], "y", behind)
+    blocks = [(0, transformed), (1, before), (-1, after), (2, jnp.concatenate([upper, lower], axis=0))]
     cross = summed_rows(product(own_cholesky, transformed, (1, 1)))
     cross = cross.transpose(1, 0, 2, 3).reshape(-1, panel)
     correction = product(secular, cross, (1, 1))
 
     applied = jnp.zeros((secular.shape[0], row_count), jnp.float32)
-    for d, block in enumerate(blocks):
+    for d, block in blocks:
         at = ((y_index - d + y_width) % y_width) * cols
         applied = lax.dynamic_update_slice(applied, product(secular, block), (0, at))
     head = applied[:, :panel]

time: 234 us -> 231 us (0.987)
  the two profiles are of different devices: /device:TPU:1 before, /device:TPU:32 now
where the time goes in v2:
time: 231 us; the launch traced here: 230 us
  starting transfers between devices  79.4 us (34%)
  waiting for transfers between devices  74.4 us (32%)
  blocking collectives  47.9 us (21%)
  matrix products  16.4 us (7%)
  local copies, waits for them, and re-layouts  7.32 us (3%)
  other arithmetic  3.7 us (2%)
    ppermute x6, waiting for transfers between devices, doubled(): other = lax.ppermute(block, axis, [(i, i ^ hop) for i in range(width)])  59.4 us
    all_to_all x2, blocking collectives, summed_rows(): parts = lax.all_to_all(parts, ('x', 'core', 'y'), 0, 0)  35.5 us
    ppermute x6, starting transfers between devices, doubled(): other = lax.ppermute(block, axis, [(i, i ^ hop) for i in range(width)])  33.8 us
    all_to_all x4, starting transfers between devices, spread(): return lax.all_to_all(copies, axis, 0, 0)  31.3 us
    dot_general x16, matrix products, product(): lax.dot_general(left, right, (((contract[0],), (contract[1],)), ((), ()))...  16.4 us
    all_to_all x4, waiting for transfers between devices, spread(): return lax.all_to_all(copies, axis, 0, 0)  12.4 us
    all_to_all x1, blocking collectives, per_device(): packed = lax.all_to_all(packed, 'y', 0, 0)  12.3 us
  transfers between devices with their start and end apart: 14, of which 9 were waited for; matrix products, arithmetic and copies ran while one was open for 7% of the time, Pallas kernels for 0%

profile of v2, /device:TPU:32, one launch (start us, length us, event | category | flops | bytes accessed | tf_op | source)
XLA Modules:
  0.0 229.5 jit_solution(2541084729927823295)
XLA Ops:
  0.0 0.7 and_select_fusion.7
  0.7 0.7 broadcast_compare_fusion
  1.4 0.2 convert_reduce_fusion
  1.6 0.2 fusion.28
  1.8 0.3 fusion.59
  2.2 1.0 pad_maximum_fusion.4
  3.1 0.2 reshape.143
  3.3 0.1 copy.50
  3.4 12.3 %all_to_all.35 = f32[4,28,768]{2,1,0:T(8,128)S(1)} all-to-all(f32[4,28,768]{2,1,0:T(8,128)S(1)} %bitcast.56), channel_id=1, replica_groups=mesh['x'=4,'zh'=2,'core'=2,'z'=8,'y'=4] {'y'}, dimensions={0} | all-to-all | bytes 688128 | tf_op jit(solution)/shard_map/all_to_all | solution.py:84
  15.7 9.1 %collective-permute-start.3 = (f32[32,768]{1,0:T(8,128)S(1)}, f32[32,768]{1,0:T(8,128)S(1)}, u32[]{:S(2)}, u32[]{:S(2)}) collective-permute-start(f32[32,768]{1,0:T(8,128)S(1)} %slice_bitcast_fusion), channel_id=1, source_target_pairs={{0,16},{4,20},{8,24},{12,28},{16,0},{20,4},{24,8},{28,12},{1,17},{... | collective-permute-start | bytes 294920 | tf_op jit(solution)/shard_map/ppermute | solution.py:30
  24.8 6.3 %collective-permute-done.3 = f32[32,768]{1,0:T(8,128)S(1)} collective-permute-done((f32[32,768]{1,0:T(8,128)S(1)}, f32[32,768]{1,0:T(8,128)S(1)}, u32[]{:S(2)}, u32[]{:S(2)}) %collective-permute-start.3) | collective-permute-done | bytes 98336 | tf_op jit(solution)/shard_map/ppermute | solution.py:30
  31.1 4.8 %collective-permute-start.4 = (f32[64,768]{1,0:T(8,128)S(1)}, f32[64,768]{1,0:T(8,128)S(1)}, u32[]{:S(2)}, u32[]{:S(2)}) collective-permute-start(f32[64,768]{1,0:T(8,128)S(1)} %pad_maximum_fusion.7), channel_id=1, source_target_pairs={{0,8},{4,12},{8,0},{12,4},{16,24},{20,28},{24,16},{28,20},{1,9},{5... | collective-permute-start | bytes 589832 | tf_op jit(solution)/shard_map/ppermute | solution.py:30
  35.9 6.4 %collective-permute-done.4 = f32[64,768]{1,0:T(8,128)S(1)} collective-permute-done((f32[64,768]{1,0:T(8,128)S(1)}, f32[64,768]{1,0:T(8,128)S(1)}, u32[]{:S(2)}, u32[]{:S(2)}) %collective-permute-start.4) | collective-permute-done | bytes 196640 | tf_op jit(solution)/shard_map/ppermute | solution.py:30
  42.3 4.1 %collective-permute-start.5 = (f32[128,768]{1,0:T(8,128)S(1)}, f32[128,768]{1,0:T(8,128)S(1)}, u32[]{:S(2)}, u32[]{:S(2)}) collective-permute-start(f32[128,768]{1,0:T(8,128)S(1)} %pad_maximum_fusion.5), channel_id=1, source_target_pairs={{0,4},{4,0},{8,12},{12,8},{16,20},{20,16},{24,28},{28,24},{1,5},{5... | collective-permute-start | bytes 1179656 | tf_op jit(solution)/shard_map/ppermute | solution.py:30
  46.6 8.7 %collective-permute-done.5 = f32[128,768]{1,0:T(8,128)S(1)} collective-permute-done((f32[128,768]{1,0:T(8,128)S(1)}, f32[128,768]{1,0:T(8,128)S(1)}, u32[]{:S(2)}, u32[]{:S(2)}) %collective-permute-start.5) | collective-permute-done | bytes 393248 | tf_op jit(solution)/shard_map/ppermute | solution.py:30
  55.3 0.8 fusion.19
  56.1 0.3 fusion.22
  56.5 0.0 copy-start.4
  56.5 0.1 broadcast_in_dim.30
  56.5 16.9 %all_to_all.36 = f32[32,12,256]{2,1,0:T(8,128)S(1)} all-to-all(f32[32,12,256]{2,1,0:T(8,128)S(1)} %bitcast.55), channel_id=1, replica_groups=mesh['x'=4,'zh'=2,'core'=2,'z'=8,'y'=4] {'x','core','y'}, dimensions={0} | all-to-all | bytes 786432 | tf_op jit(solution)/shard_map/all_to_all | solution.py:49
  73.4 0.1 reduce_sum.46
  73.5 0.7 broadcast_in_dim.31
  74.2 15.9 %all-to-all-start.2 = ((f32[16,12,256]{2,1,0:T(8,128)}), f32[16,12,256]{2,1,0:T(8,128)S(1)}, u32[]{:S(2)}, u32[]{:S(2)}) async-start(f32[16,12,256]{2,1,0:T(8,128)} %broadcast_in_dim.31), calls=%async_computation.2 | async-start | bytes 524288 | tf_op jit(solution)/shard_map/all_to_all | solution.py:42
  90.1 0.5 fusion.21
  90.6 7.3 %collective-permute-start = (f32[48,768]{1,0:T(8,128)S(1)}, f32[48,768]{1,0:T(8,128)S(1)}, u32[]{:S(2)}, u32[]{:S(2)}) collective-permute-start(f32[48,768]{1,0:T(8,128)S(1)} %reshape.144), channel_id=1, source_target_pairs={{0,16},{4,20},{8,24},{12,28},{16,0},{20,4},{24,8},{28,12},{1,17},{... | collective-permute-start | bytes 442376 | tf_op jit(solution)/shard_map/ppermute | solution.py:30
  97.9 18.4 %collective-permute-done = f32[48,768]{1,0:T(8,128)S(1)} collective-permute-done((f32[48,768]{1,0:T(8,128)S(1)}, f32[48,768]{1,0:T(8,128)S(1)}, u32[]{:S(2)}, u32[]{:S(2)}) %collective-permute-start) | collective-permute-done | bytes 147488 | tf_op jit(solution)/shard_map/ppermute | solution.py:30
  116.4 1.9 collective-permute-start.1
  118.4 0.1 copy.48
  118.4 0.8 broadcast_in_dim.32
  119.2 3.5 %all-to-all-start.3 = ((f32[4,8,12,256]{3,1,2,0:T(8,128)}), f32[4,8,12,256]{3,1,2,0:T(8,128)S(1)}, u32[]{:S(2)}, u32[]{:S(2)}) async-start(f32[4,8,12,256]{3,1,2,0:T(8,128)} %broadcast_in_dim.32), calls=%async_computation.3 | async-start | bytes 786432 | tf_op jit(solution)/shard_map/all_to_all | solution.py:42
  122.7 7.7 %collective-permute-done.1 = f32[96,768]{1,0:T(8,128)S(1)} collective-permute-done((f32[96,768]{1,0:T(8,128)S(1)}, f32[96,768]{1,0:T(8,128)S(1)}, u32[]{:S(2)}, u32[]{:S(2)}) %collective-permute-start.1) | collective-permute-done | bytes 294944 | tf_op jit(solution)/shard_map/ppermute | solution.py:30
  130.4 0.9 pad_maximum_fusion.1
  131.3 6.6 %collective-permute-start.2 = (f32[192,768]{1,0:T(8,128)}, f32[192,768]{1,0:T(8,128)}, u32[]{:S(2)}, u32[]{:S(2)}) collective-permute-start(f32[192,768]{1,0:T(8,128)} %pad_maximum_fusion.1), channel_id=1, source_target_pairs={{0,4},{4,0},{8,12},{12,8},{16,20},{20,16},{24,28},{28,24},{1,5},{5... | collective-permute-start | bytes 1769480 | tf_op jit(solution)/shard_map/ppermute | solution.py:30
  137.9 0.1 copy.40
  138.1 0.4 fusion.20
  138.5 0.4 fusion.60
  138.9 0.8 fusion.18
  139.8 11.9 %collective-permute-done.2 = f32[192,768]{1,0:T(8,128)} collective-permute-done((f32[192,768]{1,0:T(8,128)}, f32[192,768]{1,0:T(8,128)}, u32[]{:S(2)}, u32[]{:S(2)}) %collective-permute-start.2) | collective-permute-done | bytes 589856 | tf_op jit(solution)/shard_map/ppermute | solution.py:30
  151.7 2.0 convolution_subtract_fusion
  153.7 3.4 %collective-permute-start.6 = (f32[256,768]{1,0:T(8,128)S(1)}, f32[256,768]{1,0:T(8,128)}, u32[]{:S(2)}, u32[]{:S(2)}) collective-permute-start(f32[256,768]{1,0:T(8,128)S(1)} %convolution_subtract_fusion), channel_id=1, source_target_pairs={{0,1},{1,2},{2,3},{3,0},{4,5},{5,6},{6,7},{7,4},{8,9},{9,10},{10,1... | collective-permute-start | bytes 2359304 | tf_op jit(solution)/shard_map/ppermute | solution.py:110
  157.1 3.7 %collective-permute-start.7 = (f32[256,768]{1,0:T(8,128)S(1)}, f32[256,768]{1,0:T(8,128)}, u32[]{:S(2)}, u32[]{:S(2)}) collective-permute-start(f32[256,768]{1,0:T(8,128)S(1)} %convolution_subtract_fusion), channel_id=1, source_target_pairs={{0,3},{1,0},{2,1},{3,2},{4,7},{5,4},{6,5},{7,6},{8,11},{9,8},{10,9... | collective-permute-start | bytes 2359304 | tf_op jit(solution)/shard_map/ppermute | solution.py:111
  160.7 0.8 fusion.16
  161.6 0.0 copy-start.1
  161.6 18.7 %all_to_all.37 = f32[32,8,256]{2,1,0:T(8,128)S(1)} all-to-all(f32[32,8,256]{2,1,0:T(8,128)S(1)} %bitcast.59), channel_id=1, replica_groups=mesh['x'=4,'zh'=2,'core'=2,'z'=8,'y'=4] {'x','core','y'}, dimensions={0} | all-to-all | bytes 524288 | tf_op jit(solution)/shard_map/all_to_all | solution.py:49
  180.3 0.7 broadcast_in_dim.36
  181.0 7.3 %all-to-all-start.5 = ((f32[16,8,256]{2,1,0:T(8,128)}), f32[16,8,256]{2,1,0:T(8,128)S(1)}, u32[]{:S(2)}, u32[]{:S(2)}) async-start(f32[16,8,256]{2,1,0:T(8,128)} %broadcast_in_dim.36), calls=%async_computation.5 | async-start | bytes 262144 | tf_op jit(solution)/shard_map/all_to_all | solution.py:42
  188.3 0.1 broadcast_in_dim.28
  188.4 1.4 fusion.3
  189.8 12.4 %all-to-all-done.5 = f32[16,8,256]{2,1,0:T(8,128)S(1)} async-done(((f32[16,8,256]{2,1,0:T(8,128)}), f32[16,8,256]{2,1,0:T(8,128)S(1)}, u32[]{:S(2)}, u32[]{:S(2)}) %all-to-all-start.5) | async-done | bytes 131104 | tf_op jit(solution)/shard_map/all_to_all | solution.py:42
  202.2 0.7 broadcast_in_dim.37
  202.9 4.6 %all-to-all-start.6 = ((f32[4,8,8,256]{3,2,1,0:T(8,128)}), f32[4,8,8,256]{3,2,1,0:T(8,128)S(1)}, u32[]{:S(2)}, u32[]{:S(2)}) async-start(f32[4,8,8,256]{3,2,1,0:T(8,128)} %broadcast_in_dim.37), calls=%async_computation.6 | async-start | bytes 524288 | tf_op jit(solution)/shard_map/all_to_all | solution.py:42
  207.6 1.0 slice.26
  208.6 3.9 %collective-permute-start.8 = (f32[128,768]{1,0:T(8,128)S(1)}, f32[128,768]{1,0:T(8,128)}, u32[]{:S(2)}, u32[]{:S(2)}) collective-permute-start(f32[128,768]{1,0:T(8,128)S(1)} %slice.26), channel_id=1, source_target_pairs={{0,1},{1,2},{2,3},{3,0},{4,5},{5,6},{6,7},{7,4},{8,9},{9,10},{10,1... | collective-permute-start | bytes 1179656 | tf_op jit(solution)/shard_map/ppermute | solution.py:112
  212.5 1.0 slice.27
  213.6 3.3 %collective-permute-start.9 = (f32[128,768]{1,0:T(8,128)S(1)}, f32[128,768]{1,0:T(8,128)}, u32[]{:S(2)}, u32[]{:S(2)}) collective-permute-start(f32[128,768]{1,0:T(8,128)S(1)} %slice.27), channel_id=1, source_target_pairs={{0,3},{1,0},{2,1},{3,2},{4,7},{5,4},{6,5},{7,6},{8,11},{9,8},{10,9... | collective-permute-start | bytes 1179656 | tf_op jit(solution)/shard_map/ppermute | solution.py:113
  216.9 2.5 %fusion.2 = f32[128,3072]{0,1:T(8,128)S(1)} fusion(f32[128,3072]{0,1:T(8,128)S(1)} %fusion.3, s32[]{:T(128)S(6)} %select_n.159, f32[256,768]{1,0:T(8,128)} %collective-permute-done.6, f32[128,256]{1,0:T(8,128)S(1)} %copy-done.1), kind=kOutput, calls=%fused_computation.6 | convolution fusion | flops 301989888 | bytes 1310724 | tf_op jit(solution)/shard_map/dot_general | solution.py:14
  219.4 2.5 %fusion.1 = f32[128,3072]{0,1:T(8,128)S(1)} fusion(f32[128,3072]{0,1:T(8,128)S(1)} %fusion.2, s32[]{:T(128)S(6)} %select_n.161, f32[256,768]{1,0:T(8,128)} %collective-permute-done.7, f32[128,256]{1,0:T(8,128)S(1)} %copy-done.1), kind=kOutput, calls=%fused_computation.4 | convolution fusion | flops 301989888 | bytes 1310724 | tf_op jit(solution)/shard_map/dot_general | solution.py:14
  222.0 0.0 copy-start.5
  222.0 0.5 collective-permute-done.8
  222.5 2.1 collective-permute-done.9
  224.6 2.5 %fusion = f32[128,3072]{0,1:T(8,128)S(1)} fusion(f32[128,3072]{0,1:T(8,128)S(1)} %fusion.1, s32[]{:T(128)S(6)} %select_n.163, f32[128,256]{1,0:T(8,128)S(1)} %copy-done.1, f32[128,768]{1,0:T(8,128)} %collective-permute-done.9, f32[128,768]{1,0:T(8,128)} %collective-permute-done.8), kind=kOutput, calls=%fused_computation.2 | convolution fusion | flops 302186496 | bytes 1310724 | tf_op jit(solution)/shard_map/dot_general | solution.py:14
  227.1 0.4 fusion.12
  227.5 0.4 fusion.11
  227.9 1.6 copy.43
  (31 shorter events, 0.4 us)
Async XLA Ops:
  0.0 1.8 copy-start
  15.7 15.4 %collective-permute-start.3 = (f32[32,768]{1,0:T(8,128)S(1)}, f32[32,768]{1,0:T(8,128)S(1)}, u32[]{:S(2)}, u32[]{:S(2)}) collective-permute-start(f32[32,768]{1,0:T(8,128)S(1)} %slice_bitcast_fusion), channel_id=1, source_target_pairs={{0,16},{4,20},{8,24},{12,28},{16,0},{20,4},{24,8},{28,12},{1,17},{... | collective-permute-start | bytes 294920 | tf_op jit(solution)/shard_map/ppermute | solution.py:30
  31.1 11.2 %collective-permute-start.4 = (f32[64,768]{1,0:T(8,128)S(1)}, f32[64,768]{1,0:T(8,128)S(1)}, u32[]{:S(2)}, u32[]{:S(2)}) collective-permute-start(f32[64,768]{1,0:T(8,128)S(1)} %pad_maximum_fusion.7), channel_id=1, source_target_pairs={{0,8},{4,12},{8,0},{12,4},{16,24},{20,28},{24,16},{28,20},{1,9},{5... | collective-permute-start | bytes 589832 | tf_op jit(solution)/shard_map/ppermute | solution.py:30
  42.3 12.9 %collective-permute-start.5 = (f32[128,768]{1,0:T(8,128)S(1)}, f32[128,768]{1,0:T(8,128)S(1)}, u32[]{:S(2)}, u32[]{:S(2)}) collective-permute-start(f32[128,768]{1,0:T(8,128)S(1)} %pad_maximum_fusion.5), channel_id=1, source_target_pairs={{0,4},{4,0},{8,12},{12,8},{16,20},{20,16},{24,28},{28,24},{1,5},{5... | collective-permute-start | bytes 1179656 | tf_op jit(solution)/shard_map/ppermute | solution.py:30
  55.3 1.3 copy-start.2
  56.5 33.7 %copy-start.4 = (f32[256,256]{1,0:T(8,128)S(1)}, f32[256,256]{1,0:T(8,128)}, u32[]{:S(2)}) copy-start(f32[256,256]{1,0:T(8,128)} %param.11) | copy-start | bytes 786436
  74.2 44.1 %all-to-all-start.2 = ((f32[16,12,256]{2,1,0:T(8,128)}), f32[16,12,256]{2,1,0:T(8,128)S(1)}, u32[]{:S(2)}, u32[]{:S(2)}) async-start(f32[16,12,256]{2,1,0:T(8,128)} %broadcast_in_dim.31), calls=%async_computation.2 | async-start | bytes 524288 | tf_op jit(solution)/shard_map/all_to_all | solution.py:42
  90.6 25.8 %collective-permute-start = (f32[48,768]{1,0:T(8,128)S(1)}, f32[48,768]{1,0:T(8,128)S(1)}, u32[]{:S(2)}, u32[]{:S(2)}) collective-permute-start(f32[48,768]{1,0:T(8,128)S(1)} %reshape.144), channel_id=1, source_target_pairs={{0,16},{4,20},{8,24},{12,28},{16,0},{20,4},{24,8},{28,12},{1,17},{... | collective-permute-start | bytes 442376 | tf_op jit(solution)/shard_map/ppermute | solution.py:30
  116.4 14.0 %collective-permute-start.1 = (f32[96,768]{1,0:T(8,128)S(1)}, f32[96,768]{1,0:T(8,128)S(1)}, u32[]{:S(2)}, u32[]{:S(2)}) collective-permute-start(f32[96,768]{1,0:T(8,128)S(1)} %pad_maximum_fusion.6), channel_id=1, source_target_pairs={{0,8},{4,12},{8,0},{12,4},{16,24},{20,28},{24,16},{28,20},{1,9},{5... | collective-permute-start | bytes 884744 | tf_op jit(solution)/shard_map/ppermute | solution.py:30
  119.2 18.7 %all-to-all-start.3 = ((f32[4,8,12,256]{3,1,2,0:T(8,128)}), f32[4,8,12,256]{3,1,2,0:T(8,128)S(1)}, u32[]{:S(2)}, u32[]{:S(2)}) async-start(f32[4,8,12,256]{3,1,2,0:T(8,128)} %broadcast_in_dim.32), calls=%async_computation.3 | async-start | bytes 786432 | tf_op jit(solution)/shard_map/all_to_all | solution.py:42
  131.3 7.6 %copy-start.3 = (f32[128,768]{1,0:T(8,128)S(1)}, f32[128,768]{1,0:T(8,128)}, u32[]{:S(2)}) copy-start(f32[128,768]{1,0:T(8,128)} %copy-done.2) | copy-start | bytes 1179652
  131.3 20.4 %collective-permute-start.2 = (f32[192,768]{1,0:T(8,128)}, f32[192,768]{1,0:T(8,128)}, u32[]{:S(2)}, u32[]{:S(2)}) collective-permute-start(f32[192,768]{1,0:T(8,128)} %pad_maximum_fusion.1), channel_id=1, source_target_pairs={{0,4},{4,0},{8,12},{12,8},{16,20},{20,16},{24,28},{28,24},{1,5},{5... | collective-permute-start | bytes 1769480 | tf_op jit(solution)/shard_map/ppermute | solution.py:30
  153.7 53.9 %collective-permute-start.6 = (f32[256,768]{1,0:T(8,128)S(1)}, f32[256,768]{1,0:T(8,128)}, u32[]{:S(2)}, u32[]{:S(2)}) collective-permute-start(f32[256,768]{1,0:T(8,128)S(1)} %convolution_subtract_fusion), channel_id=1, source_target_pairs={{0,1},{1,2},{2,3},{3,0},{4,5},{5,6},{6,7},{7,4},{8,9},{9,10},{10,1... | collective-permute-start | bytes 2359304 | tf_op jit(solution)/shard_map/ppermute | solution.py:110
  157.1 55.5 %collective-permute-start.7 = (f32[256,768]{1,0:T(8,128)S(1)}, f32[256,768]{1,0:T(8,128)}, u32[]{:S(2)}, u32[]{:S(2)}) collective-permute-start(f32[256,768]{1,0:T(8,128)S(1)} %convolution_subtract_fusion), channel_id=1, source_target_pairs={{0,3},{1,0},{2,1},{3,2},{4,7},{5,4},{6,5},{7,6},{8,11},{9,8},{10,9... | collective-permute-start | bytes 2359304 | tf_op jit(solution)/shard_map/ppermute | solution.py:111
  161.6 26.8 %copy-start.1 = (f32[128,256]{1,0:T(8,128)S(1)}, f32[128,256]{1,0:T(8,128)}, u32[]{:S(2)}) copy-start(f32[128,256]{1,0:T(8,128)} %param.9) | copy-start | bytes 393220
  181.0 21.2 %all-to-all-start.5 = ((f32[16,8,256]{2,1,0:T(8,128)}), f32[16,8,256]{2,1,0:T(8,128)S(1)}, u32[]{:S(2)}, u32[]{:S(2)}) async-start(f32[16,8,256]{2,1,0:T(8,128)} %broadcast_in_dim.36), calls=%async_computation.5 | async-start | bytes 262144 | tf_op jit(solution)/shard_map/all_to_all | solution.py:42
  202.9 19.0 %all-to-all-start.6 = ((f32[4,8,8,256]{3,2,1,0:T(8,128)}), f32[4,8,8,256]{3,2,1,0:T(8,128)S(1)}, u32[]{:S(2)}, u32[]{:S(2)}) async-start(f32[4,8,8,256]{3,2,1,0:T(8,128)} %broadcast_in_dim.37), calls=%async_computation.6 | async-start | bytes 524288 | tf_op jit(solution)/shard_map/all_to_all | solution.py:42
  208.6 13.9 %collective-permute-start.8 = (f32[128,768]{1,0:T(8,128)S(1)}, f32[128,768]{1,0:T(8,128)}, u32[]{:S(2)}, u32[]{:S(2)}) collective-permute-start(f32[128,768]{1,0:T(8,128)S(1)} %slice.26), channel_id=1, source_target_pairs={{0,1},{1,2},{2,3},{3,0},{4,5},{5,6},{6,7},{7,4},{8,9},{9,10},{10,1... | collective-permute-start | bytes 1179656 | tf_op jit(solution)/shard_map/ppermute | solution.py:112
  213.6 11.0 %collective-permute-start.9 = (f32[128,768]{1,0:T(8,128)S(1)}, f32[128,768]{1,0:T(8,128)}, u32[]{:S(2)}, u32[]{:S(2)}) collective-permute-start(f32[128,768]{1,0:T(8,128)S(1)} %slice.27), channel_id=1, source_target_pairs={{0,3},{1,0},{2,1},{3,2},{4,7},{5,4},{6,5},{7,6},{8,11},{9,8},{10,9... | collective-permute-start | bytes 1179656 | tf_op jit(solution)/shard_map/ppermute | solution.py:113
  222.0 5.5 %copy-start.5 = (f32[256,256]{1,0:T(8,128)S(1)}, f32[256,256]{1,0:T(8,128)}, u32[]{:S(2)}) copy-start(f32[256,256]{1,0:T(8,128)} %param.13) | copy-start | bytes 786436

commit v3 on v1

--- a/solution.py
+++ b/solution.py
@@ -1,6 +1,8 @@
 import jax
 import jax.numpy as jnp
 from jax import lax
+from jax.experimental import pallas as pl
+from jax.experimental.pallas import tpu as pltpu
 from jax.sharding import Mesh
 from jax.sharding import PartitionSpec as P
 
@@ -43,7 +45,7 @@
 
 
 def summed_rows(partial):
-    parts = partial.reshape(lax.axis_size("y"), -1, partial.shape[1])
+    parts = partial.reshape(lax.axis_size("y"), -1, partial.shape[-1])
     group = lax.axis_size("x") * lax.axis_size("core")
     parts = jnp.broadcast_to(parts[None], (group, *parts.shape)).reshape(-1, *parts.shape[1:])
     parts = lax.all_to_all(parts, ("x", "core", "y"), 0, 0)
@@ -52,6 +54,10 @@
     halves = halves.reshape(lax.axis_size("zh"), -1, *own.shape)
     column = jnp.sum(halves, axis=0)
     return spread(column, "y")
+
+
+def named_permute(array, pairs):
+    return lax.ppermute(array, "y", pairs)
 
 
 def per_device(
@@ -82,44 +88,99 @@
     packed = jnp.concatenate([reflectors, cholesky_panel, buffer], axis=0)
     packed = packed.reshape(packed.shape[0], y_width, cols).transpose(1, 0, 2)
     packed = lax.all_to_all(packed, "y", 0, 0)
-    own_reflectors = packed[:, :share].reshape(-1, cols)
-    own_cholesky = packed[:, share : 2 * share].reshape(-1, cols)
-    own_slots = packed[:, 2 * share :].reshape(-1, cols)
     first = row_index * row_count + y_index * cols
     below = first + jnp.arange(cols, dtype=jnp.int32) >= panel
-    own_cholesky = jnp.where(below[None, :], own_cholesky, 0.0)
+    kept = below[None, None, :] | (jnp.arange(2 * share) < share)[None, :, None]
+    own_pairs = jnp.where(kept, packed[:, : 2 * share], 0.0)
+    own_reflectors = packed[:, :share].reshape(-1, cols)
+    own_cholesky = own_pairs[:, share:].reshape(-1, cols)
+    own_slots = packed[:, 2 * share :].reshape(-1, cols)
 
     all_reflectors = doubled(own_reflectors, "z", HOPS)
     all_slots = doubled(own_slots, "z", HOPS)
 
-    group = share * y_width
-    turned = onehot(place_of(order // group, z_index, HOPS) * group + order % group, panel)
-    inner = product(product(own_slots, all_reflectors, (1, 1)), turned, (1, 1))
-    inner = summed_rows(inner).reshape(-1, panel)
-    summed_at = ((owner % y_width) * z_width + owner // y_width) * slots + earlier
-    inner = product(onehot(summed_at, slots * vec_width), inner)
-    coeff = product(inner, product(wy_factor, turned, (0, 0)))
-
     z_place = place_of(owner // y_width, z_index, HOPS)
     held_at = (z_place * y_width + owner % y_width) * slots + earlier
     gathered = product(onehot(held_at, slots * vec_width), all_slots)
-    transformed = gathered - product(coeff, all_reflectors)
+    group = share * y_width
+    turned = onehot(place_of(order // group, z_index, HOPS) * group + order % group, panel)
 
-    blocks = [transformed]
-    for d in range(1, y_width):
-        turn = [(i, (i + d) % y_width) for i in range(y_width)]
-        blocks.append(lax.ppermute(transformed, "y", turn))
-    cross = summed_rows(product(own_cholesky, transformed, (1, 1)))
-    cross = cross.transpose(1, 0, 2, 3).reshape(-1, panel)
-    correction = product(secular, cross, (1, 1))
+    with_gathered = product(own_pairs.reshape(-1, cols), gathered, (1, 1))
+    with_reflectors = product(product(own_cholesky, all_reflectors, (1, 1)), turned, (1, 1))
+    partial = jnp.concatenate(
+        [
+            with_gathered.reshape(y_width, 2 * share, panel),
+            with_reflectors.reshape(y_width, share, panel),
+        ],
+        axis=1,
+    )
+    sums = summed_rows(partial)
+    inner, direct, cross = (
+        sums[:, :, k * share : (k + 1) * share].reshape(panel, panel) for k in range(3)
+    )
+    spot = (order // group) * share + (order % group) // share * (z_width * share) + order % share
+    by_spot = onehot(spot, panel)
+    wy_spots = product(wy_factor, by_spot)
+    inverse_spots = product(panel_inverse, by_spot)
 
-    applied = jnp.zeros((secular.shape[0], row_count), jnp.float32)
-    for d, block in enumerate(blocks):
-        at = ((y_index - d + y_width) % y_width) * cols
-        applied = lax.dynamic_update_slice(applied, product(secular, block), (0, at))
-    head = applied[:, :panel]
-    solved = product(head - correction, panel_inverse, (1, 1))
-    return lax.dynamic_update_slice(applied, jnp.where(row_index == 0, solved, head), (0, 0))
+    def turns(array):
+        return [array] + [
+            named_permute(array, [(i, (i + d) % y_width) for i in range(y_width)])
+            for d in range(1, y_width)
+        ]
+
+    reflector_blocks = turns(all_reflectors)
+    gathered_blocks = turns(gathered)
+    merged = []
+    for block in gathered_blocks:
+        merged.append(product(secular, block))
+    merged, stacked = lax.optimization_barrier((jnp.stack(merged), jnp.stack(reflector_blocks)))
+
+    projected = product(secular, inner, (1, 1))
+    coeff = product(projected, wy_spots, (1, 1))
+    coeff_held = product(coeff, turned)
+    correction = product(secular, direct, (1, 1)) - product(coeff, cross, (1, 1))
+    taken_off = product(correction, inverse_spots, (1, 1))
+    where = jnp.stack([y_index, row_index]).astype(jnp.int32)
+    return finished(where, merged, coeff_held, stacked, taken_off, panel_inverse)
+
+
+def finished(where, merged, coeff, reflectors, taken_off, panel_inverse):
+    count, vectors, cols = merged.shape
+    panel = coeff.shape[1]
+
+    def kernel(where_ref, merged_ref, coeff_ref, reflectors_ref, off_ref, inverse_ref, out_ref):
+        out_ref[...] = merged_ref[0] - product(coeff_ref[...], reflectors_ref[0])
+
+        @pl.when((pl.program_id(0) == 0) & (where_ref[1] == 0))
+        def _():
+            head = out_ref[:, :panel]
+            out_ref[:, :panel] = product(head, inverse_ref[...], (1, 1)) - off_ref[...]
+
+    def turned(q, where_ref):
+        return (lax.rem(where_ref[0] - q + count, count), 0, 0)
+
+    def whole(q, where_ref):
+        return (0, 0)
+
+    grid = pltpu.PrefetchScalarGridSpec(
+        num_scalar_prefetch=1,
+        grid=(count,),
+        in_specs=[
+            pl.BlockSpec((1, vectors, cols), turned),
+            pl.BlockSpec(coeff.shape, whole),
+            pl.BlockSpec((1, panel, cols), turned),
+            pl.BlockSpec(taken_off.shape, whole),
+            pl.BlockSpec(panel_inverse.shape, whole),
+        ],
+        out_specs=pl.BlockSpec((vectors, cols), lambda q, where_ref: (0, q)),
+    )
+    return pl.pallas_call(
+        kernel,
+        grid_spec=grid,
+        out_shape=jax.ShapeDtypeStruct((vectors, count * cols), jnp.float32),
+        name="finished",
+    )(where, merged, coeff, reflectors, taken_off, panel_inverse)
 
 
 def solution(mesh):

time: 234 us -> 218 us (0.932)
  starting transfers between devices: 82.8 us -> 72.3 us
  blocking collectives: 29.3 us -> 19.3 us
  Pallas kernels: 0 us -> 5.91 us
  other arithmetic: 3.7 us -> 6.87 us
  local copies, waits for them, and re-layouts: 5.98 us -> 2.89 us
  matrix products: 16.4 us -> 13.4 us
    ppermute x3 -> x6, waiting for transfers between devices: 0.01 us -> 37.3 us  [named_permute(): return lax.ppermute(array, 'y', pairs)]
    all_to_all x1, waiting for transfers between devices: 26.8 us -> 6.22 us  [per_device(): packed = lax.all_to_all(packed, 'y', 0, 0)]
    ppermute x6, waiting for transfers between devices: 56.9 us -> 40 us  [doubled(): other = lax.ppermute(block, axis, [(i, i ^ hop) for i in range(width)])]
    all_to_all x1 -> x0, blocking collectives: 11 us -> none  [per_device(): packed = lax.all_to_all(packed, 'y', 0, 0)]
    all_to_all x4 -> x2, starting transfers between devices: 28.5 us -> 17.9 us  [spread(): return lax.all_to_all(copies, axis, 0, 0)]
    ppermute x3 -> x6, starting transfers between devices: 9.78 us -> 17.2 us  [named_permute(): return lax.ppermute(array, 'y', pairs)]
    ppermute x6, starting transfers between devices: 38.5 us -> 32.2 us  [doubled(): other = lax.ppermute(block, axis, [(i, i ^ hop) for i in range(width)])]
    pallas_call x0 -> x1, Pallas kernels: none -> 5.91 us  [finished(): pl.pallas_call(kernel, grid_spec=grid, out_shape=jax.ShapeDtypeStruct((ve...]
  transfers between devices with their start and end apart: 14 -> 15, of which waited for: 8 -> 12; matrix products, arithmetic and copies ran while one was open for 7% -> 6% of each run, Pallas kernels for 0% -> 0%
where the time goes in v3:
time: 218 us; the launch traced here: 214 us
  waiting for transfers between devices  93.2 us (43%)
  starting transfers between devices  72.3 us (33%)
  blocking collectives  19.3 us (9%)
  matrix products  13.4 us (6%)
  other arithmetic  6.87 us (3%)
  Pallas kernels  5.91 us (3%)
  local copies, waits for them, and re-layouts  2.89 us (1%)
    ppermute x6, waiting for transfers between devices, doubled(): other = lax.ppermute(block, axis, [(i, i ^ hop) for i in range(width)])  40 us
    ppermute x6, waiting for transfers between devices, named_permute(): return lax.ppermute(array, 'y', pairs)  37.3 us
    ppermute x6, starting transfers between devices, doubled(): other = lax.ppermute(block, axis, [(i, i ^ hop) for i in range(width)])  32.2 us
    all_to_all x1, blocking collectives, summed_rows(): parts = lax.all_to_all(parts, ('x', 'core', 'y'), 0, 0)  19.3 us
    all_to_all x2, starting transfers between devices, spread(): return lax.all_to_all(copies, axis, 0, 0)  17.9 us
    ppermute x6, starting transfers between devices, named_permute(): return lax.ppermute(array, 'y', pairs)  17.2 us
    dot_general x18, matrix products, product(): lax.dot_general(left, right, (((contract[0],), (contract[1],)), ((), ()))...  13.4 us
    all_to_all x2, waiting for transfers between devices, spread(): return lax.all_to_all(copies, axis, 0, 0)  9.65 us
  transfers between devices with their start and end apart: 15, of which 12 were waited for; matrix products, arithmetic and copies ran while one was open for 6% of the time, Pallas kernels for 0%

profile of v3, /device:TPU:1, one launch (start us, length us, event | category | flops | bytes accessed | tf_op | source)
XLA Modules:
  0.0 214.3 jit_solution(17613400097534380934)
XLA Ops:
  0.0 0.7 and_select_fusion.9
  0.7 0.7 broadcast_compare_fusion
  1.4 0.2 convert_reduce_fusion
  1.6 0.2 fusion.22
  1.8 0.3 fusion.50
  2.2 1.0 pad_maximum_fusion.4
  3.1 0.2 reshape.199
  3.3 0.8 copy.30
  4.1 5.0 %all-to-all-start = ((f32[4,28,768]{2,1,0:T(8,128)}), f32[4,28,768]{2,1,0:T(8,128)S(1)}, u32[]{:S(2)}, u32[]{:S(2)}) async-start(f32[4,28,768]{2,1,0:T(8,128)} %bitcast.67), calls=%async_computation | async-start | bytes 786432 | tf_op jit(solution)/shard_map/all_to_all | solution.py:90
  9.1 6.2 %all-to-all-done = f32[4,28,768]{2,1,0:T(8,128)S(1)} async-done(((f32[4,28,768]{2,1,0:T(8,128)}), f32[4,28,768]{2,1,0:T(8,128)S(1)}, u32[]{:S(2)}, u32[]{:S(2)}) %all-to-all-start) | async-done | bytes 344096 | tf_op jit(solution)/shard_map/all_to_all | solution.py:90
  15.4 9.5 %collective-permute-start.6 = (f32[32,768]{1,0:T(8,128)S(1)}, f32[32,768]{1,0:T(8,128)S(1)}, u32[]{:S(2)}, u32[]{:S(2)}) collective-permute-start(f32[32,768]{1,0:T(8,128)S(1)} %slice_bitcast_fusion.2), channel_id=1, source_target_pairs={{0,16},{4,20},{8,24},{12,28},{16,0},{20,4},{24,8},{28,12},{1,17},{... | collective-permute-start | bytes 294920 | tf_op jit(solution)/shard_map/ppermute | solution.py:32
  24.9 1.9 collective-permute-start
  26.9 0.1 broadcast_or_fusion
  27.0 15.0 %collective-permute-start.7 = (f32[64,768]{1,0:T(8,128)S(1)}, f32[64,768]{1,0:T(8,128)S(1)}, u32[]{:S(2)}, u32[]{:S(2)}) collective-permute-start(f32[64,768]{1,0:T(8,128)S(1)} %pad_maximum_fusion.7), channel_id=1, source_target_pairs={{0,8},{4,12},{8,0},{12,4},{16,24},{20,28},{24,16},{28,20},{1,9},{5... | collective-permute-start | bytes 589832 | tf_op jit(solution)/shard_map/ppermute | solution.py:32
  42.0 4.9 %collective-permute-done = f32[48,768]{1,0:T(8,128)S(1)} collective-permute-done((f32[48,768]{1,0:T(8,128)S(1)}, f32[48,768]{1,0:T(8,128)S(1)}, u32[]{:S(2)}, u32[]{:S(2)}) %collective-permute-start) | collective-permute-done | bytes 147488 | tf_op jit(solution)/shard_map/ppermute | solution.py:32
  46.8 1.9 collective-permute-start.1
  48.8 12.1 %collective-permute-done.7 = f32[64,768]{1,0:T(8,128)S(1)} collective-permute-done((f32[64,768]{1,0:T(8,128)S(1)}, f32[64,768]{1,0:T(8,128)S(1)}, u32[]{:S(2)}, u32[]{:S(2)}) %collective-permute-start.7) | collective-permute-done | bytes 196640 | tf_op jit(solution)/shard_map/ppermute | solution.py:32
  60.9 1.9 collective-permute-start.8
  62.8 4.4 %collective-permute-done.1 = f32[96,768]{1,0:T(8,128)S(1)} collective-permute-done((f32[96,768]{1,0:T(8,128)S(1)}, f32[96,768]{1,0:T(8,128)S(1)}, u32[]{:S(2)}, u32[]{:S(2)}) %collective-permute-start.1) | collective-permute-done | bytes 294944 | tf_op jit(solution)/shard_map/ppermute | solution.py:32
  67.3 1.9 collective-permute-start.2
  69.2 7.2 %collective-permute-done.8 = f32[128,768]{1,0:T(8,128)S(1)} collective-permute-done((f32[128,768]{1,0:T(8,128)S(1)}, f32[128,768]{1,0:T(8,128)S(1)}, u32[]{:S(2)}, u32[]{:S(2)}) %collective-permute-start.8) | collective-permute-done | bytes 393248 | tf_op jit(solution)/shard_map/ppermute | solution.py:32
  76.5 0.8 fusion.23
  77.3 0.3 convolution_bitcast_fusion.5
  77.6 11.5 %collective-permute-done.2 = f32[192,768]{1,0:T(8,128)S(1)} collective-permute-done((f32[192,768]{1,0:T(8,128)S(1)}, f32[192,768]{1,0:T(8,128)S(1)}, u32[]{:S(2)}, u32[]{:S(2)}) %collective-permute-start.2) | collective-permute-done | bytes 589856 | tf_op jit(solution)/shard_map/ppermute | solution.py:32
  89.1 0.9 fusion
  90.0 0.8 fusion.8
  90.9 0.1 broadcast_in_dim.20
  91.0 19.3 %all_to_all.20 = f32[32,24,256]{2,1,0:T(8,128)S(1)} all-to-all(f32[32,24,256]{2,1,0:T(8,128)S(1)} %bitcast.68), channel_id=1, replica_groups=mesh['x'=4,'zh'=2,'core'=2,'z'=8,'y'=4] {'x','core','y'}, dimensions={0} | all-to-all | bytes 1572864 | tf_op jit(solution)/shard_map/all_to_all | solution.py:51
  110.2 0.1 reduce_sum.28
  110.3 0.8 broadcast_in_dim.21
  111.1 13.2 %all-to-all-start.2 = ((f32[16,24,256]{2,1,0:T(8,128)}), f32[16,24,256]{2,1,0:T(8,128)S(1)}, u32[]{:S(2)}, u32[]{:S(2)}) async-start(f32[16,24,256]{2,1,0:T(8,128)} %broadcast_in_dim.21), calls=%async_computation.2 | async-start | bytes 786432 | tf_op jit(solution)/shard_map/all_to_all | solution.py:44
  124.3 0.0 copy-start.2
  124.3 0.1 fusion.48
  124.4 2.4 %collective-permute-start.9 = (f32[256,768]{1,0:T(8,128)S(1)}, f32[256,768]{1,0:T(8,128)S(1)}, u32[]{:S(2)}, u32[]{:S(2)}) collective-permute-start(f32[256,768]{1,0:T(8,128)S(1)} %get-tuple-element.15), channel_id=1, source_target_pairs={{0,1},{1,2},{2,3},{3,0},{4,5},{5,6},{6,7},{7,4},{8,9},{9,10},{10,1... | collective-permute-start | bytes 2359304 | tf_op jit(solution)/shard_map/ppermute | solution.py:60
  126.8 3.9 %collective-permute-start.10 = (f32[256,768]{1,0:T(8,128)S(1)}, f32[256,768]{1,0:T(8,128)S(1)}, u32[]{:S(2)}, u32[]{:S(2)}) collective-permute-start(f32[256,768]{1,0:T(8,128)S(1)} %get-tuple-element.15), channel_id=1, source_target_pairs={{0,2},{1,3},{2,0},{3,1},{4,6},{5,7},{6,4},{7,5},{8,10},{9,11},{10,... | collective-permute-start | bytes 2359304 | tf_op jit(solution)/shard_map/ppermute | solution.py:60
  130.7 2.8 %collective-permute-start.11 = (f32[256,768]{1,0:T(8,128)S(1)}, f32[256,768]{1,0:T(8,128)S(1)}, u32[]{:S(2)}, u32[]{:S(2)}) collective-permute-start(f32[256,768]{1,0:T(8,128)S(1)} %get-tuple-element.15), channel_id=1, source_target_pairs={{0,3},{1,0},{2,1},{3,2},{4,7},{5,4},{6,5},{7,6},{8,11},{9,8},{10,9... | collective-permute-start | bytes 2359304 | tf_op jit(solution)/shard_map/ppermute | solution.py:60
  133.5 2.3 %collective-permute-start.5 = (f32[256,768]{1,0:T(8,128)S(1)}, f32[256,768]{1,0:T(8,128)}, u32[]{:S(2)}, u32[]{:S(2)}) collective-permute-start(f32[256,768]{1,0:T(8,128)S(1)} %fusion), channel_id=1, source_target_pairs={{0,3},{1,0},{2,1},{3,2},{4,7},{5,4},{6,5},{7,6},{8,11},{9,8},{10,9... | collective-permute-start | bytes 2359304 | tf_op jit(solution)/shard_map/ppermute | solution.py:60
  135.9 0.4 fusion.16
  136.3 3.9 %collective-permute-start.4 = (f32[256,768]{1,0:T(8,128)S(1)}, f32[256,768]{1,0:T(8,128)}, u32[]{:S(2)}, u32[]{:S(2)}) collective-permute-start(f32[256,768]{1,0:T(8,128)S(1)} %fusion), channel_id=1, source_target_pairs={{0,2},{1,3},{2,0},{3,1},{4,6},{5,7},{6,4},{7,5},{8,10},{9,11},{10,... | collective-permute-start | bytes 2359304 | tf_op jit(solution)/shard_map/ppermute | solution.py:60
  140.1 5.1 %collective-permute-done.9 = f32[256,768]{1,0:T(8,128)S(1)} collective-permute-done((f32[256,768]{1,0:T(8,128)S(1)}, f32[256,768]{1,0:T(8,128)S(1)}, u32[]{:S(2)}, u32[]{:S(2)}) %collective-permute-start.9) | collective-permute-done | bytes 786464 | tf_op jit(solution)/shard_map/ppermute | solution.py:60
  145.2 2.0 collective-permute-start.3
  147.2 0.4 fusion.14
  147.6 0.6 pad_add_fusion.where_ref
  148.2 0.6 convolution_bitcast_fusion.3
  148.8 13.6 %collective-permute-done.10 = f32[256,768]{1,0:T(8,128)S(1)} collective-permute-done((f32[256,768]{1,0:T(8,128)S(1)}, f32[256,768]{1,0:T(8,128)S(1)}, u32[]{:S(2)}, u32[]{:S(2)}) %collective-permute-start.10) | collective-permute-done | bytes 786464 | tf_op jit(solution)/shard_map/ppermute | solution.py:60
  162.3 3.0 %collective-permute-done.11 = f32[256,768]{1,0:T(8,128)S(1)} collective-permute-done((f32[256,768]{1,0:T(8,128)S(1)}, f32[256,768]{1,0:T(8,128)S(1)}, u32[]{:S(2)}, u32[]{:S(2)}) %collective-permute-start.11) | collective-permute-done | bytes 786464 | tf_op jit(solution)/shard_map/ppermute | solution.py:60
  165.3 1.9 pad_maximum_fusion.reflectors_ref
  167.3 0.9 broadcast_in_dim.22
  168.2 4.7 %all-to-all-start.3 = ((f32[4,8,24,256]{3,2,1,0:T(8,128)}), f32[4,8,24,256]{3,2,1,0:T(8,128)S(1)}, u32[]{:S(2)}, u32[]{:S(2)}) async-start(f32[4,8,24,256]{3,2,1,0:T(8,128)} %broadcast_in_dim.22), calls=%async_computation.3 | async-start | bytes 1572864 | tf_op jit(solution)/shard_map/all_to_all | solution.py:44
  172.9 10.8 %collective-permute-done.5 = f32[256,768]{1,0:T(8,128)} collective-permute-done((f32[256,768]{1,0:T(8,128)S(1)}, f32[256,768]{1,0:T(8,128)}, u32[]{:S(2)}, u32[]{:S(2)}) %collective-permute-start.5) | collective-permute-done | bytes 786464 | tf_op jit(solution)/shard_map/ppermute | solution.py:60
  183.7 1.7 convolution_bitcast_fusion
  185.4 1.7 convolution_bitcast_fusion.1
  187.1 4.9 %collective-permute-done.3 = f32[256,768]{1,0:T(8,128)} collective-permute-done((f32[256,768]{1,0:T(8,128)S(1)}, f32[256,768]{1,0:T(8,128)}, u32[]{:S(2)}, u32[]{:S(2)}) %collective-permute-start.3) | collective-permute-done | bytes 786464 | tf_op jit(solution)/shard_map/ppermute | solution.py:60
  192.1 1.7 convolution_bitcast_fusion.2
  193.8 1.3 pad_maximum_fusion.1.merged_ref
  195.1 9.6 %all-to-all-done.3 = f32[4,8,24,256]{3,2,1,0:T(8,128)S(1)} async-done(((f32[4,8,24,256]{3,2,1,0:T(8,128)}), f32[4,8,24,256]{3,2,1,0:T(8,128)S(1)}, u32[]{:S(2)}, u32[]{:S(2)}) %all-to-all-start.3) | async-done | bytes 786464 | tf_op jit(solution)/shard_map/all_to_all | solution.py:44
  204.7 0.1 fusion.49
  204.8 0.4 fusion.51
  205.2 0.4 convolution_bitcast_fusion.4
  205.6 0.4 fusion.52
  206.0 1.0 fusion.10.coeff_ref
  206.9 0.4 convolution_subtract_fusion
  207.3 1.0 fusion.53.off_ref
  208.4 5.9 %finished.1 = f32[128,3072]{1,0:T(8,128)} custom-call(s32[2]{0:T(128)} %pad_add_fusion.where_ref, f32[4,128,768]{2,1,0:T(8,128)} %pad_maximum_fusion.1.merged_ref, f32[128,256]{1,0:T(8,128)} %fusion.10.coeff_ref, f32[4,256,768]{2,1,0:T(8,128)} %pad_maximum_fusion.reflectors_ref, f32[128,256]{1,0:T(8,128)} %fusion.53.off_ref, f32[256,256]{1,0:T(8,128)} %inverse_ref.1), custom_call_target="tpu_custom_call" | custom-call | tf_op jit(solution)/shard_map/finished/pallas_call | solution.py:178
  (25 shorter events, 0.3 us)
Async XLA Ops:
  0.0 1.8 copy-start
  4.1 11.2 %all-to-all-start = ((f32[4,28,768]{2,1,0:T(8,128)}), f32[4,28,768]{2,1,0:T(8,128)S(1)}, u32[]{:S(2)}, u32[]{:S(2)}) async-start(f32[4,28,768]{2,1,0:T(8,128)} %bitcast.67), calls=%async_computation | async-start | bytes 786432 | tf_op jit(solution)/shard_map/all_to_all | solution.py:90
  15.4 11.6 %collective-permute-start.6 = (f32[32,768]{1,0:T(8,128)S(1)}, f32[32,768]{1,0:T(8,128)S(1)}, u32[]{:S(2)}, u32[]{:S(2)}) collective-permute-start(f32[32,768]{1,0:T(8,128)S(1)} %slice_bitcast_fusion.2), channel_id=1, source_target_pairs={{0,16},{4,20},{8,24},{12,28},{16,0},{20,4},{24,8},{28,12},{1,17},{... | collective-permute-start | bytes 294920 | tf_op jit(solution)/shard_map/ppermute | solution.py:32
  24.9 21.9 %collective-permute-start = (f32[48,768]{1,0:T(8,128)S(1)}, f32[48,768]{1,0:T(8,128)S(1)}, u32[]{:S(2)}, u32[]{:S(2)}) collective-permute-start(f32[48,768]{1,0:T(8,128)S(1)} %reshape.200), channel_id=1, source_target_pairs={{0,16},{4,20},{8,24},{12,28},{16,0},{20,4},{24,8},{28,12},{1,17},{... | collective-permute-start | bytes 442376 | tf_op jit(solution)/shard_map/ppermute | solution.py:32
  27.0 33.9 %collective-permute-start.7 = (f32[64,768]{1,0:T(8,128)S(1)}, f32[64,768]{1,0:T(8,128)S(1)}, u32[]{:S(2)}, u32[]{:S(2)}) collective-permute-start(f32[64,768]{1,0:T(8,128)S(1)} %pad_maximum_fusion.7), channel_id=1, source_target_pairs={{0,8},{4,12},{8,0},{12,4},{16,24},{20,28},{24,16},{28,20},{1,9},{5... | collective-permute-start | bytes 589832 | tf_op jit(solution)/shard_map/ppermute | solution.py:32
  46.8 20.4 %collective-permute-start.1 = (f32[96,768]{1,0:T(8,128)S(1)}, f32[96,768]{1,0:T(8,128)S(1)}, u32[]{:S(2)}, u32[]{:S(2)}) collective-permute-start(f32[96,768]{1,0:T(8,128)S(1)} %pad_maximum_fusion.6), channel_id=1, source_target_pairs={{0,8},{4,12},{8,0},{12,4},{16,24},{20,28},{24,16},{28,20},{1,9},{5... | collective-permute-start | bytes 884744 | tf_op jit(solution)/shard_map/ppermute | solution.py:32
  60.9 15.6 %collective-permute-start.8 = (f32[128,768]{1,0:T(8,128)S(1)}, f32[128,768]{1,0:T(8,128)S(1)}, u32[]{:S(2)}, u32[]{:S(2)}) collective-permute-start(f32[128,768]{1,0:T(8,128)S(1)} %pad_maximum_fusion.5), channel_id=1, source_target_pairs={{0,4},{4,0},{8,12},{12,8},{16,20},{20,16},{24,28},{28,24},{1,5},{5... | collective-permute-start | bytes 1179656 | tf_op jit(solution)/shard_map/ppermute | solution.py:32
  67.3 21.8 %collective-permute-start.2 = (f32[192,768]{1,0:T(8,128)S(1)}, f32[192,768]{1,0:T(8,128)S(1)}, u32[]{:S(2)}, u32[]{:S(2)}) collective-permute-start(f32[192,768]{1,0:T(8,128)S(1)} %pad_maximum_fusion.3), channel_id=1, source_target_pairs={{0,4},{4,0},{8,12},{12,8},{16,20},{20,16},{24,28},{28,24},{1,5},{5... | collective-permute-start | bytes 1769480 | tf_op jit(solution)/shard_map/ppermute | solution.py:32
  111.1 24.8 %copy-start.3 = (f32[256,256]{1,0:T(8,128)S(1)}, f32[256,256]{1,0:T(8,128)}, u32[]{:S(2)}) copy-start(f32[256,256]{1,0:T(8,128)} %param.11) | copy-start | bytes 786436
  111.1 56.2 %all-to-all-start.2 = ((f32[16,24,256]{2,1,0:T(8,128)}), f32[16,24,256]{2,1,0:T(8,128)S(1)}, u32[]{:S(2)}, u32[]{:S(2)}) async-start(f32[16,24,256]{2,1,0:T(8,128)} %broadcast_in_dim.21), calls=%async_computation.2 | async-start | bytes 786432 | tf_op jit(solution)/shard_map/all_to_all | solution.py:44
  124.3 22.9 %copy-start.2 = (f32[256,256]{1,0:T(8,128)S(1)}, f32[256,256]{1,0:T(8,128)}, u32[]{:S(2)}) copy-start(f32[256,256]{1,0:T(8,128)} %inverse_ref.1) | copy-start | bytes 786436
  124.3 23.9 %copy-start.1 = (f32[128,256]{1,0:T(8,128)S(1)}, f32[128,256]{1,0:T(8,128)}, u32[]{:S(2)}) copy-start(f32[128,256]{1,0:T(8,128)} %param.9) | copy-start | bytes 393220
  124.4 20.8 %collective-permute-start.9 = (f32[256,768]{1,0:T(8,128)S(1)}, f32[256,768]{1,0:T(8,128)S(1)}, u32[]{:S(2)}, u32[]{:S(2)}) collective-permute-start(f32[256,768]{1,0:T(8,128)S(1)} %get-tuple-element.15), channel_id=1, source_target_pairs={{0,1},{1,2},{2,3},{3,0},{4,5},{5,6},{6,7},{7,4},{8,9},{9,10},{10,1... | collective-permute-start | bytes 2359304 | tf_op jit(solution)/shard_map/ppermute | solution.py:60
  126.8 35.5 %collective-permute-start.10 = (f32[256,768]{1,0:T(8,128)S(1)}, f32[256,768]{1,0:T(8,128)S(1)}, u32[]{:S(2)}, u32[]{:S(2)}) collective-permute-start(f32[256,768]{1,0:T(8,128)S(1)} %get-tuple-element.15), channel_id=1, source_target_pairs={{0,2},{1,3},{2,0},{3,1},{4,6},{5,7},{6,4},{7,5},{8,10},{9,11},{10,... | collective-permute-start | bytes 2359304 | tf_op jit(solution)/shard_map/ppermute | solution.py:60
  130.7 34.6 %collective-permute-start.11 = (f32[256,768]{1,0:T(8,128)S(1)}, f32[256,768]{1,0:T(8,128)S(1)}, u32[]{:S(2)}, u32[]{:S(2)}) collective-permute-start(f32[256,768]{1,0:T(8,128)S(1)} %get-tuple-element.15), channel_id=1, source_target_pairs={{0,3},{1,0},{2,1},{3,2},{4,7},{5,4},{6,5},{7,6},{8,11},{9,8},{10,9... | collective-permute-start | bytes 2359304 | tf_op jit(solution)/shard_map/ppermute | solution.py:60
  133.5 50.2 %collective-permute-start.5 = (f32[256,768]{1,0:T(8,128)S(1)}, f32[256,768]{1,0:T(8,128)}, u32[]{:S(2)}, u32[]{:S(2)}) collective-permute-start(f32[256,768]{1,0:T(8,128)S(1)} %fusion), channel_id=1, source_target_pairs={{0,3},{1,0},{2,1},{3,2},{4,7},{5,4},{6,5},{7,6},{8,11},{9,8},{10,9... | collective-permute-start | bytes 2359304 | tf_op jit(solution)/shard_map/ppermute | solution.py:60
  136.3 49.1 %collective-permute-start.4 = (f32[256,768]{1,0:T(8,128)S(1)}, f32[256,768]{1,0:T(8,128)}, u32[]{:S(2)}, u32[]{:S(2)}) collective-permute-start(f32[256,768]{1,0:T(8,128)S(1)} %fusion), channel_id=1, source_target_pairs={{0,2},{1,3},{2,0},{3,1},{4,6},{5,7},{6,4},{7,5},{8,10},{9,11},{10,... | collective-permute-start | bytes 2359304 | tf_op jit(solution)/shard_map/ppermute | solution.py:60
  145.2 46.9 %collective-permute-start.3 = (f32[256,768]{1,0:T(8,128)S(1)}, f32[256,768]{1,0:T(8,128)}, u32[]{:S(2)}, u32[]{:S(2)}) collective-permute-start(f32[256,768]{1,0:T(8,128)S(1)} %fusion), channel_id=1, source_target_pairs={{0,1},{1,2},{2,3},{3,0},{4,5},{5,6},{6,7},{7,4},{8,9},{9,10},{10,1... | collective-permute-start | bytes 2359304 | tf_op jit(solution)/shard_map/ppermute | solution.py:60
  168.2 36.5 %all-to-all-start.3 = ((f32[4,8,24,256]{3,2,1,0:T(8,128)}), f32[4,8,24,256]{3,2,1,0:T(8,128)S(1)}, u32[]{:S(2)}, u32[]{:S(2)}) async-start(f32[4,8,24,256]{3,2,1,0:T(8,128)} %broadcast_in_dim.22), calls=%async_computation.3 | async-start | bytes 1572864 | tf_op jit(solution)/shard_map/all_to_all | solution.py:44

commit v4 on v3

--- a/solution.py
+++ b/solution.py
@@ -44,16 +44,13 @@
     return lax.all_to_all(copies, axis, 0, 0)
 
 
-def summed_rows(partial):
-    parts = partial.reshape(lax.axis_size("y"), -1, partial.shape[-1])
-    group = lax.axis_size("x") * lax.axis_size("core")
-    parts = jnp.broadcast_to(parts[None], (group, *parts.shape)).reshape(-1, *parts.shape[1:])
-    parts = lax.all_to_all(parts, ("x", "core", "y"), 0, 0)
+def summed_tiles(tiles):
+    lead, tile = tiles.shape[:3], tiles.shape[3:]
+    parts = lax.all_to_all(tiles.reshape(-1, *tile), ("x", "core", "y"), 0, 0)
     own = jnp.sum(parts, axis=0)
-    halves = spread(own, ("zh", "z"))
-    halves = halves.reshape(lax.axis_size("zh"), -1, *own.shape)
+    halves = spread(own, ("zh", "z")).reshape(lax.axis_size("zh"), -1, *tile)
     column = jnp.sum(halves, axis=0)
-    return spread(column, "y")
+    return spread(column, ("x", "core", "y")).reshape(*lead, -1, *tile)
 
 
 def named_permute(array, pairs):
@@ -106,17 +103,21 @@
     turned = onehot(place_of(order // group, z_index, HOPS) * group + order % group, panel)
 
     with_gathered = product(own_pairs.reshape(-1, cols), gathered, (1, 1))
-    with_reflectors = product(product(own_cholesky, all_reflectors, (1, 1)), turned, (1, 1))
+    with_reflectors = product(own_cholesky, all_reflectors, (1, 1))
+    with_reflectors = product(with_reflectors, turned, (1, 1))
     partial = jnp.concatenate(
         [
             with_gathered.reshape(y_width, 2 * share, panel),
             with_reflectors.reshape(y_width, share, panel),
+            jnp.zeros((y_width, share, panel), jnp.float32),
         ],
         axis=1,
     )
-    sums = summed_rows(partial)
+    lanes = panel // lax.axis_size("core")
+    tiles = partial.reshape(y_width, lax.axis_size("x"), share, -1, lanes).transpose(1, 3, 0, 2, 4)
+    sums = summed_tiles(tiles)
     inner, direct, cross = (
-        sums[:, :, k * share : (k + 1) * share].reshape(panel, panel) for k in range(3)
+        sums[k].transpose(1, 2, 3, 0, 4).reshape(panel, panel) for k in range(3)
     )
     spot = (order // group) * share + (order % group) // share * (z_width * share) + order % share
     by_spot = onehot(spot, panel)

time: 218 us -> 196 us (0.90)
  blocking collectives: 19.3 us -> 0 us
  waiting for transfers between devices: 93.2 us -> 74.6 us
  starting transfers between devices: 72.3 us -> 83.2 us
  other arithmetic: 6.87 us -> 9.53 us
    all_to_all x1 -> x0, blocking collectives: 19.3 us -> none  [summed_rows(): parts = lax.all_to_all(parts, ('x', 'core', 'y'), 0, 0)]
    ppermute x6, waiting for transfers between devices: 37.3 us -> 19.3 us  [named_permute(): return lax.ppermute(array, 'y', pairs)]
    all_to_all x0 -> x1, starting transfers between devices: none -> 5.85 us  [summed_tiles(): parts = lax.all_to_all(tiles.reshape(-1, *tile), ('x', 'core', 'y'), 0, 0)]
    all_to_all x2, starting transfers between devices: 17.9 us -> 22.3 us  [spread(): return lax.all_to_all(copies, axis, 0, 0)]
    ppermute x6, waiting for transfers between devices: 40 us -> 36.9 us  [doubled(): other = lax.ppermute(block, axis, [(i, i ^ hop) for i in range(width)])]
    another operation x2, other arithmetic: 2.03 us -> 4.58 us  [per_device(): jnp.stack(reflector_blocks)]
    all_to_all x2, waiting for transfers between devices: 9.65 us -> 12.2 us  [spread(): return lax.all_to_all(copies, axis, 0, 0)]
  transfers between devices with their start and end apart: 15 -> 16, of which waited for: 12 -> 10; matrix products, arithmetic and copies ran while one was open for 6% -> 11% of each run, Pallas kernels for 0% -> 0%
where the time goes in v4:
time: 196 us; the launch traced here: 192 us
  starting transfers between devices  83.2 us (42%)
  waiting for transfers between devices  74.6 us (38%)
  matrix products  15 us (8%)
  other arithmetic  9.53 us (5%)
  Pallas kernels  5.91 us (3%)
  local copies, waits for them, and re-layouts  3.73 us (2%)
    ppermute x6, waiting for transfers between devices, doubled(): other = lax.ppermute(block, axis, [(i, i ^ hop) for i in range(width)])  36.9 us
    ppermute x6, starting transfers between devices, doubled(): other = lax.ppermute(block, axis, [(i, i ^ hop) for i in range(width)])  32.2 us
    all_to_all x2, starting transfers between devices, spread(): return lax.all_to_all(copies, axis, 0, 0)  22.3 us
    ppermute x6, waiting for transfers between devices, named_permute(): return lax.ppermute(array, 'y', pairs)  19.3 us
    ppermute x6, starting transfers between devices, named_permute(): return lax.ppermute(array, 'y', pairs)  17.8 us
    dot_general x18, matrix products, product(): lax.dot_general(left, right, (((contract[0],), (contract[1],)), ((), ()))...  15 us
    all_to_all x2, waiting for transfers between devices, spread(): return lax.all_to_all(copies, axis, 0, 0)  12.2 us
    all_to_all x1, waiting for transfers between devices, per_device(): packed = lax.all_to_all(packed, 'y', 0, 0)  6.22 us
  transfers between devices with their start and end apart: 16, of which 10 were waited for; matrix products, arithmetic and copies ran while one was open for 11% of the time, Pallas kernels for 0%

profile of v4, /device:TPU:1, one launch (start us, length us, event | category | flops | bytes accessed | tf_op | source)
XLA Modules:
  0.0 192.3 jit_solution(8963202727697350986)
XLA Ops:
  0.0 0.7 and_select_fusion.9
  0.7 0.7 broadcast_compare_fusion
  1.4 0.2 convert_reduce_fusion
  1.6 0.2 fusion.22
  1.8 0.3 fusion.50
  2.2 1.0 pad_maximum_fusion.4
  3.1 0.2 reshape.208
  3.3 0.8 copy.45
  4.1 5.0 %all-to-all-start = ((f32[4,28,768]{2,1,0:T(8,128)}), f32[4,28,768]{2,1,0:T(8,128)S(1)}, u32[]{:S(2)}, u32[]{:S(2)}) async-start(f32[4,28,768]{2,1,0:T(8,128)} %bitcast.80), calls=%async_computation | async-start | bytes 786432 | tf_op jit(solution)/shard_map/all_to_all | solution.py:87
  9.1 6.2 %all-to-all-done = f32[4,28,768]{2,1,0:T(8,128)S(1)} async-done(((f32[4,28,768]{2,1,0:T(8,128)}), f32[4,28,768]{2,1,0:T(8,128)S(1)}, u32[]{:S(2)}, u32[]{:S(2)}) %all-to-all-start) | async-done | bytes 344096 | tf_op jit(solution)/shard_map/all_to_all | solution.py:87
  15.4 9.5 %collective-permute-start.6 = (f32[32,768]{1,0:T(8,128)S(1)}, f32[32,768]{1,0:T(8,128)S(1)}, u32[]{:S(2)}, u32[]{:S(2)}) collective-permute-start(f32[32,768]{1,0:T(8,128)S(1)} %slice_bitcast_fusion.2), channel_id=1, source_target_pairs={{0,16},{4,20},{8,24},{12,28},{16,0},{20,4},{24,8},{28,12},{1,17},{... | collective-permute-start | bytes 294920 | tf_op jit(solution)/shard_map/ppermute | solution.py:32
  24.9 1.9 collective-permute-start
  26.9 0.1 broadcast_or_fusion
  27.0 15.0 %collective-permute-start.7 = (f32[64,768]{1,0:T(8,128)S(1)}, f32[64,768]{1,0:T(8,128)S(1)}, u32[]{:S(2)}, u32[]{:S(2)}) collective-permute-start(f32[64,768]{1,0:T(8,128)S(1)} %pad_maximum_fusion.7), channel_id=1, source_target_pairs={{0,8},{4,12},{8,0},{12,4},{16,24},{20,28},{24,16},{28,20},{1,9},{5... | collective-permute-start | bytes 589832 | tf_op jit(solution)/shard_map/ppermute | solution.py:32
  42.0 4.9 %collective-permute-done = f32[48,768]{1,0:T(8,128)S(1)} collective-permute-done((f32[48,768]{1,0:T(8,128)S(1)}, f32[48,768]{1,0:T(8,128)S(1)}, u32[]{:S(2)}, u32[]{:S(2)}) %collective-permute-start) | collective-permute-done | bytes 147488 | tf_op jit(solution)/shard_map/ppermute | solution.py:32
  46.8 1.9 collective-permute-start.1
  48.8 12.1 %collective-permute-done.7 = f32[64,768]{1,0:T(8,128)S(1)} collective-permute-done((f32[64,768]{1,0:T(8,128)S(1)}, f32[64,768]{1,0:T(8,128)S(1)}, u32[]{:S(2)}, u32[]{:S(2)}) %collective-permute-start.7) | collective-permute-done | bytes 196640 | tf_op jit(solution)/shard_map/ppermute | solution.py:32
  60.9 1.9 collective-permute-start.8
  62.9 0.1 pad.2.clone
  63.0 4.3 %collective-permute-done.1 = f32[96,768]{1,0:T(8,128)S(1)} collective-permute-done((f32[96,768]{1,0:T(8,128)S(1)}, f32[96,768]{1,0:T(8,128)S(1)}, u32[]{:S(2)}, u32[]{:S(2)}) %collective-permute-start.1) | collective-permute-done | bytes 294944 | tf_op jit(solution)/shard_map/ppermute | solution.py:32
  67.3 1.9 collective-permute-start.2
  69.2 7.2 %collective-permute-done.8 = f32[128,768]{1,0:T(8,128)S(1)} collective-permute-done((f32[128,768]{1,0:T(8,128)S(1)}, f32[128,768]{1,0:T(8,128)S(1)}, u32[]{:S(2)}, u32[]{:S(2)}) %collective-permute-start.8) | collective-permute-done | bytes 393248 | tf_op jit(solution)/shard_map/ppermute | solution.py:32
  76.5 1.0 fusion.48
  77.4 2.2 %collective-permute-start.9 = (f32[256,768]{1,0:T(8,128)}, f32[256,768]{1,0:T(8,128)}, u32[]{:S(2)}, u32[]{:S(2)}) collective-permute-start(f32[256,768]{1,0:T(8,128)} %get-tuple-element.15), channel_id=1, source_target_pairs={{0,1},{1,2},{2,3},{3,0},{4,5},{5,6},{6,7},{7,4},{8,9},{9,10},{10,1... | collective-permute-start | bytes 2359304 | tf_op jit(solution)/shard_map/ppermute | solution.py:57
  79.6 0.8 fusion.23
  80.4 0.3 convolution_bitcast_fusion.5
  80.8 8.4 %collective-permute-done.2 = f32[192,768]{1,0:T(8,128)S(1)} collective-permute-done((f32[192,768]{1,0:T(8,128)S(1)}, f32[192,768]{1,0:T(8,128)S(1)}, u32[]{:S(2)}, u32[]{:S(2)}) %collective-permute-start.2) | collective-permute-done | bytes 589856 | tf_op jit(solution)/shard_map/ppermute | solution.py:32
  89.2 0.9 fusion
  90.1 0.0 copy-start.2
  90.2 0.8 fusion.8
  91.0 0.1 maximum_bitcast_fusion
  91.1 0.7 copy.34
  91.8 5.9 %all-to-all-start.1 = ((f32[32,8,128]{2,1,0:T(8,128)}), f32[32,8,128]{2,1,0:T(8,128)S(1)}, u32[]{:S(2)}, u32[]{:S(2)}) async-start(f32[32,8,128]{2,1,0:T(8,128)} %bitcast.21), calls=%async_computation.1 | async-start | bytes 262144 | tf_op jit(solution)/shard_map/all_to_all | solution.py:49
  97.6 4.8 %collective-permute-start.10 = (f32[256,768]{1,0:T(8,128)}, f32[256,768]{1,0:T(8,128)}, u32[]{:S(2)}, u32[]{:S(2)}) collective-permute-start(f32[256,768]{1,0:T(8,128)} %get-tuple-element.15), channel_id=1, source_target_pairs={{0,2},{1,3},{2,0},{3,1},{4,6},{5,7},{6,4},{7,5},{8,10},{9,11},{10,... | collective-permute-start | bytes 2359304 | tf_op jit(solution)/shard_map/ppermute | solution.py:57
  102.4 2.8 %collective-permute-start.11 = (f32[256,768]{1,0:T(8,128)}, f32[256,768]{1,0:T(8,128)}, u32[]{:S(2)}, u32[]{:S(2)}) collective-permute-start(f32[256,768]{1,0:T(8,128)} %get-tuple-element.15), channel_id=1, source_target_pairs={{0,3},{1,0},{2,1},{3,2},{4,7},{5,4},{6,5},{7,6},{8,11},{9,8},{10,9... | collective-permute-start | bytes 2359304 | tf_op jit(solution)/shard_map/ppermute | solution.py:57
  105.2 1.9 collective-permute-start.5
  107.2 0.6 broadcast_in_dim.21
  107.8 13.1 %all-to-all-start.2 = ((f32[16,8,128]{2,1,0:T(8,128)}), f32[16,8,128]{2,1,0:T(8,128)S(1)}, u32[]{:S(2)}, u32[]{:S(2)}) async-start(f32[16,8,128]{2,1,0:T(8,128)} %broadcast_in_dim.21), calls=%async_computation.2 | async-start | bytes 131072 | tf_op jit(solution)/shard_map/all_to_all | solution.py:44
  120.9 1.1 fusion.16
  122.1 4.3 %collective-permute-start.4 = (f32[256,768]{1,0:T(8,128)S(1)}, f32[256,768]{1,0:T(8,128)}, u32[]{:S(2)}, u32[]{:S(2)}) collective-permute-start(f32[256,768]{1,0:T(8,128)S(1)} %fusion), channel_id=1, source_target_pairs={{0,2},{1,3},{2,0},{3,1},{4,6},{5,7},{6,4},{7,5},{8,10},{9,11},{10,... | collective-permute-start | bytes 2359304 | tf_op jit(solution)/shard_map/ppermute | solution.py:57
  126.3 1.9 collective-permute-start.3
  128.3 1.1 fusion.14
  129.4 3.1 %all-to-all-done.2 = f32[16,8,128]{2,1,0:T(8,128)S(1)} async-done(((f32[16,8,128]{2,1,0:T(8,128)}), f32[16,8,128]{2,1,0:T(8,128)S(1)}, u32[]{:S(2)}, u32[]{:S(2)}) %all-to-all-start.2) | async-done | bytes 65568 | tf_op jit(solution)/shard_map/all_to_all | solution.py:44
  132.5 1.1 broadcast_in_dim.22
  133.6 9.2 %all-to-all-start.3 = ((f32[32,8,8,128]{3,2,1,0:T(8,128)}), f32[32,8,8,128]{3,2,1,0:T(8,128)S(1)}, u32[]{:S(2)}, u32[]{:S(2)}) async-start(f32[32,8,8,128]{3,2,1,0:T(8,128)} %broadcast_in_dim.22), calls=%async_computation.3 | async-start | bytes 2097152 | tf_op jit(solution)/shard_map/all_to_all | solution.py:44
  142.8 0.7 pad_add_fusion.where_ref
  143.5 0.6 convolution_bitcast_fusion.3
  144.1 3.6 %pad_maximum_fusion.reflectors_ref = f32[4,256,768]{2,1,0:T(8,128)} fusion(f32[1,256,768]{2,1,0:T(8,128)} %bitcast.15, f32[1,256,768]{2,1,0:T(8,128)} %bitcast.14, f32[1,256,768]{2,1,0:T(8,128)} %bitcast.13, f32[1,256,768]{2,1,0:T(8,128)S(1)} %get-tuple-element.14), kind=kLoop, calls=%fused_computation | loop fusion | flops 2359296 | bytes 6291456 | tf_op jit(solution)/shard_map/stack | solution.py:138
  147.7 14.7 %collective-permute-done.5 = f32[256,768]{1,0:T(8,128)} collective-permute-done((f32[256,768]{1,0:T(8,128)S(1)}, f32[256,768]{1,0:T(8,128)}, u32[]{:S(2)}, u32[]{:S(2)}) %collective-permute-start.5) | collective-permute-done | bytes 786464 | tf_op jit(solution)/shard_map/ppermute | solution.py:57
  162.4 1.7 convolution_bitcast_fusion
  164.1 1.7 convolution_bitcast_fusion.1
  165.8 4.6 %collective-permute-done.3 = f32[256,768]{1,0:T(8,128)} collective-permute-done((f32[256,768]{1,0:T(8,128)S(1)}, f32[256,768]{1,0:T(8,128)}, u32[]{:S(2)}, u32[]{:S(2)}) %collective-permute-start.3) | collective-permute-done | bytes 786464 | tf_op jit(solution)/shard_map/ppermute | solution.py:57
  170.4 1.7 convolution_bitcast_fusion.2
  172.1 1.3 pad_maximum_fusion.1.merged_ref
  173.5 9.1 %all-to-all-done.3 = f32[32,8,8,128]{3,2,1,0:T(8,128)S(1)} async-done(((f32[32,8,8,128]{3,2,1,0:T(8,128)}), f32[32,8,8,128]{3,2,1,0:T(8,128)S(1)}, u32[]{:S(2)}, u32[]{:S(2)}) %all-to-all-start.3) | async-done | bytes 1048608 | tf_op jit(solution)/shard_map/all_to_all | solution.py:44
  182.5 0.1 fusion.49
  182.7 0.4 fusion.51
  183.1 0.4 convolution_bitcast_fusion.4
  183.5 0.1 copy-done.3
  183.6 0.4 fusion.52
  184.0 1.0 fusion.10.coeff_ref
  185.0 0.4 convolution_subtract_fusion
  185.3 1.1 fusion.53.off_ref
  186.4 5.9 %finished.1 = f32[128,3072]{1,0:T(8,128)} custom-call(s32[2]{0:T(128)} %pad_add_fusion.where_ref, f32[4,128,768]{2,1,0:T(8,128)} %pad_maximum_fusion.1.merged_ref, f32[128,256]{1,0:T(8,128)} %fusion.10.coeff_ref, f32[4,256,768]{2,1,0:T(8,128)} %pad_maximum_fusion.reflectors_ref, f32[128,256]{1,0:T(8,128)} %fusion.53.off_ref, f32[256,256]{1,0:T(8,128)} %inverse_ref.1), custom_call_target="tpu_custom_call" | custom-call | tf_op jit(solution)/shard_map/finished/pallas_call | solution.py:179
  (35 shorter events, 0.4 us)
Async XLA Ops:
  0.0 1.8 copy-start
  4.1 11.2 %all-to-all-start = ((f32[4,28,768]{2,1,0:T(8,128)}), f32[4,28,768]{2,1,0:T(8,128)S(1)}, u32[]{:S(2)}, u32[]{:S(2)}) async-start(f32[4,28,768]{2,1,0:T(8,128)} %bitcast.80), calls=%async_computation | async-start | bytes 786432 | tf_op jit(solution)/shard_map/all_to_all | solution.py:87
  15.4 11.6 %collective-permute-start.6 = (f32[32,768]{1,0:T(8,128)S(1)}, f32[32,768]{1,0:T(8,128)S(1)}, u32[]{:S(2)}, u32[]{:S(2)}) collective-permute-start(f32[32,768]{1,0:T(8,128)S(1)} %slice_bitcast_fusion.2), channel_id=1, source_target_pairs={{0,16},{4,20},{8,24},{12,28},{16,0},{20,4},{24,8},{28,12},{1,17},{... | collective-permute-start | bytes 294920 | tf_op jit(solution)/shard_map/ppermute | solution.py:32
  24.9 21.9 %collective-permute-start = (f32[48,768]{1,0:T(8,128)S(1)}, f32[48,768]{1,0:T(8,128)S(1)}, u32[]{:S(2)}, u32[]{:S(2)}) collective-permute-start(f32[48,768]{1,0:T(8,128)S(1)} %reshape.209), channel_id=1, source_target_pairs={{0,16},{4,20},{8,24},{12,28},{16,0},{20,4},{24,8},{28,12},{1,17},{... | collective-permute-start | bytes 442376 | tf_op jit(solution)/shard_map/ppermute | solution.py:32
  27.0 33.9 %collective-permute-start.7 = (f32[64,768]{1,0:T(8,128)S(1)}, f32[64,768]{1,0:T(8,128)S(1)}, u32[]{:S(2)}, u32[]{:S(2)}) collective-permute-start(f32[64,768]{1,0:T(8,128)S(1)} %pad_maximum_fusion.7), channel_id=1, source_target_pairs={{0,8},{4,12},{8,0},{12,4},{16,24},{20,28},{24,16},{28,20},{1,9},{5... | collective-permute-start | bytes 589832 | tf_op jit(solution)/shard_map/ppermute | solution.py:32
  46.8 20.4 %collective-permute-start.1 = (f32[96,768]{1,0:T(8,128)S(1)}, f32[96,768]{1,0:T(8,128)S(1)}, u32[]{:S(2)}, u32[]{:S(2)}) collective-permute-start(f32[96,768]{1,0:T(8,128)S(1)} %pad_maximum_fusion.6), channel_id=1, source_target_pairs={{0,8},{4,12},{8,0},{12,4},{16,24},{20,28},{24,16},{28,20},{1,9},{5... | collective-permute-start | bytes 884744 | tf_op jit(solution)/shard_map/ppermute | solution.py:32
  60.9 15.6 %collective-permute-start.8 = (f32[128,768]{1,0:T(8,128)S(1)}, f32[128,768]{1,0:T(8,128)S(1)}, u32[]{:S(2)}, u32[]{:S(2)}) collective-permute-start(f32[128,768]{1,0:T(8,128)S(1)} %pad_maximum_fusion.5), channel_id=1, source_target_pairs={{0,4},{4,0},{8,12},{12,8},{16,20},{20,16},{24,28},{28,24},{1,5},{5... | collective-permute-start | bytes 1179656 | tf_op jit(solution)/shard_map/ppermute | solution.py:32
  67.3 21.9 %collective-permute-start.2 = (f32[192,768]{1,0:T(8,128)S(1)}, f32[192,768]{1,0:T(8,128)S(1)}, u32[]{:S(2)}, u32[]{:S(2)}) collective-permute-start(f32[192,768]{1,0:T(8,128)S(1)} %pad_maximum_fusion.3), channel_id=1, source_target_pairs={{0,4},{4,0},{8,12},{12,8},{16,20},{20,16},{24,28},{28,24},{1,5},{5... | collective-permute-start | bytes 1769480 | tf_op jit(solution)/shard_map/ppermute | solution.py:32
  77.4 48.9 %collective-permute-start.9 = (f32[256,768]{1,0:T(8,128)}, f32[256,768]{1,0:T(8,128)}, u32[]{:S(2)}, u32[]{:S(2)}) collective-permute-start(f32[256,768]{1,0:T(8,128)} %get-tuple-element.15), channel_id=1, source_target_pairs={{0,1},{1,2},{2,3},{3,0},{4,5},{5,6},{6,7},{7,4},{8,9},{9,10},{10,1... | collective-permute-start | bytes 2359304 | tf_op jit(solution)/shard_map/ppermute | solution.py:57
  90.1 30.8 %copy-start.5 = (f32[256,256]{1,0:T(8,128)S(1)}, f32[256,256]{1,0:T(8,128)}, u32[]{:S(2)}) copy-start(f32[256,256]{1,0:T(8,128)} %param.11) | copy-start | bytes 786436
  90.1 38.1 %copy-start.2 = (f32[256,256]{1,0:T(8,128)S(1)}, f32[256,256]{1,0:T(8,128)}, u32[]{:S(2)}) copy-start(f32[256,256]{1,0:T(8,128)} %inverse_ref.1) | copy-start | bytes 786436
  91.8 15.4 %all-to-all-start.1 = ((f32[32,8,128]{2,1,0:T(8,128)}), f32[32,8,128]{2,1,0:T(8,128)S(1)}, u32[]{:S(2)}, u32[]{:S(2)}) async-start(f32[32,8,128]{2,1,0:T(8,128)} %bitcast.21), calls=%async_computation.1 | async-start | bytes 262144 | tf_op jit(solution)/shard_map/all_to_all | solution.py:49
  97.6 46.4 %collective-permute-start.10 = (f32[256,768]{1,0:T(8,128)}, f32[256,768]{1,0:T(8,128)}, u32[]{:S(2)}, u32[]{:S(2)}) collective-permute-start(f32[256,768]{1,0:T(8,128)} %get-tuple-element.15), channel_id=1, source_target_pairs={{0,2},{1,3},{2,0},{3,1},{4,6},{5,7},{6,4},{7,5},{8,10},{9,11},{10,... | collective-permute-start | bytes 2359304 | tf_op jit(solution)/shard_map/ppermute | solution.py:57
  102.4 41.7 %collective-permute-start.11 = (f32[256,768]{1,0:T(8,128)}, f32[256,768]{1,0:T(8,128)}, u32[]{:S(2)}, u32[]{:S(2)}) collective-permute-start(f32[256,768]{1,0:T(8,128)} %get-tuple-element.15), channel_id=1, source_target_pairs={{0,3},{1,0},{2,1},{3,2},{4,7},{5,4},{6,5},{7,6},{8,11},{9,8},{10,9... | collective-permute-start | bytes 2359304 | tf_op jit(solution)/shard_map/ppermute | solution.py:57
  105.2 57.2 %collective-permute-start.5 = (f32[256,768]{1,0:T(8,128)S(1)}, f32[256,768]{1,0:T(8,128)}, u32[]{:S(2)}, u32[]{:S(2)}) collective-permute-start(f32[256,768]{1,0:T(8,128)S(1)} %fusion), channel_id=1, source_target_pairs={{0,3},{1,0},{2,1},{3,2},{4,7},{5,4},{6,5},{7,6},{8,11},{9,8},{10,9... | collective-permute-start | bytes 2359304 | tf_op jit(solution)/shard_map/ppermute | solution.py:57
  107.8 24.7 %all-to-all-start.2 = ((f32[16,8,128]{2,1,0:T(8,128)}), f32[16,8,128]{2,1,0:T(8,128)S(1)}, u32[]{:S(2)}, u32[]{:S(2)}) async-start(f32[16,8,128]{2,1,0:T(8,128)} %broadcast_in_dim.21), calls=%async_computation.2 | async-start | bytes 131072 | tf_op jit(solution)/shard_map/all_to_all | solution.py:44
  122.1 42.0 %collective-permute-start.4 = (f32[256,768]{1,0:T(8,128)S(1)}, f32[256,768]{1,0:T(8,128)}, u32[]{:S(2)}, u32[]{:S(2)}) collective-permute-start(f32[256,768]{1,0:T(8,128)S(1)} %fusion), channel_id=1, source_target_pairs={{0,2},{1,3},{2,0},{3,1},{4,6},{5,7},{6,4},{7,5},{8,10},{9,11},{10,... | collective-permute-start | bytes 2359304 | tf_op jit(solution)/shard_map/ppermute | solution.py:57
  126.3 44.1 %collective-permute-start.3 = (f32[256,768]{1,0:T(8,128)S(1)}, f32[256,768]{1,0:T(8,128)}, u32[]{:S(2)}, u32[]{:S(2)}) collective-permute-start(f32[256,768]{1,0:T(8,128)S(1)} %fusion), channel_id=1, source_target_pairs={{0,1},{1,2},{2,3},{3,0},{4,5},{5,6},{6,7},{7,4},{8,9},{9,10},{10,1... | collective-permute-start | bytes 2359304 | tf_op jit(solution)/shard_map/ppermute | solution.py:57
  132.5 11.0 %copy-start.1 = (f32[128,256]{1,0:T(8,128)S(1)}, f32[128,256]{1,0:T(8,128)}, u32[]{:S(2)}) copy-start(f32[128,256]{1,0:T(8,128)} %param.9) | copy-start | bytes 393220
  133.6 48.9 %all-to-all-start.3 = ((f32[32,8,8,128]{3,2,1,0:T(8,128)}), f32[32,8,8,128]{3,2,1,0:T(8,128)S(1)}, u32[]{:S(2)}, u32[]{:S(2)}) async-start(f32[32,8,8,128]{3,2,1,0:T(8,128)} %broadcast_in_dim.22), calls=%async_computation.3 | async-start | bytes 2097152 | tf_op jit(solution)/shard_map/all_to_all | solution.py:44
  182.6 1.0 copy-start.3
  183.0 2.3 %copy-start.4 = (f32[256,256]{1,0:T(8,128)S(1)}, f32[256,256]{1,0:T(8,128)}, u32[]{:S(2)}) copy-start(f32[256,256]{1,0:T(8,128)} %fusion.14) | copy-start | bytes 786436

commit v5 on v4

--- a/solution.py
+++ b/solution.py
@@ -102,6 +102,12 @@
     group = share * y_width
     turned = onehot(place_of(order // group, z_index, HOPS) * group + order % group, panel)
 
+    spot = (order // group) * share + (order % group) // share * (z_width * share) + order % share
+    by_spot = onehot(spot, panel)
+    wy_spots = product(wy_factor, by_spot)
+    inverse_spots = product(panel_inverse, by_spot)
+    shaped = product(product(wy_spots, turned, (0, 0)), all_reflectors)
+
     with_gathered = product(own_pairs.reshape(-1, cols), gathered, (1, 1))
     with_reflectors = product(own_cholesky, all_reflectors, (1, 1))
     with_reflectors = product(with_reflectors, turned, (1, 1))
@@ -119,10 +125,6 @@
     inner, direct, cross = (
         sums[k].transpose(1, 2, 3, 0, 4).reshape(panel, panel) for k in range(3)
     )
-    spot = (order // group) * share + (order % group) // share * (z_width * share) + order % share
-    by_spot = onehot(spot, panel)
-    wy_spots = product(wy_factor, by_spot)
-    inverse_spots = product(panel_inverse, by_spot)
 
     def turns(array):
         return [array] + [
@@ -130,28 +132,40 @@
             for d in range(1, y_width)
         ]
 
-    reflector_blocks = turns(all_reflectors)
+    shaped_blocks = turns(shaped)
     gathered_blocks = turns(gathered)
     merged = []
     for block in gathered_blocks:
         merged.append(product(secular, block))
-    merged, stacked = lax.optimization_barrier((jnp.stack(merged), jnp.stack(reflector_blocks)))
+    stacked = jnp.stack(shaped_blocks)
+    high = lax.reduce_precision(stacked, 8, 7)
+    low = (stacked - high).astype(jnp.bfloat16)
+    merged, high, low = lax.optimization_barrier(
+        (jnp.stack(merged), high.astype(jnp.bfloat16), low)
+    )
 
     projected = product(secular, inner, (1, 1))
     coeff = product(projected, wy_spots, (1, 1))
-    coeff_held = product(coeff, turned)
     correction = product(secular, direct, (1, 1)) - product(coeff, cross, (1, 1))
     taken_off = product(correction, inverse_spots, (1, 1))
     where = jnp.stack([y_index, row_index]).astype(jnp.int32)
-    return finished(where, merged, coeff_held, stacked, taken_off, panel_inverse)
-
-
-def finished(where, merged, coeff, reflectors, taken_off, panel_inverse):
+    return finished(where, merged, projected, high, low, taken_off, panel_inverse)
+
+
+def finished(where, merged, factor, high, low, taken_off, panel_inverse):
     count, vectors, cols = merged.shape
-    panel = coeff.shape[1]
-
-    def kernel(where_ref, merged_ref, coeff_ref, reflectors_ref, off_ref, inverse_ref, out_ref):
-        out_ref[...] = merged_ref[0] - product(coeff_ref[...], reflectors_ref[0])
+    panel = factor.shape[1]
+
+    def once(left, right):
+        return jnp.dot(left, right, preferred_element_type=jnp.float32)
+
+    def kernel(where_ref, merged_ref, factor_ref, high_ref, low_ref, off_ref, inverse_ref, out_ref):
+        left = factor_ref[...]
+        left_high = left.astype(jnp.bfloat16)
+        left_low = (left - left_high.astype(jnp.float32)).astype(jnp.bfloat16)
+        taken = once(left_high, low_ref[0]) + once(left_low, high_ref[0])
+        taken = taken + once(left_high, high_ref[0])
+        out_ref[...] = merged_ref[0] - taken
 
         @pl.when((pl.program_id(0) == 0) & (where_ref[1] == 0))
         def _():
@@ -169,7 +183,8 @@
         grid=(count,),
         in_specs=[
             pl.BlockSpec((1, vectors, cols), turned),
-            pl.BlockSpec(coeff.shape, whole),
+            pl.BlockSpec(factor.shape, whole),
+            pl.BlockSpec((1, panel, cols), turned),
             pl.BlockSpec((1, panel, cols), turned),
             pl.BlockSpec(taken_off.shape, whole),
             pl.BlockSpec(panel_inverse.shape, whole),
@@ -181,7 +196,7 @@
         grid_spec=grid,
         out_shape=jax.ShapeDtypeStruct((vectors, count * cols), jnp.float32),
         name="finished",
-    )(where, merged, coeff, reflectors, taken_off, panel_inverse)
+    )(where, merged, factor, high, low, taken_off, panel_inverse)
 
 
 def solution(mesh):

time: 196 us -> 198 us (1.010); the launches traced: 192 us -> 197 us
  waiting for transfers between devices: 74.6 us -> 79.2 us
    all_to_all x1, waiting for transfers between devices: 0.01 us -> 20.1 us  [summed_tiles(): parts = lax.all_to_all(tiles.reshape(-1, *tile), ('x', 'core', 'y'), 0, 0)]
    all_to_all x2, waiting for transfers between devices: 12.2 us -> 4.1 us  [spread(): return lax.all_to_all(copies, axis, 0, 0)]
    ppermute x6, waiting for transfers between devices: 36.9 us -> 30.7 us  [doubled(): other = lax.ppermute(block, axis, [(i, i ^ hop) for i in range(width)])]
    another operation x2 -> x0, other arithmetic: 4.58 us -> none  [per_device(): jnp.stack(reflector_blocks)]
    convert_element_type x0 -> x1, other arithmetic: none -> 3.74 us  [per_device(): low = (stacked - high).astype(jnp.bfloat16)]
    dot_general x18 -> x19, matrix products: 15 us -> 14.4 us  [product(): lax.dot_general(left, right, (((contract[0],), (contract[1],)), ((), ()))...]
  transfers between devices with their start and end apart: 16 -> 16, of which waited for: 10 -> 9; matrix products, arithmetic and copies ran while one was open for 11% -> 10% of each run, Pallas kernels for 0% -> 0%
where the time goes in v5:
time: 198 us; the launch traced here: 197 us
  starting transfers between devices  83.9 us (42%)
  waiting for transfers between devices  79.2 us (40%)
  matrix products  14.4 us (7%)
  other arithmetic  8.61 us (4%)
  Pallas kernels  5.67 us (3%)
  local copies, waits for them, and re-layouts  4.39 us (2%)
    ppermute x6, starting transfers between devices, doubled(): other = lax.ppermute(block, axis, [(i, i ^ hop) for i in range(width)])  32.2 us
    ppermute x6, waiting for transfers between devices, doubled(): other = lax.ppermute(block, axis, [(i, i ^ hop) for i in range(width)])  30.7 us
    all_to_all x2, starting transfers between devices, spread(): return lax.all_to_all(copies, axis, 0, 0)  20.4 us
    all_to_all x1, waiting for transfers between devices, summed_tiles(): parts = lax.all_to_all(tiles.reshape(-1, *tile), ('x', 'core', 'y'), 0, 0)  20.1 us
    ppermute x6, starting transfers between devices, named_permute(): return lax.ppermute(array, 'y', pairs)  19.2 us
    ppermute x6, waiting for transfers between devices, named_permute(): return lax.ppermute(array, 'y', pairs)  18.9 us
    dot_general x19, matrix products, product(): lax.dot_general(left, right, (((contract[0],), (contract[1],)), ((), ()))...  14.4 us
    all_to_all x1, starting transfers between devices, summed_tiles(): parts = lax.all_to_all(tiles.reshape(-1, *tile), ('x', 'core', 'y'), 0, 0)  7.06 us
  transfers between devices with their start and end apart: 16, of which 9 were waited for; matrix products, arithmetic and copies ran while one was open for 10% of the time, Pallas kernels for 0%

profile of v5, /device:TPU:1, one launch (start us, length us, event | category | flops | bytes accessed | tf_op | source)
XLA Modules:
  0.0 196.7 jit_solution(18275630103385433976)
XLA Ops:
  0.0 0.7 and_select_fusion.9
  0.7 0.7 broadcast_compare_fusion
  1.4 0.2 convert_reduce_fusion
  1.6 0.2 fusion.25
  1.8 0.3 fusion.53
  2.2 0.0 copy-start.4
  2.2 1.0 pad_maximum_fusion.6
  3.2 0.2 reshape.207
  3.4 0.8 copy.49
  4.2 5.0 %all-to-all-start = ((f32[4,28,768]{2,1,0:T(8,128)}), f32[4,28,768]{2,1,0:T(8,128)S(1)}, u32[]{:S(2)}, u32[]{:S(2)}) async-start(f32[4,28,768]{2,1,0:T(8,128)} %bitcast.81), calls=%async_computation | async-start | bytes 786432 | tf_op jit(solution)/shard_map/all_to_all | solution.py:87
  9.2 0.4 fusion.19
  9.7 0.4 fusion.13
  10.0 5.4 %all-to-all-done = f32[4,28,768]{2,1,0:T(8,128)S(1)} async-done(((f32[4,28,768]{2,1,0:T(8,128)}), f32[4,28,768]{2,1,0:T(8,128)S(1)}, u32[]{:S(2)}, u32[]{:S(2)}) %all-to-all-start) | async-done | bytes 344096 | tf_op jit(solution)/shard_map/all_to_all | solution.py:87
  15.4 9.5 %collective-permute-start.6 = (f32[32,768]{1,0:T(8,128)S(1)}, f32[32,768]{1,0:T(8,128)S(1)}, u32[]{:S(2)}, u32[]{:S(2)}) collective-permute-start(f32[32,768]{1,0:T(8,128)S(1)} %slice_bitcast_fusion.2), channel_id=1, source_target_pairs={{0,16},{4,20},{8,24},{12,28},{16,0},{20,4},{24,8},{28,12},{1,17},{... | collective-permute-start | bytes 294920 | tf_op jit(solution)/shard_map/ppermute | solution.py:32
  25.0 1.9 collective-permute-start
  27.0 15.1 %collective-permute-start.7 = (f32[64,768]{1,0:T(8,128)S(1)}, f32[64,768]{1,0:T(8,128)S(1)}, u32[]{:S(2)}, u32[]{:S(2)}) collective-permute-start(f32[64,768]{1,0:T(8,128)S(1)} %pad_maximum_fusion.9), channel_id=1, source_target_pairs={{0,8},{4,12},{8,0},{12,4},{16,24},{20,28},{24,16},{28,20},{1,9},{5... | collective-permute-start | bytes 589832 | tf_op jit(solution)/shard_map/ppermute | solution.py:32
  42.0 0.1 broadcast_or_fusion
  42.1 4.8 %collective-permute-done = f32[48,768]{1,0:T(8,128)S(1)} collective-permute-done((f32[48,768]{1,0:T(8,128)S(1)}, f32[48,768]{1,0:T(8,128)S(1)}, u32[]{:S(2)}, u32[]{:S(2)}) %collective-permute-start) | collective-permute-done | bytes 147488 | tf_op jit(solution)/shard_map/ppermute | solution.py:32
  46.9 1.9 collective-permute-start.1
  48.8 12.1 %collective-permute-done.7 = f32[64,768]{1,0:T(8,128)S(1)} collective-permute-done((f32[64,768]{1,0:T(8,128)S(1)}, f32[64,768]{1,0:T(8,128)S(1)}, u32[]{:S(2)}, u32[]{:S(2)}) %collective-permute-start.7) | collective-permute-done | bytes 196640 | tf_op jit(solution)/shard_map/ppermute | solution.py:32
  61.0 1.9 collective-permute-start.8
  62.9 0.1 pad.2.clone
  63.0 4.2 %collective-permute-done.1 = f32[96,768]{1,0:T(8,128)S(1)} collective-permute-done((f32[96,768]{1,0:T(8,128)S(1)}, f32[96,768]{1,0:T(8,128)S(1)}, u32[]{:S(2)}, u32[]{:S(2)}) %collective-permute-start.1) | collective-permute-done | bytes 294944 | tf_op jit(solution)/shard_map/ppermute | solution.py:32
  67.3 1.9 collective-permute-start.2
  69.2 7.3 %collective-permute-done.8 = f32[128,768]{1,0:T(8,128)S(1)} collective-permute-done((f32[128,768]{1,0:T(8,128)S(1)}, f32[128,768]{1,0:T(8,128)S(1)}, u32[]{:S(2)}, u32[]{:S(2)}) %collective-permute-start.8) | collective-permute-done | bytes 393248 | tf_op jit(solution)/shard_map/ppermute | solution.py:32
  76.5 0.8 fusion.12
  77.3 2.2 %collective-permute-start.9 = (f32[256,768]{1,0:T(8,128)S(1)}, f32[256,768]{1,0:T(8,128)}, u32[]{:S(2)}, u32[]{:S(2)}) collective-permute-start(f32[256,768]{1,0:T(8,128)S(1)} %fusion.12), channel_id=1, source_target_pairs={{0,1},{1,2},{2,3},{3,0},{4,5},{5,6},{6,7},{7,4},{8,9},{9,10},{10,1... | collective-permute-start | bytes 2359304 | tf_op jit(solution)/shard_map/ppermute | solution.py:57
  79.5 3.7 %collective-permute-start.10 = (f32[256,768]{1,0:T(8,128)S(1)}, f32[256,768]{1,0:T(8,128)}, u32[]{:S(2)}, u32[]{:S(2)}) collective-permute-start(f32[256,768]{1,0:T(8,128)S(1)} %fusion.12), channel_id=1, source_target_pairs={{0,2},{1,3},{2,0},{3,1},{4,6},{5,7},{6,4},{7,5},{8,10},{9,11},{10,... | collective-permute-start | bytes 2359304 | tf_op jit(solution)/shard_map/ppermute | solution.py:57
  83.2 2.5 %collective-permute-start.11 = (f32[256,768]{1,0:T(8,128)S(1)}, f32[256,768]{1,0:T(8,128)}, u32[]{:S(2)}, u32[]{:S(2)}) collective-permute-start(f32[256,768]{1,0:T(8,128)S(1)} %fusion.12), channel_id=1, source_target_pairs={{0,3},{1,0},{2,1},{3,2},{4,7},{5,4},{6,5},{7,6},{8,11},{9,8},{10,9... | collective-permute-start | bytes 2359304 | tf_op jit(solution)/shard_map/ppermute | solution.py:57
  85.8 0.8 fusion.11
  86.6 0.3 convolution_bitcast_fusion.5
  86.9 2.3 %collective-permute-done.2 = f32[192,768]{1,0:T(8,128)S(1)} collective-permute-done((f32[192,768]{1,0:T(8,128)S(1)}, f32[192,768]{1,0:T(8,128)S(1)}, u32[]{:S(2)}, u32[]{:S(2)}) %collective-permute-start.2) | collective-permute-done | bytes 589856 | tf_op jit(solution)/shard_map/ppermute | solution.py:32
  89.3 0.9 fusion.1
  90.2 0.0 copy-start.2
  90.2 0.8 fusion.9
  91.0 0.1 maximum_bitcast_fusion
  91.1 0.7 copy.37
  91.8 7.1 %all-to-all-start.1 = ((f32[32,8,128]{2,1,0:T(8,128)}), f32[32,8,128]{2,1,0:T(8,128)S(1)}, u32[]{:S(2)}, u32[]{:S(2)}) async-start(f32[32,8,128]{2,1,0:T(8,128)} %bitcast.21), calls=%async_computation.1 | async-start | bytes 262144 | tf_op jit(solution)/shard_map/all_to_all | solution.py:49
  98.9 4.5 %collective-permute-start.5 = (f32[256,768]{1,0:T(8,128)S(1)}, f32[256,768]{1,0:T(8,128)}, u32[]{:S(2)}, u32[]{:S(2)}) collective-permute-start(f32[256,768]{1,0:T(8,128)S(1)} %fusion.1), channel_id=1, source_target_pairs={{0,3},{1,0},{2,1},{3,2},{4,7},{5,4},{6,5},{7,6},{8,11},{9,8},{10,9... | collective-permute-start | bytes 2359304 | tf_op jit(solution)/shard_map/ppermute | solution.py:57
  103.3 20.1 %all-to-all-done.1 = f32[32,8,128]{2,1,0:T(8,128)S(1)} async-done(((f32[32,8,128]{2,1,0:T(8,128)}), f32[32,8,128]{2,1,0:T(8,128)S(1)}, u32[]{:S(2)}, u32[]{:S(2)}) %all-to-all-start.1) | async-done | bytes 131104 | tf_op jit(solution)/shard_map/all_to_all | solution.py:49
  123.5 0.6 broadcast_in_dim.21
  124.1 12.1 %all-to-all-start.2 = ((f32[16,8,128]{2,1,0:T(8,128)}), f32[16,8,128]{2,1,0:T(8,128)S(1)}, u32[]{:S(2)}, u32[]{:S(2)}) async-start(f32[16,8,128]{2,1,0:T(8,128)} %broadcast_in_dim.21), calls=%async_computation.2 | async-start | bytes 131072 | tf_op jit(solution)/shard_map/all_to_all | solution.py:44
  136.2 2.3 %collective-permute-start.4 = (f32[256,768]{1,0:T(8,128)S(1)}, f32[256,768]{1,0:T(8,128)}, u32[]{:S(2)}, u32[]{:S(2)}) collective-permute-start(f32[256,768]{1,0:T(8,128)S(1)} %fusion.1), channel_id=1, source_target_pairs={{0,2},{1,3},{2,0},{3,1},{4,6},{5,7},{6,4},{7,5},{8,10},{9,11},{10,... | collective-permute-start | bytes 2359304 | tf_op jit(solution)/shard_map/ppermute | solution.py:57
  138.5 4.1 %collective-permute-start.3 = (f32[256,768]{1,0:T(8,128)S(1)}, f32[256,768]{1,0:T(8,128)}, u32[]{:S(2)}, u32[]{:S(2)}) collective-permute-start(f32[256,768]{1,0:T(8,128)S(1)} %fusion.1), channel_id=1, source_target_pairs={{0,1},{1,2},{2,3},{3,0},{4,5},{5,6},{6,7},{7,4},{8,9},{9,10},{10,1... | collective-permute-start | bytes 2359304 | tf_op jit(solution)/shard_map/ppermute | solution.py:57
  142.6 1.1 fusion.17
  143.7 4.1 %all-to-all-done.2 = f32[16,8,128]{2,1,0:T(8,128)S(1)} async-done(((f32[16,8,128]{2,1,0:T(8,128)}), f32[16,8,128]{2,1,0:T(8,128)S(1)}, u32[]{:S(2)}, u32[]{:S(2)}) %all-to-all-start.2) | async-done | bytes 65568 | tf_op jit(solution)/shard_map/all_to_all | solution.py:44
  147.8 1.1 broadcast_in_dim.22
  148.9 8.3 %all-to-all-start.3 = ((f32[32,8,8,128]{3,2,1,0:T(8,128)}), f32[32,8,8,128]{3,2,1,0:T(8,128)S(1)}, u32[]{:S(2)}, u32[]{:S(2)}) async-start(f32[32,8,8,128]{3,2,1,0:T(8,128)} %broadcast_in_dim.22), calls=%async_computation.3 | async-start | bytes 2097152 | tf_op jit(solution)/shard_map/all_to_all | solution.py:44
  157.2 0.6 pad_add_fusion.where_ref
  157.8 0.6 convolution_bitcast_fusion.3
  158.4 3.7 %fusion = (bf16[4,256,768]{2,1,0:T(8,128)(2,1)}, bf16[4,256,768]{2,1,0:T(8,128)(2,1)}) fusion(f32[1,256,768]{2,1,0:T(8,128)} %bitcast.15, f32[1,256,768]{2,1,0:T(8,128)} %bitcast.14, f32[1,256,768]{2,1,0:T(8,128)} %bitcast.13, f32[1,256,768]{2,1,0:T(8,128)S(1)} %bitcast.82), kind=kLoop, calls=%fused_computation.2 | loop fusion | flops 5505024 | bytes 6291456 | tf_op jit(solution)/shard_map/convert_element_type | solution.py:142
  162.1 1.7 convolution_bitcast_fusion
  163.9 1.7 convolution_bitcast_fusion.1
  165.6 18.9 %collective-permute-done.3 = f32[256,768]{1,0:T(8,128)} collective-permute-done((f32[256,768]{1,0:T(8,128)S(1)}, f32[256,768]{1,0:T(8,128)}, u32[]{:S(2)}, u32[]{:S(2)}) %collective-permute-start.3) | collective-permute-done | bytes 786464 | tf_op jit(solution)/shard_map/ppermute | solution.py:57
  184.4 1.7 convolution_bitcast_fusion.2
  186.2 1.3 pad_maximum_fusion.1.merged_ref
  187.5 0.1 fusion.52
  187.6 0.4 fusion.54
  188.0 0.4 fusion.55
  188.4 0.8 copy.39
  189.1 0.4 convolution_bitcast_fusion.4
  189.5 0.4 convolution_subtract_fusion
  189.9 1.1 fusion.56.off_ref
  191.0 5.7 %finished.1 = f32[128,3072]{1,0:T(8,128)} custom-call(s32[2]{0:T(128)} %pad_add_fusion.where_ref, f32[4,128,768]{2,1,0:T(8,128)} %pad_maximum_fusion.1.merged_ref, f32[128,256]{1,0:T(8,128)} %bitcast.89, bf16[4,256,768]{2,1,0:T(8,128)(2,1)} %get-tuple-element.9.high_ref, bf16[4,256,768]{2,1,0:T(8,128)(2,1)} %get-tuple-element.10.low_ref, ...), custom_call_target="tpu_custom_call" | custom-call | tf_op jit(solution)/shard_map/finished/pallas_call | solution.py:194
  (34 shorter events, 0.4 us)
Async XLA Ops:
  0.0 1.8 copy-start
  2.2 7.1 %copy-start.4 = (f32[256,256]{1,0:T(8,128)S(1)}, f32[256,256]{1,0:T(8,128)}, u32[]{:S(2)}) copy-start(f32[256,256]{1,0:T(8,128)} %param.11) | copy-start | bytes 786436
  4.2 11.2 %all-to-all-start = ((f32[4,28,768]{2,1,0:T(8,128)}), f32[4,28,768]{2,1,0:T(8,128)S(1)}, u32[]{:S(2)}, u32[]{:S(2)}) async-start(f32[4,28,768]{2,1,0:T(8,128)} %bitcast.81), calls=%async_computation | async-start | bytes 786432 | tf_op jit(solution)/shard_map/all_to_all | solution.py:87
  15.4 11.5 %collective-permute-start.6 = (f32[32,768]{1,0:T(8,128)S(1)}, f32[32,768]{1,0:T(8,128)S(1)}, u32[]{:S(2)}, u32[]{:S(2)}) collective-permute-start(f32[32,768]{1,0:T(8,128)S(1)} %slice_bitcast_fusion.2), channel_id=1, source_target_pairs={{0,16},{4,20},{8,24},{12,28},{16,0},{20,4},{24,8},{28,12},{1,17},{... | collective-permute-start | bytes 294920 | tf_op jit(solution)/shard_map/ppermute | solution.py:32
  25.0 21.9 %collective-permute-start = (f32[48,768]{1,0:T(8,128)S(1)}, f32[48,768]{1,0:T(8,128)S(1)}, u32[]{:S(2)}, u32[]{:S(2)}) collective-permute-start(f32[48,768]{1,0:T(8,128)S(1)} %reshape.208), channel_id=1, source_target_pairs={{0,16},{4,20},{8,24},{12,28},{16,0},{20,4},{24,8},{28,12},{1,17},{... | collective-permute-start | bytes 442376 | tf_op jit(solution)/shard_map/ppermute | solution.py:32
  27.0 34.0 %collective-permute-start.7 = (f32[64,768]{1,0:T(8,128)S(1)}, f32[64,768]{1,0:T(8,128)S(1)}, u32[]{:S(2)}, u32[]{:S(2)}) collective-permute-start(f32[64,768]{1,0:T(8,128)S(1)} %pad_maximum_fusion.9), channel_id=1, source_target_pairs={{0,8},{4,12},{8,0},{12,4},{16,24},{20,28},{24,16},{28,20},{1,9},{5... | collective-permute-start | bytes 589832 | tf_op jit(solution)/shard_map/ppermute | solution.py:32
  46.9 20.4 %collective-permute-start.1 = (f32[96,768]{1,0:T(8,128)S(1)}, f32[96,768]{1,0:T(8,128)S(1)}, u32[]{:S(2)}, u32[]{:S(2)}) collective-permute-start(f32[96,768]{1,0:T(8,128)S(1)} %pad_maximum_fusion.8), channel_id=1, source_target_pairs={{0,8},{4,12},{8,0},{12,4},{16,24},{20,28},{24,16},{28,20},{1,9},{5... | collective-permute-start | bytes 884744 | tf_op jit(solution)/shard_map/ppermute | solution.py:32
  61.0 15.6 %collective-permute-start.8 = (f32[128,768]{1,0:T(8,128)S(1)}, f32[128,768]{1,0:T(8,128)S(1)}, u32[]{:S(2)}, u32[]{:S(2)}) collective-permute-start(f32[128,768]{1,0:T(8,128)S(1)} %pad_maximum_fusion.7), channel_id=1, source_target_pairs={{0,4},{4,0},{8,12},{12,8},{16,20},{20,16},{24,28},{28,24},{1,5},{5... | collective-permute-start | bytes 1179656 | tf_op jit(solution)/shard_map/ppermute | solution.py:32
  67.3 21.9 %collective-permute-start.2 = (f32[192,768]{1,0:T(8,128)S(1)}, f32[192,768]{1,0:T(8,128)S(1)}, u32[]{:S(2)}, u32[]{:S(2)}) collective-permute-start(f32[192,768]{1,0:T(8,128)S(1)} %pad_maximum_fusion.3), channel_id=1, source_target_pairs={{0,4},{4,0},{8,12},{12,8},{16,20},{20,16},{24,28},{28,24},{1,5},{5... | collective-permute-start | bytes 1769480 | tf_op jit(solution)/shard_map/ppermute | solution.py:32
  77.3 61.1 %collective-permute-start.9 = (f32[256,768]{1,0:T(8,128)S(1)}, f32[256,768]{1,0:T(8,128)}, u32[]{:S(2)}, u32[]{:S(2)}) collective-permute-start(f32[256,768]{1,0:T(8,128)S(1)} %fusion.12), channel_id=1, source_target_pairs={{0,1},{1,2},{2,3},{3,0},{4,5},{5,6},{6,7},{7,4},{8,9},{9,10},{10,1... | collective-permute-start | bytes 2359304 | tf_op jit(solution)/shard_map/ppermute | solution.py:57
  79.5 78.8 %collective-permute-start.10 = (f32[256,768]{1,0:T(8,128)S(1)}, f32[256,768]{1,0:T(8,128)}, u32[]{:S(2)}, u32[]{:S(2)}) collective-permute-start(f32[256,768]{1,0:T(8,128)S(1)} %fusion.12), channel_id=1, source_target_pairs={{0,2},{1,3},{2,0},{3,1},{4,6},{5,7},{6,4},{7,5},{8,10},{9,11},{10,... | collective-permute-start | bytes 2359304 | tf_op jit(solution)/shard_map/ppermute | solution.py:57
  83.2 75.1 %collective-permute-start.11 = (f32[256,768]{1,0:T(8,128)S(1)}, f32[256,768]{1,0:T(8,128)}, u32[]{:S(2)}, u32[]{:S(2)}) collective-permute-start(f32[256,768]{1,0:T(8,128)S(1)} %fusion.12), channel_id=1, source_target_pairs={{0,3},{1,0},{2,1},{3,2},{4,7},{5,4},{6,5},{7,6},{8,11},{9,8},{10,9... | collective-permute-start | bytes 2359304 | tf_op jit(solution)/shard_map/ppermute | solution.py:57
  90.2 52.4 %copy-start.2 = (f32[256,256]{1,0:T(8,128)S(1)}, f32[256,256]{1,0:T(8,128)}, u32[]{:S(2)}) copy-start(f32[256,256]{1,0:T(8,128)} %inverse_ref.1) | copy-start | bytes 786436
  91.8 31.7 %all-to-all-start.1 = ((f32[32,8,128]{2,1,0:T(8,128)}), f32[32,8,128]{2,1,0:T(8,128)S(1)}, u32[]{:S(2)}, u32[]{:S(2)}) async-start(f32[32,8,128]{2,1,0:T(8,128)} %bitcast.21), calls=%async_computation.1 | async-start | bytes 262144 | tf_op jit(solution)/shard_map/all_to_all | solution.py:49
  98.9 63.3 %collective-permute-start.5 = (f32[256,768]{1,0:T(8,128)S(1)}, f32[256,768]{1,0:T(8,128)}, u32[]{:S(2)}, u32[]{:S(2)}) collective-permute-start(f32[256,768]{1,0:T(8,128)S(1)} %fusion.1), channel_id=1, source_target_pairs={{0,3},{1,0},{2,1},{3,2},{4,7},{5,4},{6,5},{7,6},{8,11},{9,8},{10,9... | collective-permute-start | bytes 2359304 | tf_op jit(solution)/shard_map/ppermute | solution.py:57
  124.1 23.7 %all-to-all-start.2 = ((f32[16,8,128]{2,1,0:T(8,128)}), f32[16,8,128]{2,1,0:T(8,128)S(1)}, u32[]{:S(2)}, u32[]{:S(2)}) async-start(f32[16,8,128]{2,1,0:T(8,128)} %broadcast_in_dim.21), calls=%async_computation.2 | async-start | bytes 131072 | tf_op jit(solution)/shard_map/all_to_all | solution.py:44
  136.2 27.7 %collective-permute-start.4 = (f32[256,768]{1,0:T(8,128)S(1)}, f32[256,768]{1,0:T(8,128)}, u32[]{:S(2)}, u32[]{:S(2)}) collective-permute-start(f32[256,768]{1,0:T(8,128)S(1)} %fusion.1), channel_id=1, source_target_pairs={{0,2},{1,3},{2,0},{3,1},{4,6},{5,7},{6,4},{7,5},{8,10},{9,11},{10,... | collective-permute-start | bytes 2359304 | tf_op jit(solution)/shard_map/ppermute | solution.py:57
  138.5 46.0 %collective-permute-start.3 = (f32[256,768]{1,0:T(8,128)S(1)}, f32[256,768]{1,0:T(8,128)}, u32[]{:S(2)}, u32[]{:S(2)}) collective-permute-start(f32[256,768]{1,0:T(8,128)S(1)} %fusion.1), channel_id=1, source_target_pairs={{0,1},{1,2},{2,3},{3,0},{4,5},{5,6},{6,7},{7,4},{8,9},{9,10},{10,1... | collective-permute-start | bytes 2359304 | tf_op jit(solution)/shard_map/ppermute | solution.py:57
  147.8 10.0 %copy-start.1 = (f32[128,256]{1,0:T(8,128)S(1)}, f32[128,256]{1,0:T(8,128)}, u32[]{:S(2)}) copy-start(f32[128,256]{1,0:T(8,128)} %param.9) | copy-start | bytes 393220
  148.9 38.6 %all-to-all-start.3 = ((f32[32,8,8,128]{3,2,1,0:T(8,128)}), f32[32,8,8,128]{3,2,1,0:T(8,128)S(1)}, u32[]{:S(2)}, u32[]{:S(2)}) async-start(f32[32,8,8,128]{3,2,1,0:T(8,128)} %broadcast_in_dim.22), calls=%async_computation.3 | async-start | bytes 2097152 | tf_op jit(solution)/shard_map/all_to_all | solution.py:44
  187.9 2.0 %copy-start.3 = (f32[256,256]{1,0:T(8,128)S(1)}, f32[256,256]{1,0:T(8,128)}, u32[]{:S(2)}) copy-start(f32[256,256]{1,0:T(8,128)} %fusion.17) | copy-start | bytes 786436

commit v6 on v5

--- a/solution.py
+++ b/solution.py
@@ -144,59 +144,66 @@
         (jnp.stack(merged), high.astype(jnp.bfloat16), low)
     )
 
-    projected = product(secular, inner, (1, 1))
-    coeff = product(projected, wy_spots, (1, 1))
-    correction = product(secular, direct, (1, 1)) - product(coeff, cross, (1, 1))
-    taken_off = product(correction, inverse_spots, (1, 1))
     where = jnp.stack([y_index, row_index]).astype(jnp.int32)
-    return finished(where, merged, projected, high, low, taken_off, panel_inverse)
-
-
-def finished(where, merged, factor, high, low, taken_off, panel_inverse):
+    small = (secular, inner, direct, cross, wy_spots, inverse_spots, panel_inverse)
+    return finished(where, merged, high, low, small)
+
+
+def finished(where, merged, high, low, small):
     count, vectors, cols = merged.shape
-    panel = factor.shape[1]
+    panel = high.shape[1]
 
     def once(left, right):
         return jnp.dot(left, right, preferred_element_type=jnp.float32)
 
-    def kernel(where_ref, merged_ref, factor_ref, high_ref, low_ref, off_ref, inverse_ref, out_ref):
-        left = factor_ref[...]
-        left_high = left.astype(jnp.bfloat16)
-        left_low = (left - left_high.astype(jnp.float32)).astype(jnp.bfloat16)
-        taken = once(left_high, low_ref[0]) + once(left_low, high_ref[0])
-        taken = taken + once(left_high, high_ref[0])
-        out_ref[...] = merged_ref[0] - taken
-
-        @pl.when((pl.program_id(0) == 0) & (where_ref[1] == 0))
+    def kernel(where_ref, merged_ref, high_ref, low_ref, *refs):
+        secular_ref, inner_ref, direct_ref, cross_ref, wy_ref, spots_ref, inverse_ref = refs[:7]
+        out_ref, factor_ref, factor_high, factor_low = refs[7:]
+        step = pl.program_id(0)
+
+        @pl.when(step == 0)
         def _():
-            head = out_ref[:, :panel]
-            out_ref[:, :panel] = product(head, inverse_ref[...], (1, 1)) - off_ref[...]
-
-    def turned(q, where_ref):
-        return (lax.rem(where_ref[0] - q + count, count), 0, 0)
-
-    def whole(q, where_ref):
-        return (0, 0)
-
+            factor = product(secular_ref[...], inner_ref[...], (1, 1))
+            rounded = factor.astype(jnp.bfloat16)
+            factor_ref[...] = factor
+            factor_high[...] = rounded
+            factor_low[...] = (factor - rounded.astype(jnp.float32)).astype(jnp.bfloat16)
+
+        block = lax.rem(where_ref[0] - step + count, count)
+        taken = once(factor_high[...], low_ref[block]) + once(factor_low[...], high_ref[block])
+        taken = taken + once(factor_high[...], high_ref[block])
+        out_ref[...] = merged_ref[block] - taken
+
+        @pl.when((step == 0) & (where_ref[1] == 0))
+        def _():
+            coeff = product(factor_ref[...], wy_ref[...], (1, 1))
+            correction = product(secular_ref[...], direct_ref[...], (1, 1))
+            correction = correction - product(coeff, cross_ref[...], (1, 1))
+            solved = product(out_ref[:, :panel], inverse_ref[...], (1, 1))
+            out_ref[:, :panel] = solved - product(correction, spots_ref[...], (1, 1))
+
+    operands = [
+        pltpu.with_memory_space_constraint(array, pltpu.VMEM)
+        for array in (merged, high, low, *small)
+    ]
     grid = pltpu.PrefetchScalarGridSpec(
         num_scalar_prefetch=1,
         grid=(count,),
-        in_specs=[
-            pl.BlockSpec((1, vectors, cols), turned),
-            pl.BlockSpec(factor.shape, whole),
-            pl.BlockSpec((1, panel, cols), turned),
-            pl.BlockSpec((1, panel, cols), turned),
-            pl.BlockSpec(taken_off.shape, whole),
-            pl.BlockSpec(panel_inverse.shape, whole),
+        in_specs=[pl.BlockSpec(memory_space=pltpu.VMEM)] * len(operands),
+        out_specs=pl.BlockSpec((vectors, cols), lambda q, where_ref: (0, q)),
+        scratch_shapes=[
+            pltpu.VMEM((vectors, panel), jnp.float32),
+            pltpu.VMEM((vectors, panel), jnp.bfloat16),
+            pltpu.VMEM((vectors, panel), jnp.bfloat16),
         ],
-        out_specs=pl.BlockSpec((vectors, cols), lambda q, where_ref: (0, q)),
     )
     return pl.pallas_call(
         kernel,
         grid_spec=grid,
         out_shape=jax.ShapeDtypeStruct((vectors, count * cols), jnp.float32),
+        compiler_params=pltpu.CompilerParams(vmem_limit_bytes=16 * 2**20),
         name="finished",
-    )(where, merged, factor, high, low, taken_off, panel_inverse)
+    )(where, *operands)
 
 
 def solution(mesh):

time: 198 us -> 194 us (0.980)
  other arithmetic: 8.61 us -> 6.24 us
  Pallas kernels: 5.67 us -> 3.48 us
    pallas_call x1, Pallas kernels: 5.67 us -> 3.48 us  [finished(): pl.pallas_call(kernel, grid_spec=grid, out_shape=jax.ShapeDtypeStruct((ve...]
    all_to_all x1, waiting for transfers between devices: 20.1 us -> 18.1 us  [summed_tiles(): parts = lax.all_to_all(tiles.reshape(-1, *tile), ('x', 'core', 'y'), 0, 0)]
    dot_general x19 -> x14, matrix products: 14.4 us -> 15 us  [product(): lax.dot_general(left, right, (((contract[0],), (contract[1],)), ((), ()))...]
  transfers between devices with their start and end apart: 16 -> 16, of which waited for: 9 -> 10; matrix products, arithmetic and copies ran while one was open for 10% -> 11% of each run, Pallas kernels for 0% -> 0%
where the time goes in v6:
time: 194 us; the launch traced here: 193 us
  starting transfers between devices  84 us (43%)
  waiting for transfers between devices  77.4 us (40%)
  matrix products  15 us (8%)
  other arithmetic  6.24 us (3%)
  local copies, waits for them, and re-layouts  6.16 us (3%)
  Pallas kernels  3.48 us (2%)
    ppermute x6, starting transfers between devices, doubled(): other = lax.ppermute(block, axis, [(i, i ^ hop) for i in range(width)])  32.2 us
    ppermute x6, waiting for transfers between devices, doubled(): other = lax.ppermute(block, axis, [(i, i ^ hop) for i in range(width)])  30.6 us
    all_to_all x2, starting transfers between devices, spread(): return lax.all_to_all(copies, axis, 0, 0)  20.4 us
    ppermute x6, starting transfers between devices, named_permute(): return lax.ppermute(array, 'y', pairs)  19.2 us
    ppermute x6, waiting for transfers between devices, named_permute(): return lax.ppermute(array, 'y', pairs)  19.1 us
    all_to_all x1, waiting for transfers between devices, summed_tiles(): parts = lax.all_to_all(tiles.reshape(-1, *tile), ('x', 'core', 'y'), 0, 0)  18.1 us
    dot_general x14, matrix products, product(): lax.dot_general(left, right, (((contract[0],), (contract[1],)), ((), ()))...  15 us
    all_to_all x1, starting transfers between devices, summed_tiles(): parts = lax.all_to_all(tiles.reshape(-1, *tile), ('x', 'core', 'y'), 0, 0)  7.16 us
  transfers between devices with their start and end apart: 16, of which 10 were waited for; matrix products, arithmetic and copies ran while one was open for 11% of the time, Pallas kernels for 0%

profile of v6, /device:TPU:1, one launch (start us, length us, event | category | flops | bytes accessed | tf_op | source)
XLA Modules:
  0.0 192.8 jit_solution(15462601335026855925)
XLA Ops:
  0.0 0.7 and_select_fusion.9
  0.7 0.7 broadcast_compare_fusion
  1.4 0.2 convert_reduce_fusion
  1.6 0.2 fusion.23
  1.8 0.3 fusion.51
  2.2 0.0 copy-start.10
  2.2 1.0 pad_maximum_fusion.6
  3.2 0.2 reshape.207
  3.4 0.8 copy.43
  4.2 5.0 %all-to-all-start = ((f32[4,28,768]{2,1,0:T(8,128)}), f32[4,28,768]{2,1,0:T(8,128)S(1)}, u32[]{:S(2)}, u32[]{:S(2)}) async-start(f32[4,28,768]{2,1,0:T(8,128)} %bitcast.71), calls=%async_computation | async-start | bytes 786432 | tf_op jit(solution)/shard_map/all_to_all | solution.py:87
  9.2 0.4 fusion.17
  9.7 0.4 fusion.13
  10.0 5.4 %all-to-all-done = f32[4,28,768]{2,1,0:T(8,128)S(1)} async-done(((f32[4,28,768]{2,1,0:T(8,128)}), f32[4,28,768]{2,1,0:T(8,128)S(1)}, u32[]{:S(2)}, u32[]{:S(2)}) %all-to-all-start) | async-done | bytes 344096 | tf_op jit(solution)/shard_map/all_to_all | solution.py:87
  15.4 9.5 %collective-permute-start.6 = (f32[32,768]{1,0:T(8,128)S(1)}, f32[32,768]{1,0:T(8,128)S(1)}, u32[]{:S(2)}, u32[]{:S(2)}) collective-permute-start(f32[32,768]{1,0:T(8,128)S(1)} %slice_bitcast_fusion.2), channel_id=1, source_target_pairs={{0,16},{4,20},{8,24},{12,28},{16,0},{20,4},{24,8},{28,12},{1,17},{... | collective-permute-start | bytes 294920 | tf_op jit(solution)/shard_map/ppermute | solution.py:32
  25.0 1.9 collective-permute-start
  27.0 15.1 %collective-permute-start.7 = (f32[64,768]{1,0:T(8,128)S(1)}, f32[64,768]{1,0:T(8,128)S(1)}, u32[]{:S(2)}, u32[]{:S(2)}) collective-permute-start(f32[64,768]{1,0:T(8,128)S(1)} %pad_maximum_fusion.9), channel_id=1, source_target_pairs={{0,8},{4,12},{8,0},{12,4},{16,24},{20,28},{24,16},{28,20},{1,9},{5... | collective-permute-start | bytes 589832 | tf_op jit(solution)/shard_map/ppermute | solution.py:32
  42.0 0.1 broadcast_or_fusion
  42.1 4.8 %collective-permute-done = f32[48,768]{1,0:T(8,128)S(1)} collective-permute-done((f32[48,768]{1,0:T(8,128)S(1)}, f32[48,768]{1,0:T(8,128)S(1)}, u32[]{:S(2)}, u32[]{:S(2)}) %collective-permute-start) | collective-permute-done | bytes 147488 | tf_op jit(solution)/shard_map/ppermute | solution.py:32
  46.9 1.9 collective-permute-start.1
  48.8 12.1 %collective-permute-done.7 = f32[64,768]{1,0:T(8,128)S(1)} collective-permute-done((f32[64,768]{1,0:T(8,128)S(1)}, f32[64,768]{1,0:T(8,128)S(1)}, u32[]{:S(2)}, u32[]{:S(2)}) %collective-permute-start.7) | collective-permute-done | bytes 196640 | tf_op jit(solution)/shard_map/ppermute | solution.py:32
  61.0 1.9 collective-permute-start.8
  62.9 0.1 pad.2.clone
  63.0 4.2 %collective-permute-done.1 = f32[96,768]{1,0:T(8,128)S(1)} collective-permute-done((f32[96,768]{1,0:T(8,128)S(1)}, f32[96,768]{1,0:T(8,128)S(1)}, u32[]{:S(2)}, u32[]{:S(2)}) %collective-permute-start.1) | collective-permute-done | bytes 294944 | tf_op jit(solution)/shard_map/ppermute | solution.py:32
  67.3 1.9 collective-permute-start.2
  69.2 7.3 %collective-permute-done.8 = f32[128,768]{1,0:T(8,128)S(1)} collective-permute-done((f32[128,768]{1,0:T(8,128)S(1)}, f32[128,768]{1,0:T(8,128)S(1)}, u32[]{:S(2)}, u32[]{:S(2)}) %collective-permute-start.8) | collective-permute-done | bytes 393248 | tf_op jit(solution)/shard_map/ppermute | solution.py:32
  76.5 0.8 fusion.12
  77.3 2.2 %collective-permute-start.9 = (f32[256,768]{1,0:T(8,128)S(1)}, f32[256,768]{1,0:T(8,128)S(1)}, u32[]{:S(2)}, u32[]{:S(2)}) collective-permute-start(f32[256,768]{1,0:T(8,128)S(1)} %fusion.12), channel_id=1, source_target_pairs={{0,1},{1,2},{2,3},{3,0},{4,5},{5,6},{6,7},{7,4},{8,9},{9,10},{10,1... | collective-permute-start | bytes 2359304 | tf_op jit(solution)/shard_map/ppermute | solution.py:57
  79.5 3.7 %collective-permute-start.10 = (f32[256,768]{1,0:T(8,128)S(1)}, f32[256,768]{1,0:T(8,128)}, u32[]{:S(2)}, u32[]{:S(2)}) collective-permute-start(f32[256,768]{1,0:T(8,128)S(1)} %fusion.12), channel_id=1, source_target_pairs={{0,2},{1,3},{2,0},{3,1},{4,6},{5,7},{6,4},{7,5},{8,10},{9,11},{10,... | collective-permute-start | bytes 2359304 | tf_op jit(solution)/shard_map/ppermute | solution.py:57
  83.2 2.5 %collective-permute-start.11 = (f32[256,768]{1,0:T(8,128)S(1)}, f32[256,768]{1,0:T(8,128)}, u32[]{:S(2)}, u32[]{:S(2)}) collective-permute-start(f32[256,768]{1,0:T(8,128)S(1)} %fusion.12), channel_id=1, source_target_pairs={{0,3},{1,0},{2,1},{3,2},{4,7},{5,4},{6,5},{7,6},{8,11},{9,8},{10,9... | collective-permute-start | bytes 2359304 | tf_op jit(solution)/shard_map/ppermute | solution.py:57
  85.8 0.8 fusion.11
  86.6 0.3 convolution_bitcast_fusion.5
  86.9 2.2 %collective-permute-done.2 = f32[192,768]{1,0:T(8,128)S(1)} collective-permute-done((f32[192,768]{1,0:T(8,128)S(1)}, f32[192,768]{1,0:T(8,128)S(1)}, u32[]{:S(2)}, u32[]{:S(2)}) %collective-permute-start.2) | collective-permute-done | bytes 589856 | tf_op jit(solution)/shard_map/ppermute | solution.py:32
  89.2 1.8 fusion.1
  91.0 2.0 %fusion.9 = f32[4,16,256]{2,1,0:T(8,128)S(1)} fusion(f32[4,16,768]{2,1,0:T(8,128)S(1)} %slice_select_fusion, f32[256,768]{1,0:T(8,128)} %fusion.1), kind=kOutput, calls=%fused_computation.20 | convolution fusion | flops 150994944 | bytes 1048576 | tf_op jit(solution)/shard_map/dot_general | solution.py:16
  93.0 0.1 maximum_bitcast_fusion
  93.1 0.7 copy.31
  93.7 7.2 %all-to-all-start.1 = ((f32[32,8,128]{2,1,0:T(8,128)}), f32[32,8,128]{2,1,0:T(8,128)S(1)}, u32[]{:S(2)}, u32[]{:S(2)}) async-start(f32[32,8,128]{2,1,0:T(8,128)} %bitcast.21), calls=%async_computation.1 | async-start | bytes 262144 | tf_op jit(solution)/shard_map/all_to_all | solution.py:49
  100.9 4.5 %collective-permute-start.5 = (f32[256,768]{1,0:T(8,128)}, f32[256,768]{1,0:T(8,128)}, u32[]{:S(2)}, u32[]{:S(2)}) collective-permute-start(f32[256,768]{1,0:T(8,128)} %fusion.1), channel_id=1, source_target_pairs={{0,3},{1,0},{2,1},{3,2},{4,7},{5,4},{6,5},{7,6},{8,11},{9,8},{10,9... | collective-permute-start | bytes 2359304 | tf_op jit(solution)/shard_map/ppermute | solution.py:57
  105.4 18.1 %all-to-all-done.1 = f32[32,8,128]{2,1,0:T(8,128)S(1)} async-done(((f32[32,8,128]{2,1,0:T(8,128)}), f32[32,8,128]{2,1,0:T(8,128)S(1)}, u32[]{:S(2)}, u32[]{:S(2)}) %all-to-all-start.1) | async-done | bytes 131104 | tf_op jit(solution)/shard_map/all_to_all | solution.py:49
  123.5 0.6 broadcast_in_dim.21
  124.1 12.1 %all-to-all-start.2 = ((f32[16,8,128]{2,1,0:T(8,128)}), f32[16,8,128]{2,1,0:T(8,128)S(1)}, u32[]{:S(2)}, u32[]{:S(2)}) async-start(f32[16,8,128]{2,1,0:T(8,128)} %broadcast_in_dim.21), calls=%async_computation.2 | async-start | bytes 131072 | tf_op jit(solution)/shard_map/all_to_all | solution.py:44
  136.2 2.3 %collective-permute-start.4 = (f32[256,768]{1,0:T(8,128)}, f32[256,768]{1,0:T(8,128)}, u32[]{:S(2)}, u32[]{:S(2)}) collective-permute-start(f32[256,768]{1,0:T(8,128)} %fusion.1), channel_id=1, source_target_pairs={{0,2},{1,3},{2,0},{3,1},{4,6},{5,7},{6,4},{7,5},{8,10},{9,11},{10,... | collective-permute-start | bytes 2359304 | tf_op jit(solution)/shard_map/ppermute | solution.py:57
  138.5 4.1 %collective-permute-start.3 = (f32[256,768]{1,0:T(8,128)}, f32[256,768]{1,0:T(8,128)}, u32[]{:S(2)}, u32[]{:S(2)}) collective-permute-start(f32[256,768]{1,0:T(8,128)} %fusion.1), channel_id=1, source_target_pairs={{0,1},{1,2},{2,3},{3,0},{4,5},{5,6},{6,7},{7,4},{8,9},{9,10},{10,1... | collective-permute-start | bytes 2359304 | tf_op jit(solution)/shard_map/ppermute | solution.py:57
  142.6 1.1 convolution_bitcast_fusion.4.refs_5_
  143.6 0.9 copy.35
  144.5 3.3 %all-to-all-done.2 = f32[16,8,128]{2,1,0:T(8,128)S(1)} async-done(((f32[16,8,128]{2,1,0:T(8,128)}), f32[16,8,128]{2,1,0:T(8,128)S(1)}, u32[]{:S(2)}, u32[]{:S(2)}) %all-to-all-start.2) | async-done | bytes 65568 | tf_op jit(solution)/shard_map/all_to_all | solution.py:44
  147.8 1.1 broadcast_in_dim.22
  148.9 8.4 %all-to-all-start.3 = ((f32[32,8,8,128]{3,2,1,0:T(8,128)}), f32[32,8,8,128]{3,2,1,0:T(8,128)}, u32[]{:S(2)}, u32[]{:S(2)}) async-start(f32[32,8,8,128]{3,2,1,0:T(8,128)} %broadcast_in_dim.22), calls=%async_computation.3 | async-start | bytes 2097152 | tf_op jit(solution)/shard_map/all_to_all | solution.py:44
  157.2 0.0 copy-start.9
  157.3 0.1 pad_add_fusion.where_ref
  157.3 1.8 convolution_bitcast_fusion.3
  159.1 3.0 %fusion = (bf16[4,256,768]{2,1,0:T(8,128)(2,1)S(1)}, bf16[4,256,768]{2,1,0:T(8,128)(2,1)}) fusion(f32[1,256,768]{2,1,0:T(8,128)} %bitcast.15, f32[1,256,768]{2,1,0:T(8,128)} %bitcast.14, f32[1,256,768]{2,1,0:T(8,128)S(1)} %bitcast.80, f32[1,256,768]{2,1,0:T(8,128)S(1)} %bitcast.76), kind=kLoop, calls=%fused_computation.2 | loop fusion | flops 5505024 | bytes 6291456 | tf_op jit(solution)/shard_map/convert_element_type | solution.py:142
  162.2 1.7 convolution_bitcast_fusion
  163.9 1.7 convolution_bitcast_fusion.1
  165.6 19.1 %collective-permute-done.3 = f32[256,768]{1,0:T(8,128)} collective-permute-done((f32[256,768]{1,0:T(8,128)}, f32[256,768]{1,0:T(8,128)}, u32[]{:S(2)}, u32[]{:S(2)}) %collective-permute-start.3) | collective-permute-done | bytes 786464 | tf_op jit(solution)/shard_map/ppermute | solution.py:57
  184.6 1.7 convolution_bitcast_fusion.2
  186.4 0.1 pad_maximum_fusion.1.merged_ref
  186.5 0.9 all-to-all-done.3
  187.5 1.3 fusion.50
  188.9 0.2 copy-done.1
  189.1 0.1 copy-done.5
  189.2 0.1 copy-done.6
  189.2 0.1 copy-done.7
  189.3 3.5 %finished.1 = f32[128,3072]{1,0:T(8,128)} custom-call(s32[2]{0:T(128)S(1)} %pad_add_fusion.where_ref, f32[4,128,768]{2,1,0:T(8,128)S(1)} %pad_maximum_fusion.1.merged_ref, bf16[4,256,768]{2,1,0:T(8,128)(2,1)S(1)} %copy-done.1, bf16[4,256,768]{2,1,0:T(8,128)(2,1)S(1)} %get-tuple-element.10.low_ref, f32[128,256]{1,0:T(8,128)S(1)} %copy-done.3, ...), custom_call_target="tpu_custom_call" | custom-call | tf_op jit(solution)/shard_map/finished/pallas_call | solution.py:200
  (41 shorter events, 0.4 us)
Async XLA Ops:
  0.0 1.8 copy-start
  2.2 7.1 %copy-start.10 = (f32[256,256]{1,0:T(8,128)S(1)}, f32[256,256]{1,0:T(8,128)}, u32[]{:S(2)}) copy-start(f32[256,256]{1,0:T(8,128)} %param.11) | copy-start | bytes 786436
  4.2 11.2 %all-to-all-start = ((f32[4,28,768]{2,1,0:T(8,128)}), f32[4,28,768]{2,1,0:T(8,128)S(1)}, u32[]{:S(2)}, u32[]{:S(2)}) async-start(f32[4,28,768]{2,1,0:T(8,128)} %bitcast.71), calls=%async_computation | async-start | bytes 786432 | tf_op jit(solution)/shard_map/all_to_all | solution.py:87
  15.4 11.5 %collective-permute-start.6 = (f32[32,768]{1,0:T(8,128)S(1)}, f32[32,768]{1,0:T(8,128)S(1)}, u32[]{:S(2)}, u32[]{:S(2)}) collective-permute-start(f32[32,768]{1,0:T(8,128)S(1)} %slice_bitcast_fusion.2), channel_id=1, source_target_pairs={{0,16},{4,20},{8,24},{12,28},{16,0},{20,4},{24,8},{28,12},{1,17},{... | collective-permute-start | bytes 294920 | tf_op jit(solution)/shard_map/ppermute | solution.py:32
  25.0 21.9 %collective-permute-start = (f32[48,768]{1,0:T(8,128)S(1)}, f32[48,768]{1,0:T(8,128)S(1)}, u32[]{:S(2)}, u32[]{:S(2)}) collective-permute-start(f32[48,768]{1,0:T(8,128)S(1)} %reshape.208), channel_id=1, source_target_pairs={{0,16},{4,20},{8,24},{12,28},{16,0},{20,4},{24,8},{28,12},{1,17},{... | collective-permute-start | bytes 442376 | tf_op jit(solution)/shard_map/ppermute | solution.py:32
  27.0 34.0 %collective-permute-start.7 = (f32[64,768]{1,0:T(8,128)S(1)}, f32[64,768]{1,0:T(8,128)S(1)}, u32[]{:S(2)}, u32[]{:S(2)}) collective-permute-start(f32[64,768]{1,0:T(8,128)S(1)} %pad_maximum_fusion.9), channel_id=1, source_target_pairs={{0,8},{4,12},{8,0},{12,4},{16,24},{20,28},{24,16},{28,20},{1,9},{5... | collective-permute-start | bytes 589832 | tf_op jit(solution)/shard_map/ppermute | solution.py:32
  46.9 20.4 %collective-permute-start.1 = (f32[96,768]{1,0:T(8,128)S(1)}, f32[96,768]{1,0:T(8,128)S(1)}, u32[]{:S(2)}, u32[]{:S(2)}) collective-permute-start(f32[96,768]{1,0:T(8,128)S(1)} %pad_maximum_fusion.8), channel_id=1, source_target_pairs={{0,8},{4,12},{8,0},{12,4},{16,24},{20,28},{24,16},{28,20},{1,9},{5... | collective-permute-start | bytes 884744 | tf_op jit(solution)/shard_map/ppermute | solution.py:32
  61.0 15.6 %collective-permute-start.8 = (f32[128,768]{1,0:T(8,128)S(1)}, f32[128,768]{1,0:T(8,128)S(1)}, u32[]{:S(2)}, u32[]{:S(2)}) collective-permute-start(f32[128,768]{1,0:T(8,128)S(1)} %pad_maximum_fusion.7), channel_id=1, source_target_pairs={{0,4},{4,0},{8,12},{12,8},{16,20},{20,16},{24,28},{28,24},{1,5},{5... | collective-permute-start | bytes 1179656 | tf_op jit(solution)/shard_map/ppermute | solution.py:32
  67.3 21.8 %collective-permute-start.2 = (f32[192,768]{1,0:T(8,128)S(1)}, f32[192,768]{1,0:T(8,128)S(1)}, u32[]{:S(2)}, u32[]{:S(2)}) collective-permute-start(f32[192,768]{1,0:T(8,128)S(1)} %pad_maximum_fusion.3), channel_id=1, source_target_pairs={{0,4},{4,0},{8,12},{12,8},{16,20},{20,16},{24,28},{28,24},{1,5},{5... | collective-permute-start | bytes 1769480 | tf_op jit(solution)/shard_map/ppermute | solution.py:32
  77.3 61.1 %collective-permute-start.9 = (f32[256,768]{1,0:T(8,128)S(1)}, f32[256,768]{1,0:T(8,128)S(1)}, u32[]{:S(2)}, u32[]{:S(2)}) collective-permute-start(f32[256,768]{1,0:T(8,128)S(1)} %fusion.12), channel_id=1, source_target_pairs={{0,1},{1,2},{2,3},{3,0},{4,5},{5,6},{6,7},{7,4},{8,9},{9,10},{10,1... | collective-permute-start | bytes 2359304 | tf_op jit(solution)/shard_map/ppermute | solution.py:57
  79.5 79.6 %collective-permute-start.10 = (f32[256,768]{1,0:T(8,128)S(1)}, f32[256,768]{1,0:T(8,128)}, u32[]{:S(2)}, u32[]{:S(2)}) collective-permute-start(f32[256,768]{1,0:T(8,128)S(1)} %fusion.12), channel_id=1, source_target_pairs={{0,2},{1,3},{2,0},{3,1},{4,6},{5,7},{6,4},{7,5},{8,10},{9,11},{10,... | collective-permute-start | bytes 2359304 | tf_op jit(solution)/shard_map/ppermute | solution.py:57
  83.2 75.9 %collective-permute-start.11 = (f32[256,768]{1,0:T(8,128)S(1)}, f32[256,768]{1,0:T(8,128)}, u32[]{:S(2)}, u32[]{:S(2)}) collective-permute-start(f32[256,768]{1,0:T(8,128)S(1)} %fusion.12), channel_id=1, source_target_pairs={{0,3},{1,0},{2,1},{3,2},{4,7},{5,4},{6,5},{7,6},{8,11},{9,8},{10,9... | collective-permute-start | bytes 2359304 | tf_op jit(solution)/shard_map/ppermute | solution.py:57
  91.0 51.6 %copy-start.4 = (f32[256,256]{1,0:T(8,128)S(1)}, f32[256,256]{1,0:T(8,128)}, u32[]{:S(2)}) copy-start(f32[256,256]{1,0:T(8,128)} %refs_6_.1) | copy-start | bytes 786436
  93.7 29.7 %all-to-all-start.1 = ((f32[32,8,128]{2,1,0:T(8,128)}), f32[32,8,128]{2,1,0:T(8,128)S(1)}, u32[]{:S(2)}, u32[]{:S(2)}) async-start(f32[32,8,128]{2,1,0:T(8,128)} %bitcast.21), calls=%async_computation.1 | async-start | bytes 262144 | tf_op jit(solution)/shard_map/all_to_all | solution.py:49
  100.9 61.3 %collective-permute-start.5 = (f32[256,768]{1,0:T(8,128)}, f32[256,768]{1,0:T(8,128)}, u32[]{:S(2)}, u32[]{:S(2)}) collective-permute-start(f32[256,768]{1,0:T(8,128)} %fusion.1), channel_id=1, source_target_pairs={{0,3},{1,0},{2,1},{3,2},{4,7},{5,4},{6,5},{7,6},{8,11},{9,8},{10,9... | collective-permute-start | bytes 2359304 | tf_op jit(solution)/shard_map/ppermute | solution.py:57
  124.1 23.7 %all-to-all-start.2 = ((f32[16,8,128]{2,1,0:T(8,128)}), f32[16,8,128]{2,1,0:T(8,128)S(1)}, u32[]{:S(2)}, u32[]{:S(2)}) async-start(f32[16,8,128]{2,1,0:T(8,128)} %broadcast_in_dim.21), calls=%async_computation.2 | async-start | bytes 131072 | tf_op jit(solution)/shard_map/all_to_all | solution.py:44
  136.2 27.7 %collective-permute-start.4 = (f32[256,768]{1,0:T(8,128)}, f32[256,768]{1,0:T(8,128)}, u32[]{:S(2)}, u32[]{:S(2)}) collective-permute-start(f32[256,768]{1,0:T(8,128)} %fusion.1), channel_id=1, source_target_pairs={{0,2},{1,3},{2,0},{3,1},{4,6},{5,7},{6,4},{7,5},{8,10},{9,11},{10,... | collective-permute-start | bytes 2359304 | tf_op jit(solution)/shard_map/ppermute | solution.py:57
  138.5 10.4 %copy-start.8 = (f32[256,768]{1,0:T(8,128)}, f32[256,768]{1,0:T(8,128)S(1)}, u32[]{:S(2)}) copy-start(f32[256,768]{1,0:T(8,128)S(1)} %collective-permute-done.9) | copy-start | bytes 2359300
  138.5 46.2 %collective-permute-start.3 = (f32[256,768]{1,0:T(8,128)}, f32[256,768]{1,0:T(8,128)}, u32[]{:S(2)}, u32[]{:S(2)}) collective-permute-start(f32[256,768]{1,0:T(8,128)} %fusion.1), channel_id=1, source_target_pairs={{0,1},{1,2},{2,3},{3,0},{4,5},{5,6},{6,7},{7,4},{8,9},{9,10},{10,1... | collective-permute-start | bytes 2359304 | tf_op jit(solution)/shard_map/ppermute | solution.py:57
  147.8 9.6 %copy-start.2 = (f32[128,256]{1,0:T(8,128)S(1)}, f32[128,256]{1,0:T(8,128)}, u32[]{:S(2)}) copy-start(f32[128,256]{1,0:T(8,128)} %refs_0_.1) | copy-start | bytes 393220
  148.9 38.6 %all-to-all-start.3 = ((f32[32,8,8,128]{3,2,1,0:T(8,128)}), f32[32,8,8,128]{3,2,1,0:T(8,128)}, u32[]{:S(2)}, u32[]{:S(2)}) async-start(f32[32,8,8,128]{3,2,1,0:T(8,128)} %broadcast_in_dim.22), calls=%async_computation.3 | async-start | bytes 2097152 | tf_op jit(solution)/shard_map/all_to_all | solution.py:44
  157.2 1.9 copy-start.9
  187.5 1.6 copy-start.1
  187.5 1.6 copy-start.3
  187.5 1.7 copy-start.5
  187.5 1.8 copy-start.6
  187.5 1.8 copy-start.7
